TPU v7x, 512 devices: a whole 4x4x16 slice. The times are simulated.
512 devices in a mesh: section: 8 (over y, core), shard: 64 (over x, z).
Axes of the slice: x: 4, y: 4, z: 16, core: 2. Of those that a mesh axis runs over, the one named last changes fastest.
Arguments:
- section_input: bfloat16 [4, 64, 196, 256], P(None, 'shard'), may hold values from -6 to 6
- conv_one: bfloat16 [8, 2304, 256], P('section'), may hold values from -0.125 to 0.125
- conv_two: bfloat16 [8, 2304, 256], P('section'), may hold values from -0.125 to 0.125
- unit_gain: float32 [8, 256], P('section'), may hold values from 0.5 to 1.5
- offset_bias: float32 [8, 256], P('section'), may hold values from -3 to 3
- leak_slope: float32 [8, 256], P('section'), may hold values from 0.1 to 0.4
- depthwise: bfloat16 [196, 256], replicated, may hold values from -0.4375 to 0.4375
- embed_weight: bfloat16 [256, 512], replicated, may hold values from -0.375 to 0.375
- class_centers: bfloat16 [106496, 512], P('shard'), may hold values from -6 to 6
- labels: int32 [4, 64], replicated, may hold values from 0 to 106495
- class_offsets: int32 [64], P('shard'), may hold values from 0 to 104832, as said below
Outputs:
- section_grads: bfloat16 [8, 4, 64, 196, 256], P('section', None, 'shard')
Inputs may be any that keep to these rules, and one draw needn't show every extreme that they name: `class_offsets`: each entry is 1664 times a different number of 0 to 63, so the blocks of class_centers hold every class of 0 to 106495 once.
All inputs are finite; a program needn't handle non-finite values.
Results may differ from a plain program's by a relative error of at most 0.03.
Values may be sent and summed in bfloat16 or wider, within the bound.
No kernel may reach another device: no remote copies, remote signals or barrier semaphores. Data moves between devices by JAX's collectives and lax.ppermute only.
A program may use at most 64 MiB of HBM per device.

v0:
```python
import math

import jax
import jax.numpy as jnp
from jax import lax
from jax.sharding import PartitionSpec as P

SIDE = 14


margin_value = 0.4
scale_value = 64.0
tiny_value = 1e-06


def passed_along(value, axis, steps):
    count = lax.axis_size(axis)
    initial, last = (max(0, -steps), min(count, count - steps))
    return lax.ppermute(value, axis, [(source, source + steps) for source in range(initial, last)])


def sent_to_all(shard, axis):
    length = lax.axis_size(axis)
    return lax.all_to_all(
        jnp.broadcast_to(shard[None], (length, *shard.shape)), axis, 0, 0, tiled=True
    )


def joined_along(tiles, dim):
    lengths = list(tiles.shape[1:])
    lengths[dim] *= tiles.shape[0]
    return jnp.moveaxis(tiles, 0, dim).reshape(lengths)


def gather_directly(shard, axis, dim):
    tiles = sent_to_all(shard, axis)
    return joined_along(tiles, dim)


def cut_along(shard, dim, length):
    before, after = (shard.shape[:dim], shard.shape[dim + 1 :])
    return jnp.moveaxis(shard.reshape(*before, length, -1, *after), dim, 0)


def sum_at_owner(shard, axis, dim):
    length = lax.axis_size(axis)
    tiles = lax.all_to_all(cut_along(shard, dim, length), axis, 0, 0, tiled=True)
    return jnp.sum(tiles.astype(jnp.float32), axis=0)


def sent_together(arrays, axis, dim, along):
    columns = [a.reshape(*a.shape[:along], -1) for a in arrays]
    both = jnp.concatenate(columns, axis=along)
    filled, at, finished = (sum_at_owner(both, axis, dim), 0, [])
    for a, column in zip(arrays, columns):
        share = filled[..., at : at + column.shape[along]]
        finished.append(share.reshape(*share.shape[:along], *a.shape[along:]))
        at += column.shape[along]
    return tuple(finished)


def conv_apply(images, weights):
    image_count = images.shape[0]
    channels = images.shape[-1]
    image_grid = images.reshape(image_count, SIDE, SIDE, channels)
    padded = jnp.pad(image_grid, ((0, 0), (1, 1), (1, 1), (0, 0)))
    pieces = [
        padded[:, row_shift : row_shift + SIDE, col_shift : col_shift + SIDE, :]
        for row_shift in range(3)
        for col_shift in range(3)
    ]
    columns = jnp.concatenate(pieces, axis=3).reshape(image_count * SIDE * SIDE, 9 * channels)
    result = jnp.dot(columns, weights, preferred_element_type=jnp.float32)
    return result.reshape(image_count, SIDE * SIDE, weights.shape[1])


def flip_weights(weights):
    channels = weights.shape[1]
    tap_blocks = weights.reshape(9, channels, channels)
    return jnp.swapaxes(tap_blocks[::-1], 1, 2).reshape(9 * channels, channels)


def smooth_active(pre_active, leak):
    return leak * pre_active + (1.0 - leak) * jax.nn.softplus(4.0 * pre_active) / 4.0


def smooth_slope(pre_active, leak):
    return leak + (1.0 - leak) * jax.nn.sigmoid(4.0 * pre_active)


def unit_forward(images, first_weight, second_weight, gain_row, bias_row, leak_row):
    hidden = conv_apply(images, first_weight)
    pre_active = hidden * gain_row + bias_row
    active = smooth_active(pre_active, leak_row).astype(jnp.bfloat16)
    output = (images.astype(jnp.float32) + conv_apply(active, second_weight)).astype(jnp.bfloat16)
    return (output, pre_active)


def unit_backward(grad_out, pre_active, first_flip, second_flip, gain_row, leak_row):
    grad_active = conv_apply(grad_out, second_flip)
    grad_hidden = (grad_active * smooth_slope(pre_active, leak_row) * gain_row).astype(jnp.bfloat16)
    return (grad_out.astype(jnp.float32) + conv_apply(grad_hidden, first_flip)).astype(jnp.bfloat16)


def unit_scale(values):
    squares = jnp.mean(values * values, axis=-1, keepdims=True)
    factor = lax.rsqrt(squares + tiny_value) / math.sqrt(values.shape[-1])
    return (values * factor, squares, factor)


def on_device(
    section_input,
    conv_one,
    conv_two,
    unit_gain,
    offset_bias,
    leak_slope,
    depthwise,
    embed_weight,
    class_centers,
    labels,
    class_offsets,
):
    sections = lax.axis_size("section")
    section_index = lax.axis_index("section")
    micro_count = section_input.shape[0]
    first_weight = conv_one[0]
    second_weight = conv_two[0]
    gain_row = unit_gain[0]
    bias_row = offset_bias[0]
    leak_row = leak_slope[0]
    first_flip = flip_weights(first_weight)
    second_flip = flip_weights(second_weight)
    empty_image = jnp.zeros(section_input.shape[1:], jnp.bfloat16)
    pre_start = jnp.zeros(section_input.shape, jnp.float32)
    out_start = jnp.zeros(section_input.shape, jnp.bfloat16)
    tick_count = micro_count + sections - 1

    def forward_tick(running, step_index):
        incoming, pre_store, out_store = running
        micro_index = step_index - section_index
        is_active = jnp.logical_and(micro_index >= 0, micro_index < micro_count)
        slot_index = jnp.clip(micro_index, 0, micro_count - 1)
        fresh = lax.dynamic_index_in_dim(section_input, slot_index, 0, keepdims=False)
        source = jnp.where(section_index == 0, fresh, incoming)

        def forward_compute(stores):
            output, pre_active = unit_forward(
                source, first_weight, second_weight, gain_row, bias_row, leak_row
            )
            new_pre = lax.dynamic_update_index_in_dim(stores[0], pre_active, slot_index, 0)
            new_out = lax.dynamic_update_index_in_dim(stores[1], output, slot_index, 0)
            return (output, new_pre, new_out)

        def forward_skip_tick(stores):
            return (empty_image, stores[0], stores[1])

        output, pre_store, out_store = lax.cond(
            is_active, forward_compute, forward_skip_tick, (pre_store, out_store)
        )
        passed = passed_along(output, "section", 1)
        return ((passed, pre_store, out_store), None)

    forward_state = lax.scan(
        forward_tick, (empty_image, pre_start, out_start), jnp.arange(tick_count, dtype=jnp.int32)
    )[0]
    pre_store = forward_state[1]
    out_store = forward_state[2]
    pooled = jnp.einsum(
        "mfpc,pc->mfc", out_store, depthwise, preferred_element_type=jnp.float32
    ).astype(jnp.bfloat16)
    embedded = jnp.einsum("mfc,ce->mfe", pooled, embed_weight, preferred_element_type=jnp.float32)
    normed, squares, factor = unit_scale(embedded)
    gathered = gather_directly(normed.astype(jnp.bfloat16), "shard", 1)
    face_shape = gathered.shape
    row_count = face_shape[0] * face_shape[1]
    unit_half = gathered.reshape(row_count, face_shape[2])
    centres_unit = unit_scale(class_centers.astype(jnp.float32))[0].astype(jnp.bfloat16)
    class_ids = class_offsets[0] + jnp.arange(class_centers.shape[0], dtype=jnp.int32)
    label_hits = labels.reshape(row_count)[:, None] == class_ids[None, :]
    cosines = lax.dot_general(
        unit_half, centres_unit, (((1,), (1,)), ((), ())), preferred_element_type=jnp.float32
    )
    logits = scale_value * (cosines - margin_value * label_hits.astype(jnp.float32))
    exp_logits = jnp.exp(logits)
    weighted = jnp.dot(
        exp_logits.astype(jnp.bfloat16), centres_unit, preferred_element_type=jnp.float32
    ).reshape(face_shape)
    chosen = jnp.dot(
        label_hits.astype(jnp.bfloat16), centres_unit, preferred_element_type=jnp.float32
    ).reshape(face_shape)
    totals = jnp.sum(exp_logits, axis=1).reshape(face_shape[0], face_shape[1])
    weighted_sum, chosen_sum, total_sum = sent_together(
        (weighted.astype(jnp.bfloat16), chosen.astype(jnp.bfloat16), totals.astype(jnp.bfloat16)),
        "shard",
        1,
        2,
    )
    grad_unit = scale_value * (weighted_sum / total_sum[:, :, None] - chosen_sum)
    inner = jnp.sum(embedded * grad_unit, axis=-1, keepdims=True)
    grad_embed = factor * (
        grad_unit - embedded * inner / (embedded.shape[-1] * (squares + tiny_value))
    )
    grad_pooled = jnp.einsum(
        "mfe,ce->mfc",
        grad_embed.astype(jnp.bfloat16),
        embed_weight,
        preferred_element_type=jnp.float32,
    )
    grad_final = (
        grad_pooled[:, :, None, :] * depthwise.astype(jnp.float32)[None, None, :, :]
    ).astype(jnp.bfloat16)
    grad_start = jnp.zeros(section_input.shape, jnp.bfloat16)
    tick_count = micro_count + sections - 1

    def backward_tick(running, step_index):
        incoming, grad_store = running
        micro_index = step_index - (sections - 1 - section_index)
        is_active = jnp.logical_and(micro_index >= 0, micro_index < micro_count)
        slot_index = jnp.clip(micro_index, 0, micro_count - 1)
        fresh = lax.dynamic_index_in_dim(grad_final, slot_index, 0, keepdims=False)
        source = jnp.where(section_index == sections - 1, fresh, incoming)

        def backward_compute(store):
            pre_active = lax.dynamic_index_in_dim(pre_store, slot_index, 0, keepdims=False)
            output = unit_backward(source, pre_active, first_flip, second_flip, gain_row, leak_row)
            return (output, lax.dynamic_update_index_in_dim(store, output, slot_index, 0))

        def backward_skip_tick(store):
            return (empty_image, store)

        output, grad_store = lax.cond(is_active, backward_compute, backward_skip_tick, grad_store)
        passed = passed_along(output, "section", -1)
        return ((passed, grad_store), None)

    backward_state = lax.scan(
        backward_tick, (empty_image, grad_start), jnp.arange(tick_count, dtype=jnp.int32)
    )[0]
    return backward_state[1][None]


def solution(mesh):
    placed = (
        P(None, "shard", None, None),
        P("section", None, None),
        P("section", None, None),
        P("section", None),
        P("section", None),
        P("section", None),
        P(),
        P(),
        P("shard", None),
        P(),
        P("shard"),
    )
    return jax.shard_map(
        on_device,
        mesh=mesh,
        in_specs=placed,
        out_specs=P("section", None, "shard", None, None),
        check_vma=False,
    )
```

profile of v0, /device:TPU:1, one launch (start us, length us, event | category | flops | bytes accessed | tf_op | source)
XLA Modules:
  0.0 320.8 jit_solution(4033438780354146733)
XLA Ops:
  1.2 1.7 bitcast_convert_fusion
  4.7 111.3 %while.33 = (s32[]{:T(128)}, bf16[1,196,256]{2,1,0:T(8,128)(2,1)S(1)}, f32[4,1,196,256]{3,2,1,0:T(8,128)}, bf16[4,1,196,256]{3,2,1,0:T(8,128)(2,1)}, s32[11]{0:T...) while((s32[]{:T(128)}, ...), condition=%wide.region_3.4_spmd, body=%wide.region_0.3_spmd.sunk | while | flops 463325440 | bytes 19704256 | solution.py:164
  6.1 4.6 %collective-permute-start = (bf16[1,196,256]{2,1,0:T(8,128)(2,1)S(1)}, bf16[1,196,256]{2,1,0:T(8,128)(2,1)S(1)}, u32[]{:S(2)}, u32[]{:S(2)}) collective-permute-start(bf16[1,196,256]{2,1,0:T(8,128)(2,1)S(1)} %get-tuple-element.869), channel_id=1, source_target_pairs={{0,64},{64,128},{128,192},{192,256},{256,320},{320,384},{384,448},... | collective-permute-start | bytes 301064 | tf_op jit(solution)/shard_map/while/body/eval_jaxpr/ppermute | solution.py:19
  10.7 9.1 %collective-permute-done = bf16[1,196,256]{2,1,0:T(8,128)(2,1)S(1)} collective-permute-done((bf16[1,196,256]{2,1,0:T(8,128)(2,1)S(1)}, bf16[1,196,256]{2,1,0:T(8,128)(2,1)S(1)}, u32[]{:S(2)}, u32[]{:S(2)}) %collective-permute-start) | collective-permute-done | bytes 100384 | tf_op jit(solution)/shard_map/while/body/eval_jaxpr/ppermute | solution.py:19
  21.1 4.8 %conditional.5 = (bf16[1,196,256]{2,1,0:T(8,128)(2,1)S(1)}, f32[4,1,196,256]{3,2,1,0:T(8,128)}, bf16[4,1,196,256]{3,2,1,0:T(8,128)(2,1)}) conditional(s32[]{:T(128)} %convert_element_type.185, (f32[4,1,196,256]{3,2,1,0:T(8,128)}, bf16[4,1,196,256]{3,2,1,0:T(8,128)(2,1)}) %tuple.123, (pred[]{:T(512)}, s32[]{:T(128)}, ...), branch_computations={%region_1.1_spmd, %region_2.2_spmd} | conditional | flops 463325440 | bytes 19302488 | solution.py:158
  25.9 1.9 collective-permute-start
  27.8 1.7 collective-permute-done
  30.8 4.8 %conditional.5 = (bf16[1,196,256]{2,1,0:T(8,128)(2,1)S(1)}, f32[4,1,196,256]{3,2,1,0:T(8,128)}, bf16[4,1,196,256]{3,2,1,0:T(8,128)(2,1)}) conditional(s32[]{:T(128)} %convert_element_type.185, (f32[4,1,196,256]{3,2,1,0:T(8,128)}, bf16[4,1,196,256]{3,2,1,0:T(8,128)(2,1)}) %tuple.123, (pred[]{:T(512)}, s32[]{:T(128)}, ...), branch_computations={%region_1.1_spmd, %region_2.2_spmd} | conditional | flops 463325440 | bytes 19302488 | solution.py:158
  35.6 4.3 %collective-permute-start = (bf16[1,196,256]{2,1,0:T(8,128)(2,1)S(1)}, bf16[1,196,256]{2,1,0:T(8,128)(2,1)S(1)}, u32[]{:S(2)}, u32[]{:S(2)}) collective-permute-start(bf16[1,196,256]{2,1,0:T(8,128)(2,1)S(1)} %get-tuple-element.869), channel_id=1, source_target_pairs={{0,64},{64,128},{128,192},{192,256},{256,320},{320,384},{384,448},... | collective-permute-start | bytes 301064 | tf_op jit(solution)/shard_map/while/body/eval_jaxpr/ppermute | solution.py:19
  39.9 1.7 collective-permute-done
  42.9 4.8 %conditional.5 = (bf16[1,196,256]{2,1,0:T(8,128)(2,1)S(1)}, f32[4,1,196,256]{3,2,1,0:T(8,128)}, bf16[4,1,196,256]{3,2,1,0:T(8,128)(2,1)}) conditional(s32[]{:T(128)} %convert_element_type.185, (f32[4,1,196,256]{3,2,1,0:T(8,128)}, bf16[4,1,196,256]{3,2,1,0:T(8,128)(2,1)}) %tuple.123, (pred[]{:T(512)}, s32[]{:T(128)}, ...), branch_computations={%region_1.1_spmd, %region_2.2_spmd} | conditional | flops 463325440 | bytes 19302488 | solution.py:158
  47.8 4.3 %collective-permute-start = (bf16[1,196,256]{2,1,0:T(8,128)(2,1)S(1)}, bf16[1,196,256]{2,1,0:T(8,128)(2,1)S(1)}, u32[]{:S(2)}, u32[]{:S(2)}) collective-permute-start(bf16[1,196,256]{2,1,0:T(8,128)(2,1)S(1)} %get-tuple-element.869), channel_id=1, source_target_pairs={{0,64},{64,128},{128,192},{192,256},{256,320},{320,384},{384,448},... | collective-permute-start | bytes 301064 | tf_op jit(solution)/shard_map/while/body/eval_jaxpr/ppermute | solution.py:19
  52.1 1.7 collective-permute-done
  55.1 4.8 %conditional.5 = (bf16[1,196,256]{2,1,0:T(8,128)(2,1)S(1)}, f32[4,1,196,256]{3,2,1,0:T(8,128)}, bf16[4,1,196,256]{3,2,1,0:T(8,128)(2,1)}) conditional(s32[]{:T(128)} %convert_element_type.185, (f32[4,1,196,256]{3,2,1,0:T(8,128)}, bf16[4,1,196,256]{3,2,1,0:T(8,128)(2,1)}) %tuple.123, (pred[]{:T(512)}, s32[]{:T(128)}, ...), branch_computations={%region_1.1_spmd, %region_2.2_spmd} | conditional | flops 463325440 | bytes 19302488 | solution.py:158
  59.9 4.3 %collective-permute-start = (bf16[1,196,256]{2,1,0:T(8,128)(2,1)S(1)}, bf16[1,196,256]{2,1,0:T(8,128)(2,1)S(1)}, u32[]{:S(2)}, u32[]{:S(2)}) collective-permute-start(bf16[1,196,256]{2,1,0:T(8,128)(2,1)S(1)} %get-tuple-element.869), channel_id=1, source_target_pairs={{0,64},{64,128},{128,192},{192,256},{256,320},{320,384},{384,448},... | collective-permute-start | bytes 301064 | tf_op jit(solution)/shard_map/while/body/eval_jaxpr/ppermute | solution.py:19
  64.2 1.7 collective-permute-done
  67.2 9.1 %collective-permute-start = (bf16[1,196,256]{2,1,0:T(8,128)(2,1)S(1)}, bf16[1,196,256]{2,1,0:T(8,128)(2,1)S(1)}, u32[]{:S(2)}, u32[]{:S(2)}) collective-permute-start(bf16[1,196,256]{2,1,0:T(8,128)(2,1)S(1)} %get-tuple-element.869), channel_id=1, source_target_pairs={{0,64},{64,128},{128,192},{192,256},{256,320},{320,384},{384,448},... | collective-permute-start | bytes 301064 | tf_op jit(solution)/shard_map/while/body/eval_jaxpr/ppermute | solution.py:19
  76.3 1.7 collective-permute-done
  79.4 4.3 %collective-permute-start = (bf16[1,196,256]{2,1,0:T(8,128)(2,1)S(1)}, bf16[1,196,256]{2,1,0:T(8,128)(2,1)S(1)}, u32[]{:S(2)}, u32[]{:S(2)}) collective-permute-start(bf16[1,196,256]{2,1,0:T(8,128)(2,1)S(1)} %get-tuple-element.869), channel_id=1, source_target_pairs={{0,64},{64,128},{128,192},{192,256},{256,320},{320,384},{384,448},... | collective-permute-start | bytes 301064 | tf_op jit(solution)/shard_map/while/body/eval_jaxpr/ppermute | solution.py:19
  83.7 1.7 collective-permute-done
  86.7 4.3 %collective-permute-start = (bf16[1,196,256]{2,1,0:T(8,128)(2,1)S(1)}, bf16[1,196,256]{2,1,0:T(8,128)(2,1)S(1)}, u32[]{:S(2)}, u32[]{:S(2)}) collective-permute-start(bf16[1,196,256]{2,1,0:T(8,128)(2,1)S(1)} %get-tuple-element.869), channel_id=1, source_target_pairs={{0,64},{64,128},{128,192},{192,256},{256,320},{320,384},{384,448},... | collective-permute-start | bytes 301064 | tf_op jit(solution)/shard_map/while/body/eval_jaxpr/ppermute | solution.py:19
  91.0 1.7 collective-permute-done
  94.1 4.3 %collective-permute-start = (bf16[1,196,256]{2,1,0:T(8,128)(2,1)S(1)}, bf16[1,196,256]{2,1,0:T(8,128)(2,1)S(1)}, u32[]{:S(2)}, u32[]{:S(2)}) collective-permute-start(bf16[1,196,256]{2,1,0:T(8,128)(2,1)S(1)} %get-tuple-element.869), channel_id=1, source_target_pairs={{0,64},{64,128},{128,192},{192,256},{256,320},{320,384},{384,448},... | collective-permute-start | bytes 301064 | tf_op jit(solution)/shard_map/while/body/eval_jaxpr/ppermute | solution.py:19
  98.4 1.7 collective-permute-done
  101.4 5.5 %collective-permute-start = (bf16[1,196,256]{2,1,0:T(8,128)(2,1)S(1)}, bf16[1,196,256]{2,1,0:T(8,128)(2,1)S(1)}, u32[]{:S(2)}, u32[]{:S(2)}) collective-permute-start(bf16[1,196,256]{2,1,0:T(8,128)(2,1)S(1)} %get-tuple-element.869), channel_id=1, source_target_pairs={{0,64},{64,128},{128,192},{192,256},{256,320},{320,384},{384,448},... | collective-permute-start | bytes 301064 | tf_op jit(solution)/shard_map/while/body/eval_jaxpr/ppermute | solution.py:19
  107.0 1.7 collective-permute-done
  110.0 4.3 %collective-permute-start = (bf16[1,196,256]{2,1,0:T(8,128)(2,1)S(1)}, bf16[1,196,256]{2,1,0:T(8,128)(2,1)S(1)}, u32[]{:S(2)}, u32[]{:S(2)}) collective-permute-start(bf16[1,196,256]{2,1,0:T(8,128)(2,1)S(1)} %get-tuple-element.869), channel_id=1, source_target_pairs={{0,64},{64,128},{128,192},{192,256},{256,320},{320,384},{384,448},... | collective-permute-start | bytes 301064 | tf_op jit(solution)/shard_map/while/body/eval_jaxpr/ppermute | solution.py:19
  114.4 1.7 collective-permute-done
  118.7 13.2 %all-to-all-start = ((bf16[64,4,1,512]{3,1,2,0:T(4,128)(2,1)}), bf16[64,4,1,512]{3,1,2,0:T(4,128)(2,1)}, u32[]{:S(2)}, u32[]{:S(2)}) async-start(bf16[64,4,1,512]{3,1,2,0:T(4,128)(2,1)} %broadcast_in_dim.51), calls=%async_computation | async-start | bytes 524288 | tf_op jit(solution)/shard_map/all_to_all | solution.py:24
  134.7 16.3 %all-to-all-done = bf16[64,4,1,512]{3,1,2,0:T(4,128)(2,1)} async-done(((bf16[64,4,1,512]{3,1,2,0:T(4,128)(2,1)}), bf16[64,4,1,512]{3,1,2,0:T(4,128)(2,1)}, u32[]{:S(2)}, u32[]{:S(2)}) %all-to-all-start) | async-done | bytes 262176 | tf_op jit(solution)/shard_map/all_to_all | solution.py:24
  152.0 2.0 fusion.42
  154.3 2.0 convolution_convert_fusion
  157.6 6.2 %all-to-all-start.1 = ((bf16[64,4,1,1025]{3,1,2,0:T(4,128)(2,1)}), bf16[64,4,1,1025]{3,1,2,0:T(4,128)(2,1)S(1)}, u32[]{:S(2)}, u32[]{:S(2)}) async-start(bf16[64,4,1,1025]{3,1,2,0:T(4,128)(2,1)} %maximum_bitcast_fusion), calls=%async_computation.1 | async-start | bytes 1179648 | tf_op jit(solution)/shard_map/all_to_all | solution.py:47
  167.1 30.2 %all-to-all-done.1 = bf16[64,4,1,1025]{3,1,2,0:T(4,128)(2,1)S(1)} async-done(((bf16[64,4,1,1025]{3,1,2,0:T(4,128)(2,1)}), bf16[64,4,1,1025]{3,1,2,0:T(4,128)(2,1)S(1)}, u32[]{:S(2)}, u32[]{:S(2)}) %all-to-all-start.1) | async-done | bytes 524832 | tf_op jit(solution)/shard_map/all_to_all | solution.py:47
  198.1 121.8 %while.34 = (s32[]{:T(128)}, bf16[1,196,256]{2,1,0:T(8,128)(2,1)S(1)}, bf16[4,1,196,256]{3,2,1,0:T(8,128)(2,1)S(1)}, s32[11]{0:T(128)S(1)}, s32[]{:T(128)}, /*in...) while((s32[]{:T(128)}, ...), condition=%wide.region_12.13_spmd.clone, body=%wide.region_9.12_spmd.clone.sunk | while | flops 463475968 | bytes 19926432 | solution.py:236
  199.6 2.9 collective-permute-start.1
  202.5 7.4 %collective-permute-done.1 = bf16[1,196,256]{2,1,0:T(8,128)(2,1)S(1)} collective-permute-done((bf16[1,196,256]{2,1,0:T(8,128)(2,1)S(1)}, bf16[1,196,256]{2,1,0:T(8,128)(2,1)S(1)}, u32[]{:S(2)}, u32[]{:S(2)}) %collective-permute-start.1) | collective-permute-done | bytes 100384 | tf_op jit(solution)/shard_map/while/body/eval_jaxpr/ppermute | solution.py:19
  211.3 1.9 collective-permute-start.1
  213.2 4.0 %collective-permute-done.1 = bf16[1,196,256]{2,1,0:T(8,128)(2,1)S(1)} collective-permute-done((bf16[1,196,256]{2,1,0:T(8,128)(2,1)S(1)}, bf16[1,196,256]{2,1,0:T(8,128)(2,1)S(1)}, u32[]{:S(2)}, u32[]{:S(2)}) %collective-permute-start.1) | collective-permute-done | bytes 100384 | tf_op jit(solution)/shard_map/while/body/eval_jaxpr/ppermute | solution.py:19
  218.7 1.9 collective-permute-start.1
  220.7 5.8 %collective-permute-done.1 = bf16[1,196,256]{2,1,0:T(8,128)(2,1)S(1)} collective-permute-done((bf16[1,196,256]{2,1,0:T(8,128)(2,1)S(1)}, bf16[1,196,256]{2,1,0:T(8,128)(2,1)S(1)}, u32[]{:S(2)}, u32[]{:S(2)}) %collective-permute-start.1) | collective-permute-done | bytes 100384 | tf_op jit(solution)/shard_map/while/body/eval_jaxpr/ppermute | solution.py:19
  227.9 1.9 collective-permute-start.1
  229.9 4.0 %collective-permute-done.1 = bf16[1,196,256]{2,1,0:T(8,128)(2,1)S(1)} collective-permute-done((bf16[1,196,256]{2,1,0:T(8,128)(2,1)S(1)}, bf16[1,196,256]{2,1,0:T(8,128)(2,1)S(1)}, u32[]{:S(2)}, u32[]{:S(2)}) %collective-permute-start.1) | collective-permute-done | bytes 100384 | tf_op jit(solution)/shard_map/while/body/eval_jaxpr/ppermute | solution.py:19
  235.4 1.9 collective-permute-start.1
  237.3 4.0 %collective-permute-done.1 = bf16[1,196,256]{2,1,0:T(8,128)(2,1)S(1)} collective-permute-done((bf16[1,196,256]{2,1,0:T(8,128)(2,1)S(1)}, bf16[1,196,256]{2,1,0:T(8,128)(2,1)S(1)}, u32[]{:S(2)}, u32[]{:S(2)}) %collective-permute-start.1) | collective-permute-done | bytes 100384 | tf_op jit(solution)/shard_map/while/body/eval_jaxpr/ppermute | solution.py:19
  242.8 1.9 collective-permute-start.1
  244.7 21.1 %collective-permute-done.1 = bf16[1,196,256]{2,1,0:T(8,128)(2,1)S(1)} collective-permute-done((bf16[1,196,256]{2,1,0:T(8,128)(2,1)S(1)}, bf16[1,196,256]{2,1,0:T(8,128)(2,1)S(1)}, u32[]{:S(2)}, u32[]{:S(2)}) %collective-permute-start.1) | collective-permute-done | bytes 100384 | tf_op jit(solution)/shard_map/while/body/eval_jaxpr/ppermute | solution.py:19
  267.3 4.3 %conditional.6 = (bf16[1,196,256]{2,1,0:T(8,128)(2,1)S(1)}, bf16[4,1,196,256]{3,2,1,0:T(8,128)(2,1)S(1)}) conditional(s32[]{:T(128)} %convert_element_type.187, bf16[4,1,196,256]{3,2,1,0:T(8,128)(2,1)S(1)} %get-tuple-element.968, (pred[]{:T(512)}, s32[]{:T(128)}, bf16[4,1,196,256]{3,2,1,0:T(8,128)(2,1)S(1)}, bf16[1,196,256]{2,1,0:T(8,128)(2,1)S(1)}, ...), branch_computations={%region_10.10_spmd, %region_11.11_spmd} | conditional | flops 463074560 | bytes 18918480 | solution.py:232
  269.1 1.4 fusion.12
  271.6 1.9 collective-permute-start.1
  273.5 4.0 %collective-permute-done.1 = bf16[1,196,256]{2,1,0:T(8,128)(2,1)S(1)} collective-permute-done((bf16[1,196,256]{2,1,0:T(8,128)(2,1)S(1)}, bf16[1,196,256]{2,1,0:T(8,128)(2,1)S(1)}, u32[]{:S(2)}, u32[]{:S(2)}) %collective-permute-start.1) | collective-permute-done | bytes 100384 | tf_op jit(solution)/shard_map/while/body/eval_jaxpr/ppermute | solution.py:19
  278.9 4.3 %conditional.6 = (bf16[1,196,256]{2,1,0:T(8,128)(2,1)S(1)}, bf16[4,1,196,256]{3,2,1,0:T(8,128)(2,1)S(1)}) conditional(s32[]{:T(128)} %convert_element_type.187, bf16[4,1,196,256]{3,2,1,0:T(8,128)(2,1)S(1)} %get-tuple-element.968, (pred[]{:T(512)}, s32[]{:T(128)}, bf16[4,1,196,256]{3,2,1,0:T(8,128)(2,1)S(1)}, bf16[1,196,256]{2,1,0:T(8,128)(2,1)S(1)}, ...), branch_computations={%region_10.10_spmd, %region_11.11_spmd} | conditional | flops 463074560 | bytes 18918480 | solution.py:232
  280.8 1.4 fusion.12
  283.2 1.9 collective-permute-start.1
  285.1 4.0 %collective-permute-done.1 = bf16[1,196,256]{2,1,0:T(8,128)(2,1)S(1)} collective-permute-done((bf16[1,196,256]{2,1,0:T(8,128)(2,1)S(1)}, bf16[1,196,256]{2,1,0:T(8,128)(2,1)S(1)}, u32[]{:S(2)}, u32[]{:S(2)}) %collective-permute-start.1) | collective-permute-done | bytes 100384 | tf_op jit(solution)/shard_map/while/body/eval_jaxpr/ppermute | solution.py:19
  290.6 4.3 %conditional.6 = (bf16[1,196,256]{2,1,0:T(8,128)(2,1)S(1)}, bf16[4,1,196,256]{3,2,1,0:T(8,128)(2,1)S(1)}) conditional(s32[]{:T(128)} %convert_element_type.187, bf16[4,1,196,256]{3,2,1,0:T(8,128)(2,1)S(1)} %get-tuple-element.968, (pred[]{:T(512)}, s32[]{:T(128)}, bf16[4,1,196,256]{3,2,1,0:T(8,128)(2,1)S(1)}, bf16[1,196,256]{2,1,0:T(8,128)(2,1)S(1)}, ...), branch_computations={%region_10.10_spmd, %region_11.11_spmd} | conditional | flops 463074560 | bytes 18918480 | solution.py:232
  292.4 1.4 fusion.12
  294.9 1.9 collective-permute-start.1
  296.8 4.0 %collective-permute-done.1 = bf16[1,196,256]{2,1,0:T(8,128)(2,1)S(1)} collective-permute-done((bf16[1,196,256]{2,1,0:T(8,128)(2,1)S(1)}, bf16[1,196,256]{2,1,0:T(8,128)(2,1)S(1)}, u32[]{:S(2)}, u32[]{:S(2)}) %collective-permute-start.1) | collective-permute-done | bytes 100384 | tf_op jit(solution)/shard_map/while/body/eval_jaxpr/ppermute | solution.py:19
  302.2 4.3 %conditional.6 = (bf16[1,196,256]{2,1,0:T(8,128)(2,1)S(1)}, bf16[4,1,196,256]{3,2,1,0:T(8,128)(2,1)S(1)}) conditional(s32[]{:T(128)} %convert_element_type.187, bf16[4,1,196,256]{3,2,1,0:T(8,128)(2,1)S(1)} %get-tuple-element.968, (pred[]{:T(512)}, s32[]{:T(128)}, bf16[4,1,196,256]{3,2,1,0:T(8,128)(2,1)S(1)}, bf16[1,196,256]{2,1,0:T(8,128)(2,1)S(1)}, ...), branch_computations={%region_10.10_spmd, %region_11.11_spmd} | conditional | flops 463074560 | bytes 18918480 | solution.py:232
  306.5 1.9 collective-permute-start.1
  308.4 4.0 %collective-permute-done.1 = bf16[1,196,256]{2,1,0:T(8,128)(2,1)S(1)} collective-permute-done((bf16[1,196,256]{2,1,0:T(8,128)(2,1)S(1)}, bf16[1,196,256]{2,1,0:T(8,128)(2,1)S(1)}, u32[]{:S(2)}, u32[]{:S(2)}) %collective-permute-start.1) | collective-permute-done | bytes 100384 | tf_op jit(solution)/shard_map/while/body/eval_jaxpr/ppermute | solution.py:19
  313.9 3.4 %collective-permute-start.1 = (bf16[1,196,256]{2,1,0:T(8,128)(2,1)S(1)}, bf16[1,196,256]{2,1,0:T(8,128)(2,1)S(1)}, u32[]{:S(2)}, u32[]{:S(2)}) collective-permute-start(bf16[1,196,256]{2,1,0:T(8,128)(2,1)S(1)} %get-tuple-element.886), channel_id=1, source_target_pairs={{64,0},{128,64},{192,128},{256,192},{320,256},{384,320},{448,384},... | collective-permute-start | bytes 301064 | tf_op jit(solution)/shard_map/while/body/eval_jaxpr/ppermute | solution.py:19
  317.3 2.6 collective-permute-done.1
  (466 shorter events, 60.3 us)
Async XLA Ops:
  0.0 117.5 %copy-start = (bf16[256,512]{1,0:T(8,128)(2,1)S(1)}, bf16[256,512]{1,0:T(8,128)(2,1)}, u32[]{:S(2)}) copy-start(bf16[256,512]{1,0:T(8,128)(2,1)} %param.26) | copy-start | bytes 786436
  0.0 4.7 %copy-start.7 = (f32[1,256]{1,0:T(1,128)S(1)}, f32[1,256]{1,0:T(1,128)}, u32[]{:S(2)}) copy-start(f32[1,256]{1,0:T(1,128)} %param.24) | copy-start | bytes 3076
  0.0 4.7 %copy-start.10 = (f32[1,256]{1,0:T(1,128)S(1)}, f32[1,256]{1,0:T(1,128)}, u32[]{:S(2)}) copy-start(f32[1,256]{1,0:T(1,128)} %param.22) | copy-start | bytes 3076
  0.0 4.7 %copy-start.1 = (bf16[1,2304,256]{2,1,0:T(8,128)(2,1)S(1)}, bf16[1,2304,256]{2,1,0:T(8,128)(2,1)}, u32[]{:S(2)}) copy-start(bf16[1,2304,256]{2,1,0:T(8,128)(2,1)} %param.21) | copy-start | bytes 3538948
  0.0 4.6 %copy-start.9 = (f32[1,256]{1,0:T(1,128)S(1)}, f32[1,256]{1,0:T(1,128)}, u32[]{:S(2)}) copy-start(f32[1,256]{1,0:T(1,128)} %param.23) | copy-start | bytes 3076
  6.1 13.7 %collective-permute-start = (bf16[1,196,256]{2,1,0:T(8,128)(2,1)S(1)}, bf16[1,196,256]{2,1,0:T(8,128)(2,1)S(1)}, u32[]{:S(2)}, u32[]{:S(2)}) collective-permute-start(bf16[1,196,256]{2,1,0:T(8,128)(2,1)S(1)} %get-tuple-element.869), channel_id=1, source_target_pairs={{0,64},{64,128},{128,192},{192,256},{256,320},{320,384},{384,448},... | collective-permute-start | bytes 301064 | tf_op jit(solution)/shard_map/while/body/eval_jaxpr/ppermute | solution.py:19
  21.6 1.3 copy-start.3
  25.9 3.6 %collective-permute-start = (bf16[1,196,256]{2,1,0:T(8,128)(2,1)S(1)}, bf16[1,196,256]{2,1,0:T(8,128)(2,1)S(1)}, u32[]{:S(2)}, u32[]{:S(2)}) collective-permute-start(bf16[1,196,256]{2,1,0:T(8,128)(2,1)S(1)} %get-tuple-element.869), channel_id=1, source_target_pairs={{0,64},{64,128},{128,192},{192,256},{256,320},{320,384},{384,448},... | collective-permute-start | bytes 301064 | tf_op jit(solution)/shard_map/while/body/eval_jaxpr/ppermute | solution.py:19
  31.4 1.3 copy-start.3
  35.6 6.0 %collective-permute-start = (bf16[1,196,256]{2,1,0:T(8,128)(2,1)S(1)}, bf16[1,196,256]{2,1,0:T(8,128)(2,1)S(1)}, u32[]{:S(2)}, u32[]{:S(2)}) collective-permute-start(bf16[1,196,256]{2,1,0:T(8,128)(2,1)S(1)} %get-tuple-element.869), channel_id=1, source_target_pairs={{0,64},{64,128},{128,192},{192,256},{256,320},{320,384},{384,448},... | collective-permute-start | bytes 301064 | tf_op jit(solution)/shard_map/while/body/eval_jaxpr/ppermute | solution.py:19
  43.5 1.3 copy-start.3
  47.8 6.0 %collective-permute-start = (bf16[1,196,256]{2,1,0:T(8,128)(2,1)S(1)}, bf16[1,196,256]{2,1,0:T(8,128)(2,1)S(1)}, u32[]{:S(2)}, u32[]{:S(2)}) collective-permute-start(bf16[1,196,256]{2,1,0:T(8,128)(2,1)S(1)} %get-tuple-element.869), channel_id=1, source_target_pairs={{0,64},{64,128},{128,192},{192,256},{256,320},{320,384},{384,448},... | collective-permute-start | bytes 301064 | tf_op jit(solution)/shard_map/while/body/eval_jaxpr/ppermute | solution.py:19
  55.6 1.3 copy-start.3
  59.9 6.0 %collective-permute-start = (bf16[1,196,256]{2,1,0:T(8,128)(2,1)S(1)}, bf16[1,196,256]{2,1,0:T(8,128)(2,1)S(1)}, u32[]{:S(2)}, u32[]{:S(2)}) collective-permute-start(bf16[1,196,256]{2,1,0:T(8,128)(2,1)S(1)} %get-tuple-element.869), channel_id=1, source_target_pairs={{0,64},{64,128},{128,192},{192,256},{256,320},{320,384},{384,448},... | collective-permute-start | bytes 301064 | tf_op jit(solution)/shard_map/while/body/eval_jaxpr/ppermute | solution.py:19
  67.2 10.7 %collective-permute-start = (bf16[1,196,256]{2,1,0:T(8,128)(2,1)S(1)}, bf16[1,196,256]{2,1,0:T(8,128)(2,1)S(1)}, u32[]{:S(2)}, u32[]{:S(2)}) collective-permute-start(bf16[1,196,256]{2,1,0:T(8,128)(2,1)S(1)} %get-tuple-element.869), channel_id=1, source_target_pairs={{0,64},{64,128},{128,192},{192,256},{256,320},{320,384},{384,448},... | collective-permute-start | bytes 301064 | tf_op jit(solution)/shard_map/while/body/eval_jaxpr/ppermute | solution.py:19
  79.4 6.0 %collective-permute-start = (bf16[1,196,256]{2,1,0:T(8,128)(2,1)S(1)}, bf16[1,196,256]{2,1,0:T(8,128)(2,1)S(1)}, u32[]{:S(2)}, u32[]{:S(2)}) collective-permute-start(bf16[1,196,256]{2,1,0:T(8,128)(2,1)S(1)} %get-tuple-element.869), channel_id=1, source_target_pairs={{0,64},{64,128},{128,192},{192,256},{256,320},{320,384},{384,448},... | collective-permute-start | bytes 301064 | tf_op jit(solution)/shard_map/while/body/eval_jaxpr/ppermute | solution.py:19
  86.7 6.0 %collective-permute-start = (bf16[1,196,256]{2,1,0:T(8,128)(2,1)S(1)}, bf16[1,196,256]{2,1,0:T(8,128)(2,1)S(1)}, u32[]{:S(2)}, u32[]{:S(2)}) collective-permute-start(bf16[1,196,256]{2,1,0:T(8,128)(2,1)S(1)} %get-tuple-element.869), channel_id=1, source_target_pairs={{0,64},{64,128},{128,192},{192,256},{256,320},{320,384},{384,448},... | collective-permute-start | bytes 301064 | tf_op jit(solution)/shard_map/while/body/eval_jaxpr/ppermute | solution.py:19
  94.1 6.0 %collective-permute-start = (bf16[1,196,256]{2,1,0:T(8,128)(2,1)S(1)}, bf16[1,196,256]{2,1,0:T(8,128)(2,1)S(1)}, u32[]{:S(2)}, u32[]{:S(2)}) collective-permute-start(bf16[1,196,256]{2,1,0:T(8,128)(2,1)S(1)} %get-tuple-element.869), channel_id=1, source_target_pairs={{0,64},{64,128},{128,192},{192,256},{256,320},{320,384},{384,448},... | collective-permute-start | bytes 301064 | tf_op jit(solution)/shard_map/while/body/eval_jaxpr/ppermute | solution.py:19
  101.4 7.2 %collective-permute-start = (bf16[1,196,256]{2,1,0:T(8,128)(2,1)S(1)}, bf16[1,196,256]{2,1,0:T(8,128)(2,1)S(1)}, u32[]{:S(2)}, u32[]{:S(2)}) collective-permute-start(bf16[1,196,256]{2,1,0:T(8,128)(2,1)S(1)} %get-tuple-element.869), channel_id=1, source_target_pairs={{0,64},{64,128},{128,192},{192,256},{256,320},{320,384},{384,448},... | collective-permute-start | bytes 301064 | tf_op jit(solution)/shard_map/while/body/eval_jaxpr/ppermute | solution.py:19
  110.0 6.0 %collective-permute-start = (bf16[1,196,256]{2,1,0:T(8,128)(2,1)S(1)}, bf16[1,196,256]{2,1,0:T(8,128)(2,1)S(1)}, u32[]{:S(2)}, u32[]{:S(2)}) collective-permute-start(bf16[1,196,256]{2,1,0:T(8,128)(2,1)S(1)} %get-tuple-element.869), channel_id=1, source_target_pairs={{0,64},{64,128},{128,192},{192,256},{256,320},{320,384},{384,448},... | collective-permute-start | bytes 301064 | tf_op jit(solution)/shard_map/while/body/eval_jaxpr/ppermute | solution.py:19
  116.0 16.5 %copy-start.8 = (s32[4,64]{1,0:T(4,128)S(1)}, s32[4,64]{1,0:T(4,128)}, u32[]{:S(2)}) copy-start(s32[4,64]{1,0:T(4,128)} %param.28) | copy-start | bytes 3076
  116.0 16.6 %copy-start.2 = (bf16[1664,512]{1,0:T(8,128)(2,1)S(1)}, bf16[1664,512]{1,0:T(8,128)(2,1)}, u32[]{:S(2)}) copy-start(bf16[1664,512]{1,0:T(8,128)(2,1)} %param.27) | copy-start | bytes 5111812
  118.7 32.4 %all-to-all-start = ((bf16[64,4,1,512]{3,1,2,0:T(4,128)(2,1)}), bf16[64,4,1,512]{3,1,2,0:T(4,128)(2,1)}, u32[]{:S(2)}, u32[]{:S(2)}) async-start(bf16[64,4,1,512]{3,1,2,0:T(4,128)(2,1)} %broadcast_in_dim.51), calls=%async_computation | async-start | bytes 524288 | tf_op jit(solution)/shard_map/all_to_all | solution.py:24
  154.3 2.2 copy-start.6
  157.6 39.7 %all-to-all-start.1 = ((bf16[64,4,1,1025]{3,1,2,0:T(4,128)(2,1)}), bf16[64,4,1,1025]{3,1,2,0:T(4,128)(2,1)S(1)}, u32[]{:S(2)}, u32[]{:S(2)}) async-start(bf16[64,4,1,1025]{3,1,2,0:T(4,128)(2,1)} %maximum_bitcast_fusion), calls=%async_computation.1 | async-start | bytes 1179648 | tf_op jit(solution)/shard_map/all_to_all | solution.py:47
  164.6 1.7 copy-start.4
  199.6 10.3 %collective-permute-start.1 = (bf16[1,196,256]{2,1,0:T(8,128)(2,1)S(1)}, bf16[1,196,256]{2,1,0:T(8,128)(2,1)S(1)}, u32[]{:S(2)}, u32[]{:S(2)}) collective-permute-start(bf16[1,196,256]{2,1,0:T(8,128)(2,1)S(1)} %get-tuple-element.886), channel_id=1, source_target_pairs={{64,0},{128,64},{192,128},{256,192},{320,256},{384,320},{448,384},... | collective-permute-start | bytes 301064 | tf_op jit(solution)/shard_map/while/body/eval_jaxpr/ppermute | solution.py:19
  211.3 6.0 %collective-permute-start.1 = (bf16[1,196,256]{2,1,0:T(8,128)(2,1)S(1)}, bf16[1,196,256]{2,1,0:T(8,128)(2,1)S(1)}, u32[]{:S(2)}, u32[]{:S(2)}) collective-permute-start(bf16[1,196,256]{2,1,0:T(8,128)(2,1)S(1)} %get-tuple-element.886), channel_id=1, source_target_pairs={{64,0},{128,64},{192,128},{256,192},{320,256},{384,320},{448,384},... | collective-permute-start | bytes 301064 | tf_op jit(solution)/shard_map/while/body/eval_jaxpr/ppermute | solution.py:19
  218.7 7.8 %collective-permute-start.1 = (bf16[1,196,256]{2,1,0:T(8,128)(2,1)S(1)}, bf16[1,196,256]{2,1,0:T(8,128)(2,1)S(1)}, u32[]{:S(2)}, u32[]{:S(2)}) collective-permute-start(bf16[1,196,256]{2,1,0:T(8,128)(2,1)S(1)} %get-tuple-element.886), channel_id=1, source_target_pairs={{64,0},{128,64},{192,128},{256,192},{320,256},{384,320},{448,384},... | collective-permute-start | bytes 301064 | tf_op jit(solution)/shard_map/while/body/eval_jaxpr/ppermute | solution.py:19
  227.9 6.0 %collective-permute-start.1 = (bf16[1,196,256]{2,1,0:T(8,128)(2,1)S(1)}, bf16[1,196,256]{2,1,0:T(8,128)(2,1)S(1)}, u32[]{:S(2)}, u32[]{:S(2)}) collective-permute-start(bf16[1,196,256]{2,1,0:T(8,128)(2,1)S(1)} %get-tuple-element.886), channel_id=1, source_target_pairs={{64,0},{128,64},{192,128},{256,192},{320,256},{384,320},{448,384},... | collective-permute-start | bytes 301064 | tf_op jit(solution)/shard_map/while/body/eval_jaxpr/ppermute | solution.py:19
  235.4 6.0 %collective-permute-start.1 = (bf16[1,196,256]{2,1,0:T(8,128)(2,1)S(1)}, bf16[1,196,256]{2,1,0:T(8,128)(2,1)S(1)}, u32[]{:S(2)}, u32[]{:S(2)}) collective-permute-start(bf16[1,196,256]{2,1,0:T(8,128)(2,1)S(1)} %get-tuple-element.886), channel_id=1, source_target_pairs={{64,0},{128,64},{192,128},{256,192},{320,256},{384,320},{448,384},... | collective-permute-start | bytes 301064 | tf_op jit(solution)/shard_map/while/body/eval_jaxpr/ppermute | solution.py:19
  242.8 23.1 %collective-permute-start.1 = (bf16[1,196,256]{2,1,0:T(8,128)(2,1)S(1)}, bf16[1,196,256]{2,1,0:T(8,128)(2,1)S(1)}, u32[]{:S(2)}, u32[]{:S(2)}) collective-permute-start(bf16[1,196,256]{2,1,0:T(8,128)(2,1)S(1)} %get-tuple-element.886), channel_id=1, source_target_pairs={{64,0},{128,64},{192,128},{256,192},{320,256},{384,320},{448,384},... | collective-permute-start | bytes 301064 | tf_op jit(solution)/shard_map/while/body/eval_jaxpr/ppermute | solution.py:19
  267.8 1.3 copy-start.5
  271.6 6.0 %collective-permute-start.1 = (bf16[1,196,256]{2,1,0:T(8,128)(2,1)S(1)}, bf16[1,196,256]{2,1,0:T(8,128)(2,1)S(1)}, u32[]{:S(2)}, u32[]{:S(2)}) collective-permute-start(bf16[1,196,256]{2,1,0:T(8,128)(2,1)S(1)} %get-tuple-element.886), channel_id=1, source_target_pairs={{64,0},{128,64},{192,128},{256,192},{320,256},{384,320},{448,384},... | collective-permute-start | bytes 301064 | tf_op jit(solution)/shard_map/while/body/eval_jaxpr/ppermute | solution.py:19
  279.5 1.3 copy-start.5
  283.2 6.0 %collective-permute-start.1 = (bf16[1,196,256]{2,1,0:T(8,128)(2,1)S(1)}, bf16[1,196,256]{2,1,0:T(8,128)(2,1)S(1)}, u32[]{:S(2)}, u32[]{:S(2)}) collective-permute-start(bf16[1,196,256]{2,1,0:T(8,128)(2,1)S(1)} %get-tuple-element.886), channel_id=1, source_target_pairs={{64,0},{128,64},{192,128},{256,192},{320,256},{384,320},{448,384},... | collective-permute-start | bytes 301064 | tf_op jit(solution)/shard_map/while/body/eval_jaxpr/ppermute | solution.py:19
  291.1 1.3 copy-start.5
  294.9 6.0 %collective-permute-start.1 = (bf16[1,196,256]{2,1,0:T(8,128)(2,1)S(1)}, bf16[1,196,256]{2,1,0:T(8,128)(2,1)S(1)}, u32[]{:S(2)}, u32[]{:S(2)}) collective-permute-start(bf16[1,196,256]{2,1,0:T(8,128)(2,1)S(1)} %get-tuple-element.886), channel_id=1, source_target_pairs={{64,0},{128,64},{192,128},{256,192},{320,256},{384,320},{448,384},... | collective-permute-start | bytes 301064 | tf_op jit(solution)/shard_map/while/body/eval_jaxpr/ppermute | solution.py:19
  302.8 1.3 copy-start.5
  306.5 6.0 %collective-permute-start.1 = (bf16[1,196,256]{2,1,0:T(8,128)(2,1)S(1)}, bf16[1,196,256]{2,1,0:T(8,128)(2,1)S(1)}, u32[]{:S(2)}, u32[]{:S(2)}) collective-permute-start(bf16[1,196,256]{2,1,0:T(8,128)(2,1)S(1)} %get-tuple-element.886), channel_id=1, source_target_pairs={{64,0},{128,64},{192,128},{256,192},{320,256},{384,320},{448,384},... | collective-permute-start | bytes 301064 | tf_op jit(solution)/shard_map/while/body/eval_jaxpr/ppermute | solution.py:19
  313.9 6.0 %collective-permute-start.1 = (bf16[1,196,256]{2,1,0:T(8,128)(2,1)S(1)}, bf16[1,196,256]{2,1,0:T(8,128)(2,1)S(1)}, u32[]{:S(2)}, u32[]{:S(2)}) collective-permute-start(bf16[1,196,256]{2,1,0:T(8,128)(2,1)S(1)} %get-tuple-element.886), channel_id=1, source_target_pairs={{64,0},{128,64},{192,128},{256,192},{320,256},{384,320},{448,384},... | collective-permute-start | bytes 301064 | tf_op jit(solution)/shard_map/while/body/eval_jaxpr/ppermute | solution.py:19
where the time goes:
time: 322 us; the launch traced here: 321 us
  waiting for transfers between devices  137 us (43%)
  starting transfers between devices  94.2 us (29%)
  local copies, waits for them, and re-layouts  44.5 us (14%)
  matrix products  19 us (6%)
  loops' own time  18.9 us (6%)
  other arithmetic  5.99 us (2%)
    ppermute x22, waiting for transfers between devices, passed_along(): lax.ppermute(value, axis, [(source, source + steps) for source in range(i...  90.9 us
    ppermute x22, starting transfers between devices, passed_along(): lax.ppermute(value, axis, [(source, source + steps) for source in range(i...  74.8 us
    all_to_all x1, waiting for transfers between devices, sum_at_owner(): lax.all_to_all(cut_along(shard, dim, length), axis, 0, 0, tiled=True)  30.2 us
    all_to_all x1, waiting for transfers between devices, sent_to_all(): lax.all_to_all(jnp.broadcast_to(shard[None], (length, *shard.shape)), axi...  16.3 us
    dynamic_slice x22, local copies, waits for them, and re-layouts, on_device(): lax.scan(forward_tick, (empty_image, pre_start, out_start), jnp.arange(ti...  14.3 us
    dot_general x16, matrix products, conv_apply(): result = jnp.dot(columns, weights, preferred_element_type=jnp.float32)  13.8 us
    all_to_all x1, starting transfers between devices, sent_to_all(): lax.all_to_all(jnp.broadcast_to(shard[None], (length, *shard.shape)), axi...  13.2 us
    cond x144, local copies, waits for them, and re-layouts  10.1 us
  transfers between devices with their start and end apart: 24, of which 24 were waited for; matrix products, arithmetic and copies ran while one was open for 2% of the time, Pallas kernels for 0%

commit v1 on v0

v1 whole, which is shorter than its diff:
```python
import functools
import math

import jax
import jax.numpy as jnp
from jax import lax
from jax.experimental import pallas as pl
from jax.experimental.pallas import tpu as pltpu
from jax.sharding import PartitionSpec as P

SIDE = 14
WIDE = 16
ROWS = SIDE * WIDE
C = 256

margin_value = 0.4
scale_value = 64.0
tiny_value = 1e-06

VM = pl.BlockSpec(memory_space=pltpu.VMEM)
SM = pl.BlockSpec(memory_space=pltpu.SMEM)
LIMIT = 20 * 1024 * 1024


def in_vmem(x):
    return pltpu.with_memory_space_constraint(x, pltpu.VMEM)


def keep_columns(rows):
    return (lax.broadcasted_iota(jnp.int32, (rows, C), 0) % WIDE) < SIDE


def clear_border(cols):
    zero = jnp.zeros((cols.shape[0], WIDE, cols.shape[2]), cols.dtype)
    cols[:, 0:WIDE, :] = zero
    cols[:, WIDE + ROWS : 2 * WIDE + ROWS, :] = zero


def conv(value, weights, cols):
    images = cols.shape[0]
    total = images * ROWS
    before = pltpu.roll(value, 1, 0)
    after = pltpu.roll(value, total - 1, 0)
    for place, part in enumerate((before, value, after)):
        cols[:, WIDE : WIDE + ROWS, place * C : (place + 1) * C] = part.astype(jnp.bfloat16).reshape(
            images, ROWS, C
        )
    acc = None
    for step in range(3):
        left = cols[:, WIDE * step : WIDE * step + ROWS, :].reshape(total, 3 * C)
        part = jnp.dot(
            left, weights[step * 3 * C : (step + 1) * 3 * C, :], preferred_element_type=jnp.float32
        )
        acc = part if acc is None else acc + part
    return acc


def forward_body(flag, x_ref, w1_ref, w2_ref, vec_ref, z_in, out_ref, z_ref, cols, run):
    images = cols.shape[0]
    total = images * ROWS

    @pl.when(flag[0] == 1)
    def _():
        clear_border(cols)
        keep = keep_columns(total)
        run[...] = x_ref[...].astype(jnp.float32).reshape(total, C)

        def one(u, carry):
            value = run[...]
            hidden = conv(value, w1_ref.at[u], cols)
            vec = vec_ref[u]
            pre = hidden * vec[0:1] + vec[1:2]
            z_ref[u] = pre
            leak = vec[2:3]
            four = 4.0 * pre
            soft = jnp.maximum(four, 0.0) + jnp.log1p(jnp.exp(-jnp.abs(four)))
            active = leak * pre + (1.0 - leak) * soft * 0.25
            active = jnp.where(keep, active, 0.0)
            result = run[...] + conv(active, w2_ref.at[u], cols)
            result = jnp.where(keep, result, 0.0).astype(jnp.bfloat16)
            run[...] = result.astype(jnp.float32)
            return carry

        lax.fori_loop(0, 2, one, 0)
        out_ref[...] = run[...].astype(jnp.bfloat16).reshape(images, ROWS, C)


def backward_body(flag, g_ref, f1_ref, f2_ref, vec_ref, z_ref, store_in, out_ref, store, cols, run):
    images = cols.shape[0]
    total = images * ROWS

    @pl.when(flag[0] == 1)
    def _():
        clear_border(cols)
        keep = keep_columns(total)
        run[...] = g_ref[...].astype(jnp.float32).reshape(total, C)

        def one(step, carry):
            u = 1 - step
            grad_active = conv(run[...], f2_ref.at[u], cols)
            vec = vec_ref[u]
            pre = z_ref[u]
            leak = vec[2:3]
            slope = leak + (1.0 - leak) / (1.0 + jnp.exp(-4.0 * pre))
            grad_hidden = jnp.where(keep, grad_active * slope * vec[0:1], 0.0)
            result = run[...] + conv(grad_hidden, f1_ref.at[u], cols)
            result = jnp.where(keep, result, 0.0).astype(jnp.bfloat16)
            run[...] = result.astype(jnp.float32)
            store[u] = result.reshape(images, ROWS, C)
            return carry

        lax.fori_loop(0, 2, one, 0)
        out_ref[...] = run[...].astype(jnp.bfloat16).reshape(images, ROWS, C)


CONV_COST = pl.CostEstimate(flops=4 * 2 * 448 * 2304 * 256, bytes_accessed=6_000_000, transcendentals=500_000)


def forward_stage(flag, x, w1, w2, vec, z):
    images = x.shape[0]
    return pl.pallas_call(
        forward_body,
        in_specs=[SM, VM, VM, VM, VM, VM],
        out_specs=[VM, VM],
        out_shape=[jax.ShapeDtypeStruct(x.shape, jnp.bfloat16), jax.ShapeDtypeStruct(z.shape, z.dtype)],
        scratch_shapes=[
            pltpu.VMEM((images, ROWS + 2 * WIDE, 3 * C), jnp.bfloat16),
            pltpu.VMEM((images * ROWS, C), jnp.float32),
        ],
        input_output_aliases={5: 1},
        compiler_params=pltpu.CompilerParams(vmem_limit_bytes=LIMIT),
        cost_estimate=CONV_COST,
        name="forward_stage",
    )(flag, in_vmem(x), in_vmem(w1), in_vmem(w2), in_vmem(vec), in_vmem(z))


def backward_stage(flag, g, f1, f2, vec, z, store):
    images = g.shape[0]
    return pl.pallas_call(
        backward_body,
        in_specs=[SM, VM, VM, VM, VM, VM, VM],
        out_specs=[VM, VM],
        out_shape=[
            jax.ShapeDtypeStruct(g.shape, jnp.bfloat16),
            jax.ShapeDtypeStruct(store.shape, store.dtype),
        ],
        scratch_shapes=[
            pltpu.VMEM((images, ROWS + 2 * WIDE, 3 * C), jnp.bfloat16),
            pltpu.VMEM((images * ROWS, C), jnp.float32),
        ],
        input_output_aliases={6: 1},
        compiler_params=pltpu.CompilerParams(vmem_limit_bytes=LIMIT),
        cost_estimate=CONV_COST,
        name="backward_stage",
    )(flag, in_vmem(g), in_vmem(f1), in_vmem(f2), in_vmem(vec), in_vmem(z), in_vmem(store))


def flip_body(w1_ref, w2_ref, f1_ref, f2_ref):
    eye = (
        lax.broadcasted_iota(jnp.int32, (C, C), 0) == lax.broadcasted_iota(jnp.int32, (C, C), 1)
    ).astype(jnp.float32).astype(jnp.bfloat16)
    for source, target in ((w1_ref, f1_ref), (w2_ref, f2_ref)):

        def one(u, carry):
            for tap in range(9):
                block = source[u, tap * C : (tap + 1) * C, :]
                turned = lax.dot_general(
                    eye, block, (((1,), (1,)), ((), ())), preferred_element_type=jnp.float32
                )
                target[u, (8 - tap) * C : (9 - tap) * C, :] = turned.astype(jnp.bfloat16)
            return carry

        lax.fori_loop(0, 2, one, 0)


def flip_all(w1, w2):
    return pl.pallas_call(
        flip_body,
        in_specs=[VM, VM],
        out_specs=[VM, VM],
        out_shape=[jax.ShapeDtypeStruct(w1.shape, w1.dtype)] * 2,
        compiler_params=pltpu.CompilerParams(vmem_limit_bytes=LIMIT),
        cost_estimate=pl.CostEstimate(flops=36 * 2 * 256**3, bytes_accessed=9_000_000, transcendentals=0),
        name="flip_all",
    )(in_vmem(w1), in_vmem(w2))


def unit_scale(values):
    squares = jnp.mean(values * values, axis=-1, keepdims=True)
    factor = lax.rsqrt(squares + tiny_value) / math.sqrt(values.shape[-1])
    return (values * factor, squares, factor)


def on_device(
    section_input,
    conv_one,
    conv_two,
    unit_gain,
    offset_bias,
    leak_slope,
    depthwise,
    embed_weight,
    class_centers,
    labels,
    class_offsets,
):
    sections = lax.axis_size("section")
    shards = lax.axis_size("shard")
    planes = sections // 2
    section_index = lax.axis_index("section")
    plane = section_index // 2
    core = section_index % 2
    swap = [(s, s ^ 1) for s in range(sections)]

    def stacked(own):
        peer = lax.ppermute(own, "section", swap)
        both = jnp.zeros((2, *own.shape), own.dtype)
        both = lax.dynamic_update_index_in_dim(both, own, core, 0)
        return lax.dynamic_update_index_in_dim(both, peer, 1 - core, 0)

    vec = stacked(jnp.concatenate([unit_gain, offset_bias, leak_slope], axis=0))
    w1 = stacked(conv_one[0])
    w2 = stacked(conv_two[0])
    micro = section_input.shape[0] // 2

    def widened(rows):
        grid = rows.reshape(-1, SIDE, SIDE, C)
        return jnp.pad(grid, ((0, 0), (0, 0), (0, WIDE - SIDE), (0, 0))).reshape(-1, ROWS, C)

    mine = lax.dynamic_slice_in_dim(section_input[:, 0], core * micro, micro, 0)
    x = widened(mine)
    pool_weight = widened(depthwise)[0].astype(jnp.float32)
    z = jnp.zeros((2, micro * ROWS, C), jnp.float32)
    flags = [(plane == s).astype(jnp.int32).reshape(1) for s in range(planes)]

    f1 = f2 = None
    for s in range(planes):
        x, z = forward_stage(flags[s], x, w1, w2, vec, z)
        if s == 0:
            f1, f2 = flip_all(w1, w2)
        if s < planes - 1:
            x = lax.ppermute(x, "section", [(2 * s + c, 2 * s + 2 + c) for c in range(2)])

    pooled = jnp.sum(x.astype(jnp.float32) * pool_weight[None], axis=1).astype(jnp.bfloat16)
    embedded = jnp.dot(pooled, embed_weight, preferred_element_type=jnp.float32)
    normed, squares, factor = unit_scale(embedded)
    sent = jnp.broadcast_to(normed.astype(jnp.bfloat16)[None], (shards, *normed.shape))
    unit_half = lax.all_to_all(sent, "shard", 0, 0, tiled=True).reshape(shards * micro, -1)
    centres_unit = unit_scale(class_centers.astype(jnp.float32))[0].astype(jnp.bfloat16)
    class_ids = class_offsets[0] + jnp.arange(class_centers.shape[0], dtype=jnp.int32)
    my_labels = lax.dynamic_slice_in_dim(labels, core * micro, micro, 0).T.reshape(-1)
    label_hits = my_labels[:, None] == class_ids[None, :]
    cosines = lax.dot_general(
        unit_half, centres_unit, (((1,), (1,)), ((), ())), preferred_element_type=jnp.float32
    )
    logits = scale_value * (cosines - margin_value * label_hits.astype(jnp.float32))
    exp_logits = jnp.exp(logits)
    weighted = jnp.dot(
        exp_logits.astype(jnp.bfloat16), centres_unit, preferred_element_type=jnp.float32
    )
    chosen = jnp.dot(
        label_hits.astype(jnp.bfloat16), centres_unit, preferred_element_type=jnp.float32
    )
    totals = jnp.sum(exp_logits, axis=1, keepdims=True)
    sums = jnp.concatenate([weighted, chosen, totals], axis=1).astype(jnp.bfloat16)
    sums = lax.all_to_all(sums.reshape(shards, micro, -1), "shard", 0, 0, tiled=True)
    sums = jnp.sum(sums.astype(jnp.float32), axis=0)
    width = embedded.shape[-1]
    grad_unit = scale_value * (
        sums[:, :width] / sums[:, 2 * width :] - sums[:, width : 2 * width]
    )
    inner = jnp.sum(embedded * grad_unit, axis=-1, keepdims=True)
    grad_embed = factor * (grad_unit - embedded * inner / (width * (squares + tiny_value)))
    grad_pooled = lax.dot_general(
        grad_embed.astype(jnp.bfloat16),
        embed_weight,
        (((1,), (1,)), ((), ())),
        preferred_element_type=jnp.float32,
    )
    g = (grad_pooled[:, None, :] * pool_weight[None]).astype(jnp.bfloat16)

    store = jnp.zeros((2, micro, ROWS, C), jnp.bfloat16)
    for s in reversed(range(planes)):
        g, store = backward_stage(flags[s], g, f1, f2, vec, z, store)
        if s > 0:
            g = lax.ppermute(g, "section", [(2 * s + c, 2 * s - 2 + c) for c in range(2)])

    def narrowed(rows):
        return rows.reshape(-1, SIDE, WIDE, C)[:, :, :SIDE].reshape(-1, SIDE * SIDE, C)

    kept = narrowed(lax.dynamic_index_in_dim(store, core, 0, keepdims=False))
    given = narrowed(lax.dynamic_index_in_dim(store, 1 - core, 0, keepdims=False))
    taken = lax.ppermute(given, "section", swap)
    first = jnp.where(core == 0, kept, taken)
    second = jnp.where(core == 0, taken, kept)
    return jnp.concatenate([first, second], axis=0)[None, :, None]


def solution(mesh):
    placed = (
        P(None, "shard", None, None),
        P("section", None, None),
        P("section", None, None),
        P("section", None),
        P("section", None),
        P("section", None),
        P(),
        P(),
        P("shard", None),
        P(),
        P("shard"),
    )
    return jax.shard_map(
        on_device,
        mesh=mesh,
        in_specs=placed,
        out_specs=P("section", None, "shard", None, None),
        check_vma=False,
    )
```

time: 322 us -> 196 us (0.61)
  waiting for transfers between devices: 137 us -> 83.1 us
  starting transfers between devices: 94.2 us -> 48.3 us
  Pallas kernels: 0 us -> 21.6 us
  loops' own time: 18.9 us -> 0 us
  local copies, waits for them, and re-layouts: 44.5 us -> 25.8 us
  matrix products: 19 us -> 8.21 us
    ppermute x22 -> x10, starting transfers between devices: 74.8 us -> 27.9 us  [the longest x3 13.2 us: stacked(): peer = lax.ppermute(own, 'section', swap)]
    ppermute x22 -> x10, waiting for transfers between devices: 90.9 us -> 59.6 us  [the longest x3 54.2 us: on_device(): lax.ppermute(g, 'section', [(2 * s + c, 2 * s - 2 + c) for c in range(2)])]
    all_to_all x2, waiting for transfers between devices: 46.5 us -> 23.5 us  [the longest x1 13.3 us: on_device(): lax.all_to_all(sums.reshape(shards, micro, -1), 'shard', 0, 0, tiled=True)]
    pallas_call x0 -> x9, Pallas kernels: none -> 21.6 us  [the longest x4 12.2 us: forward_stage(): pl.pallas_call(forward_body, in_specs=[SM, VM, VM, VM, VM, VM], out_specs...]
    another operation x24 -> x0, loops' own time: 18.9 us -> none  [the longest x1 7.85 us: on_device(): lax.scan(backward_tick, (empty_image, grad_start), jnp.arange(tick_count,...]
    dynamic_slice x22 -> x2, local copies, waits for them, and re-layouts: 14.3 us -> 0.24 us  [the longest x1 0.21 us: on_device(): mine = lax.dynamic_slice_in_dim(section_input[:, 0], core * micro, micro, 0)]
    dot_general x18 -> x2, matrix products: 14.3 us -> 1.12 us  [the longest x1 0.87 us: on_device(): lax.dot_general(grad_embed.astype(jnp.bfloat16), embed_weight, (((1,), (1...]
    unnamed x18 -> x47, local copies, waits for them, and re-layouts: 0.6 us -> 13.7 us
  transfers between devices with their start and end apart: 24 -> 12, of which waited for: 24 -> 5; matrix products, arithmetic and copies ran while one was open for 2% -> 6% of each run, Pallas kernels for 0% -> 2%
where the time goes in v1:
time: 196 us; the launch traced here: 195 us
  waiting for transfers between devices  83.1 us (42%)
  starting transfers between devices  48.3 us (25%)
  local copies, waits for them, and re-layouts  25.8 us (13%)
  Pallas kernels  21.6 us (11%)
  matrix products  8.21 us (4%)
  other arithmetic  7.05 us (4%)
    ppermute x3, waiting for transfers between devices, on_device(): lax.ppermute(g, 'section', [(2 * s + c, 2 * s - 2 + c) for c in range(2)])  54.2 us
    unnamed x47, local copies, waits for them, and re-layouts  13.7 us
    all_to_all x1, waiting for transfers between devices, on_device(): lax.all_to_all(sums.reshape(shards, micro, -1), 'shard', 0, 0, tiled=True)  13.3 us
    ppermute x3, starting transfers between devices, stacked(): peer = lax.ppermute(own, 'section', swap)  13.2 us
    all_to_all x1, starting transfers between devices, on_device(): lax.all_to_all(sent, 'shard', 0, 0, tiled=True).reshape(shards * micro, -1)  13.1 us
    pallas_call x4, Pallas kernels, forward_stage(): pl.pallas_call(forward_body, in_specs=[SM, VM, VM, VM, VM, VM], out_specs...  12.2 us
    all_to_all x1, waiting for transfers between devices, on_device(): lax.all_to_all(sent, 'shard', 0, 0, tiled=True).reshape(shards * micro, -1)  10.2 us
    ppermute x1, starting transfers between devices, on_device(): taken = lax.ppermute(given, 'section', swap)  9.33 us
  transfers between devices with their start and end apart: 12, of which 5 were waited for; matrix products, arithmetic and copies ran while one was open for 6% of the time, Pallas kernels for 2%

profile of v1, /device:TPU:1, one launch (start us, length us, event | category | flops | bytes accessed | tf_op | source)
XLA Modules:
  0.0 195.3 jit_solution(1020468932622310815)
XLA Ops:
  0.0 8.9 %collective-permute-start.1 = (bf16[2304,256]{1,0:T(8,128)(2,1)}, bf16[2304,256]{1,0:T(8,128)(2,1)}, u32[]{:S(2)}, u32[]{:S(2)}) collective-permute-start(bf16[2304,256]{1,0:T(8,128)(2,1)} %bitcast.39), channel_id=1, source_target_pairs={{0,64},{64,0},{128,192},{192,128},{256,320},{320,256},{384,448},{4... | collective-permute-start | bytes 3538952 | tf_op jit(solution)/shard_map/ppermute | solution.py:216
  8.9 1.9 collective-permute-start
  10.8 0.7 pad_maximum_fusion.1
  11.5 2.4 %collective-permute-start.2 = (f32[3,256]{1,0:T(4,128)S(1)}, f32[3,256]{1,0:T(4,128)S(1)}, u32[]{:S(2)}, u32[]{:S(2)}) collective-permute-start(f32[3,256]{1,0:T(4,128)S(1)} %pad_maximum_fusion.1), channel_id=1, source_target_pairs={{0,64},{64,0},{128,192},{192,128},{256,320},{320,256},{384,448},{4... | collective-permute-start | bytes 9224 | tf_op jit(solution)/shard_map/ppermute | solution.py:216
  14.0 0.2 broadcast.75.clone.1
  14.1 1.1 copy-done.13
  15.2 0.1 constant_dynamic-update-slice_fusion
  15.4 1.6 broadcast.75.clone
  17.0 1.1 constant_dynamic-update-slice_fusion.1
  18.1 0.2 constant_dynamic-slice_fusion.3
  18.5 1.4 bitcast_dynamic-update-slice_fusion.w2_ref
  19.9 2.4 %bitcast_dynamic-update-slice_fusion.1.w1_ref = bf16[2,2304,256]{2,1,0:T(8,128)(2,1)} fusion(bf16[2,2304,256]{2,1,0:T(8,128)(2,1)} %constant_dynamic-update-slice_fusion.1, s32[]{:T(128)S(6)} %select_n.47, bf16[2304,256]{1,0:T(8,128)(2,1)} %collective-permute-done), kind=kLoop, calls=%fused_computation.8 | loop fusion | bytes 2359300 | tf_op jit(solution)/shard_map/jit(dynamic_update_index_in_dim)/dynamic_update_slice | solution.py:219
  22.3 7.2 %forward_stage.4 = (bf16[2,224,256]{2,1,0:T(8,128)(2,1)S(1)}, f32[2,448,256]{2,1,0:T(8,128)S(1)}) custom-call(s32[1]{0:T(128)} %bitcast.flag, bf16[2,224,256]{2,1,0:T(8,128)(2,1)S(1)} %bitcast.38, bf16[2,2304,256]{2,1,0:T(8,128)(2,1)} %bitcast_dynamic-update-slice_fusion.1.w1_ref, ...), custom_call_target="tpu_custom_call", output_to_operand_aliasing={{1}: (5, {})} | custom-call | flops 2113929216 | bytes 6000000 | tf_op jit(solution)/shard_map/forward_stage/pallas_call | solution.py:121
  29.5 0.9 copy-done.1
  30.4 1.3 collective-permute-start.3
  32.4 4.5 %collective-permute-done.3.x_ref = bf16[2,224,256]{2,1,0:T(8,128)(2,1)S(1)} collective-permute-done((bf16[2,224,256]{2,1,0:T(8,128)(2,1)S(1)}, bf16[2,224,256]{2,1,0:T(8,128)(2,1)S(1)}, u32[]{:S(2)}, u32[]{:S(2)}) %collective-permute-start.3) | collective-permute-done | bytes 229408 | tf_op jit(solution)/shard_map/ppermute | solution.py:242
  36.9 1.2 copy-done.2
  38.1 1.7 forward_stage.5
  39.8 0.9 copy-done.3
  40.7 0.7 collective-permute-start.4
  41.5 1.9 fusion
  43.3 1.2 copy-done.4
  44.5 1.7 forward_stage.6
  46.2 0.7 collective-permute-start.5
  46.9 1.7 forward_stage.7
  48.6 0.9 copy-done.5
  49.7 0.3 multiply_reduce_fusion.2
  49.9 0.6 broadcast_multiply_fusion
  50.6 0.7 broadcast_in_dim.48
  51.3 13.1 %all-to-all-start = ((bf16[64,2,512]{2,1,0:T(2,128)(2,1)}), bf16[64,2,512]{2,1,0:T(2,128)(2,1)S(1)}, u32[]{:S(2)}, u32[]{:S(2)}) async-start(bf16[64,2,512]{2,1,0:T(2,128)(2,1)} %broadcast_in_dim.48), calls=%async_computation | async-start | bytes 262144 | tf_op jit(solution)/shard_map/all_to_all | solution.py:248
  64.5 0.1 copy.29
  64.6 0.1 eq.38
  64.7 2.7 %convolution_convert_fusion = bf16[128,512]{1,0:T(8,128)(2,1)} fusion(s32[1664]{0:T(1024)S(1)} %iota_add_fusion, s32[128]{0:T(128)S(1)} %eq.38, bf16[1664,512]{1,0:T(8,128)(2,1)} %param.19, f32[1664]{0:T(1024)S(1)} %rsqrt_multiply_fusion), kind=kOutput, calls=%fused_computation.9 | convolution fusion | flops 220938240 | bytes 1848832 | tf_op jit(solution)/shard_map/dot_general | solution.py:261
  67.4 1.0 concatenate.19
  68.4 10.2 %all-to-all-done = bf16[64,2,512]{2,1,0:T(2,128)(2,1)S(1)} async-done(((bf16[64,2,512]{2,1,0:T(2,128)(2,1)}), bf16[64,2,512]{2,1,0:T(2,128)(2,1)S(1)}, u32[]{:S(2)}, u32[]{:S(2)}) %all-to-all-start) | async-done | bytes 131104 | tf_op jit(solution)/shard_map/all_to_all | solution.py:248
  78.6 0.7 reshape.106
  79.3 3.2 %fusion.20 = (bf16[128]{0:T(256)(128)(2,1)}, bf16[128,1664]{1,0:T(8,128)(2,1)S(1)}) fusion(s32[1664]{0:T(1024)S(1)} %iota_add_fusion, s32[128]{0:T(128)S(1)} %eq.38, bf16[128,512]{1,0:T(8,128)(2,1)} %reshape.106, bf16[1664,512]{1,0:T(8,128)(2,1)} %param.19, f32[1664]{0:T(1024)S(1)} %rsqrt_multiply_fusion), kind=kOutput, calls=%fused_computation.53 | convolution fusion | flops 221937536 | bytes 2275072 | tf_op jit(solution)/shard_map/dot_general | solution.py:253
  82.5 1.2 convolution_convert_fusion.1
  83.7 1.0 concatenate.18
  84.7 0.9 concatenate.23
  85.5 1.0 pad_maximum_fusion
  86.5 7.2 %all-to-all-start.1 = ((bf16[64,2,1025]{2,1,0:T(2,128)(2,1)}), bf16[64,2,1025]{2,1,0:T(2,128)(2,1)S(1)}, u32[]{:S(2)}, u32[]{:S(2)}) async-start(bf16[64,2,1025]{2,1,0:T(2,128)(2,1)} %pad_maximum_fusion), calls=%async_computation.1 | async-start | bytes 589824 | tf_op jit(solution)/shard_map/all_to_all | solution.py:266
  93.8 3.7 %flip_all.1 = (bf16[2,2304,256]{2,1,0:T(8,128)(2,1)S(1)}, bf16[2,2304,256]{2,1,0:T(8,128)(2,1)S(1)}) custom-call(bf16[2,2304,256]{2,1,0:T(8,128)(2,1)} %bitcast_dynamic-update-slice_fusion.1.w1_ref, bf16[2,2304,256]{2,1,0:T(8,128)(2,1)S(1)} %bitcast_dynamic-update-slice_fusion.w2_ref), custom_call_target="tpu_custom_call" | custom-call | flops 1207959552 | bytes 9000000 | tf_op jit(solution)/shard_map/flip_all/pallas_call | solution.py:177
  97.5 1.4 copy-done.8
  98.9 1.4 copy-done.10
  100.4 13.3 %all-to-all-done.1 = bf16[64,2,1025]{2,1,0:T(2,128)(2,1)S(1)} async-done(((bf16[64,2,1025]{2,1,0:T(2,128)(2,1)}), bf16[64,2,1025]{2,1,0:T(2,128)(2,1)S(1)}, u32[]{:S(2)}, u32[]{:S(2)}) %all-to-all-start.1) | async-done | bytes 262432 | tf_op jit(solution)/shard_map/all_to_all | solution.py:266
  113.7 0.3 convert_reduce_fusion
  114.0 0.1 slice_reduce_fusion
  114.1 0.9 multiply_reduce_fusion.1
  114.9 0.9 fusion.9
  115.9 1.2 copy-done.6
  117.1 1.7 copy-done.9
  118.8 1.7 copy-done.11
  120.4 0.7 collective-permute-start.6
  121.1 0.7 collective-permute-start.7
  121.8 1.4 collective-permute-start.8
  123.3 54.2 %collective-permute-done.8.g_ref = bf16[2,224,256]{2,1,0:T(8,128)(2,1)S(1)} collective-permute-done((bf16[2,224,256]{2,1,0:T(8,128)(2,1)S(1)}, bf16[2,224,256]{2,1,0:T(8,128)(2,1)S(1)}, u32[]{:S(2)}, u32[]{:S(2)}) %collective-permute-start.8) | collective-permute-done | bytes 229408 | tf_op jit(solution)/shard_map/ppermute | solution.py:286
  177.5 5.7 %backward_stage.7 = (bf16[2,224,256]{2,1,0:T(8,128)(2,1)}, bf16[2,2,224,256]{3,2,1,0:T(8,128)(2,1)S(1)}) custom-call(s32[1]{0:T(128)} %bitcast.flag, bf16[2,224,256]{2,1,0:T(8,128)(2,1)S(1)} %collective-permute-done.8.g_ref, bf16[2,2304,256]{2,1,0:T(8,128)(2,1)S(1)} %copy-done.9, ...), custom_call_target="tpu_custom_call", output_to_operand_aliasing={{1}: (6, {})} | custom-call | flops 2113929216 | bytes 6000000 | tf_op jit(solution)/shard_map/backward_stage/pallas_call | solution.py:139
  183.2 0.2 copy.32
  183.4 9.3 %collective-permute-start.9 = (bf16[2,196,256]{2,0,1:T(2,128)(2,1)S(1)}, bf16[2,196,256]{2,0,1:T(2,128)(2,1)S(1)}, u32[]{:S(2)}, u32[]{:S(2)}) collective-permute-start(bf16[2,196,256]{2,0,1:T(2,128)(2,1)S(1)} %bitcast.44), channel_id=1, source_target_pairs={{0,64},{64,0},{128,192},{192,128},{256,320},{320,256},{384,448},{4... | collective-permute-start | bytes 602120 | tf_op jit(solution)/shard_map/ppermute | solution.py:293
  192.7 0.2 copy.31
  192.9 0.8 collective-permute-done.9
  193.8 0.3 broadcast_select_fusion.1
  194.1 1.2 maximum_bitcast_fusion
  (62 shorter events, 0.6 us)
Async XLA Ops:
  0.0 18.1 %copy-start = (bf16[4,1,196,256]{3,0,2,1:T(4,128)(2,1)S(1)}, bf16[4,1,196,256]{3,0,2,1:T(4,128)(2,1)}, u32[]{:S(2)}) copy-start(bf16[4,1,196,256]{3,0,2,1:T(4,128)(2,1)} %param.11) | copy-start | bytes 1204228
  0.0 18.5 %collective-permute-start.1 = (bf16[2304,256]{1,0:T(8,128)(2,1)}, bf16[2304,256]{1,0:T(8,128)(2,1)}, u32[]{:S(2)}, u32[]{:S(2)}) collective-permute-start(bf16[2304,256]{1,0:T(8,128)(2,1)} %bitcast.39), channel_id=1, source_target_pairs={{0,64},{64,0},{128,192},{192,128},{256,320},{320,256},{384,448},{4... | collective-permute-start | bytes 3538952 | tf_op jit(solution)/shard_map/ppermute | solution.py:216
  8.9 11.0 %collective-permute-start = (bf16[2304,256]{1,0:T(8,128)(2,1)}, bf16[2304,256]{1,0:T(8,128)(2,1)}, u32[]{:S(2)}, u32[]{:S(2)}) collective-permute-start(bf16[2304,256]{1,0:T(8,128)(2,1)} %bitcast.40), channel_id=1, source_target_pairs={{0,64},{64,0},{128,192},{192,128},{256,320},{320,256},{384,448},{4... | collective-permute-start | bytes 3538952 | tf_op jit(solution)/shard_map/ppermute | solution.py:216
  11.5 6.9 %collective-permute-start.2 = (f32[3,256]{1,0:T(4,128)S(1)}, f32[3,256]{1,0:T(4,128)S(1)}, u32[]{:S(2)}, u32[]{:S(2)}) collective-permute-start(f32[3,256]{1,0:T(4,128)S(1)} %pad_maximum_fusion.1), channel_id=1, source_target_pairs={{0,64},{64,0},{128,192},{192,128},{256,320},{320,256},{384,448},{4... | collective-permute-start | bytes 9224 | tf_op jit(solution)/shard_map/ppermute | solution.py:216
  14.0 1.3 copy-start.13
  15.2 1.7 copy-start.14
  15.3 3.0 %copy-start.18 = (f32[1,256]{1,0:T(1,128)S(1)}, f32[1,256]{1,0:T(1,128)}, u32[]{:S(2)}) copy-start(f32[1,256]{1,0:T(1,128)} %param.16) | copy-start | bytes 3076
  15.4 3.0 %copy-start.19 = (f32[1,256]{1,0:T(1,128)S(1)}, f32[1,256]{1,0:T(1,128)}, u32[]{:S(2)}) copy-start(f32[1,256]{1,0:T(1,128)} %param.15) | copy-start | bytes 3076
  15.4 2.9 %copy-start.20 = (f32[1,256]{1,0:T(1,128)S(1)}, f32[1,256]{1,0:T(1,128)}, u32[]{:S(2)}) copy-start(f32[1,256]{1,0:T(1,128)} %param.14) | copy-start | bytes 3076
  29.5 0.9 copy-start.1
  30.4 6.5 %collective-permute-start.3 = (bf16[2,224,256]{2,1,0:T(8,128)(2,1)S(1)}, bf16[2,224,256]{2,1,0:T(8,128)(2,1)S(1)}, u32[]{:S(2)}, u32[]{:S(2)}) collective-permute-start(bf16[2,224,256]{2,1,0:T(8,128)(2,1)S(1)} %get-tuple-element.22), channel_id=1, source_target_pairs={{0,128},{64,192},{1,129},{65,193},{2,130},{66,194},{3,131},{67,195... | collective-permute-start | bytes 688136 | tf_op jit(solution)/shard_map/ppermute | solution.py:242
  36.9 1.2 copy-start.2
  38.1 3.3 %copy-start.16 = (bf16[196,256]{1,0:T(8,128)(2,1)S(1)}, bf16[196,256]{1,0:T(8,128)(2,1)}, u32[]{:S(2)}) copy-start(bf16[196,256]{1,0:T(8,128)(2,1)} %param.17) | copy-start | bytes 301060
  39.8 0.9 copy-start.3
  40.7 2.6 %collective-permute-start.4 = (bf16[2,224,256]{2,1,0:T(8,128)(2,1)S(1)}, bf16[2,224,256]{2,1,0:T(8,128)(2,1)S(1)}, u32[]{:S(2)}, u32[]{:S(2)}) collective-permute-start(bf16[2,224,256]{2,1,0:T(8,128)(2,1)S(1)} %get-tuple-element.24), channel_id=1, source_target_pairs={{128,256},{192,320},{129,257},{193,321},{130,258},{194,322},{131,2... | collective-permute-start | bytes 688136 | tf_op jit(solution)/shard_map/ppermute | solution.py:242
  43.3 1.2 copy-start.4
  46.2 0.7 collective-permute-start.5
  46.9 2.8 %copy-start.15 = (bf16[256,512]{1,0:T(8,128)(2,1)S(1)}, bf16[256,512]{1,0:T(8,128)(2,1)}, u32[]{:S(2)}) copy-start(bf16[256,512]{1,0:T(8,128)(2,1)} %param.18) | copy-start | bytes 786436
  46.9 17.5 %copy-start.21 = (s32[4,64]{1,0:T(4,128)S(1)}, s32[4,64]{1,0:T(4,128)}, u32[]{:S(2)}) copy-start(s32[4,64]{1,0:T(4,128)} %param.20) | copy-start | bytes 3076
  48.6 0.9 copy-start.5
  49.9 0.6 copy-start.17
  50.5 13.9 %copy-start.22 = (f32[2]{0:T(128)}, f32[2]{0:T(128)S(1)}, u32[]{:S(2)}) copy-start(f32[2]{0:T(128)S(1)} %get-tuple-element.46) | copy-start | bytes 28
  51.3 27.3 %all-to-all-start = ((bf16[64,2,512]{2,1,0:T(2,128)(2,1)}), bf16[64,2,512]{2,1,0:T(2,128)(2,1)S(1)}, u32[]{:S(2)}, u32[]{:S(2)}) async-start(bf16[64,2,512]{2,1,0:T(2,128)(2,1)} %broadcast_in_dim.48), calls=%async_computation | async-start | bytes 262144 | tf_op jit(solution)/shard_map/all_to_all | solution.py:248
  79.3 3.2 %copy-start.12 = (bf16[1664,512]{1,0:T(8,128)(2,1)S(1)}, bf16[1664,512]{1,0:T(8,128)(2,1)}, u32[]{:S(2)}) copy-start(bf16[1664,512]{1,0:T(8,128)(2,1)} %param.19) | copy-start | bytes 5111812
  86.5 27.1 %all-to-all-start.1 = ((bf16[64,2,1025]{2,1,0:T(2,128)(2,1)}), bf16[64,2,1025]{2,1,0:T(2,128)(2,1)S(1)}, u32[]{:S(2)}, u32[]{:S(2)}) async-start(bf16[64,2,1025]{2,1,0:T(2,128)(2,1)} %pad_maximum_fusion), calls=%async_computation.1 | async-start | bytes 589824 | tf_op jit(solution)/shard_map/all_to_all | solution.py:266
  97.5 1.4 copy-start.8
  98.9 1.5 copy-start.10
  115.9 1.2 copy-start.6
  117.1 1.7 copy-start.9
  118.7 1.7 copy-start.11
  120.4 0.7 collective-permute-start.6
  121.1 0.7 collective-permute-start.7
  121.8 55.7 %copy-start.7 = (f32[2,448,256]{2,1,0:T(8,128)S(1)}, f32[2,448,256]{2,1,0:T(8,128)}, u32[]{:S(2)}) copy-start(f32[2,448,256]{2,1,0:T(8,128)} %copy-done.5) | copy-start | bytes 2752516
  121.8 55.6 %collective-permute-start.8 = (bf16[2,224,256]{2,1,0:T(8,128)(2,1)S(1)}, bf16[2,224,256]{2,1,0:T(8,128)(2,1)S(1)}, u32[]{:S(2)}, u32[]{:S(2)}) collective-permute-start(bf16[2,224,256]{2,1,0:T(8,128)(2,1)S(1)} %get-tuple-element.36), channel_id=1, source_target_pairs={{128,0},{192,64},{129,1},{193,65},{130,2},{194,66},{131,3},{195,67... | collective-permute-start | bytes 688136 | tf_op jit(solution)/shard_map/ppermute | solution.py:286
  183.4 10.4 %collective-permute-start.9 = (bf16[2,196,256]{2,0,1:T(2,128)(2,1)S(1)}, bf16[2,196,256]{2,0,1:T(2,128)(2,1)S(1)}, u32[]{:S(2)}, u32[]{:S(2)}) collective-permute-start(bf16[2,196,256]{2,0,1:T(2,128)(2,1)S(1)} %bitcast.44), channel_id=1, source_target_pairs={{0,64},{64,0},{128,192},{192,128},{256,320},{320,256},{384,448},{4... | collective-permute-start | bytes 602120 | tf_op jit(solution)/shard_map/ppermute | solution.py:293

commit v2 on v1

v2 whole, which is shorter than its diff:
```python
import functools
import math

import jax
import jax.numpy as jnp
from jax import lax
from jax.experimental import pallas as pl
from jax.experimental.pallas import tpu as pltpu
from jax.sharding import PartitionSpec as P

SIDE = 14
WIDE = 16
ROWS = SIDE * WIDE
C = 256

margin_value = 0.4
scale_value = 64.0
tiny_value = 1e-06

VM = pl.BlockSpec(memory_space=pltpu.VMEM)
HB = pl.BlockSpec(memory_space=pltpu.HBM)
SM = pl.BlockSpec(memory_space=pltpu.SMEM)
LIMIT = 20 * 1024 * 1024


def keep_columns(rows):
    return (lax.broadcasted_iota(jnp.int32, (rows, C), 0) % WIDE) < SIDE


def build(value, cols):
    parts = (pltpu.roll(value, 1, 0), value, pltpu.roll(value, ROWS - 1, 0))
    for place, part in enumerate(parts):
        cols[WIDE : WIDE + ROWS, place * C : (place + 1) * C] = part.astype(jnp.bfloat16)


def conv(cols, weights):
    acc = None
    for step in range(3):
        part = jnp.dot(
            cols[WIDE * step : WIDE * step + ROWS, :],
            weights[step * 3 * C : (step + 1) * 3 * C, :],
            preferred_element_type=jnp.float32,
        )
        acc = part if acc is None else acc + part
    return acc


def clear_border(cols):
    for i in range(cols.shape[0]):
        cols[i, 0:WIDE, :] = jnp.zeros((WIDE, 3 * C), jnp.bfloat16)
        cols[i, WIDE + ROWS :, :] = jnp.zeros((WIDE, 3 * C), jnp.bfloat16)


def start_weights(core, sources, held, sems, order):
    def start(own_unit):
        for u, k in order:
            source = sources[0][k] if u == own_unit else sources[1][k]
            pltpu.make_async_copy(source, held.at[u, k], sems.at[u, k]).start()

    @pl.when(core == 0)
    def _():
        start(0)

    @pl.when(core == 1)
    def _():
        start(1)


def forward_body(
    flag, x_ref, own1, own2, peer1, peer2, vec_ref, out_ref, z_ref, cols, run, zed, held, sems, zsem
):
    @pl.when(flag[0] == 1)
    def _():
        sources = ((own1, own2), (peer1, peer2))
        start_weights(flag[1], sources, held, sems, ((0, 0), (0, 1), (1, 0), (1, 1)))
        clear_border(cols)
        keep = keep_columns(ROWS)
        for i in range(2):
            run[i] = x_ref[i].astype(jnp.float32)

        def one(u, carry):
            vec = vec_ref[u]
            for i in range(2):
                build(run[i], cols.at[2 * i])
            pltpu.make_async_copy(own1, held.at[u, 0], sems.at[u, 0]).wait()
            for i in range(2):
                pre = conv(cols.at[2 * i], held.at[u, 0]) * vec[0:1] + vec[1:2]
                zed[u, i * ROWS : (i + 1) * ROWS] = pre
                leak = vec[2:3]
                four = 4.0 * pre
                soft = jnp.maximum(four, 0.0) + jnp.log1p(jnp.exp(-jnp.abs(four)))
                active = leak * pre + (1.0 - leak) * soft * 0.25
                build(jnp.where(keep, active, 0.0), cols.at[2 * i + 1])
            pltpu.make_async_copy(own2, held.at[u, 1], sems.at[u, 1]).wait()
            for i in range(2):
                result = run[i] + conv(cols.at[2 * i + 1], held.at[u, 1])
                result = jnp.where(keep, result, 0.0).astype(jnp.bfloat16)
                run[i] = result.astype(jnp.float32)
            pltpu.make_async_copy(zed.at[u], z_ref.at[u], zsem.at[u]).start()
            return carry

        lax.fori_loop(0, 2, one, 0)
        for i in range(2):
            out_ref[i] = run[i].astype(jnp.bfloat16)
        for u in range(2):
            pltpu.make_async_copy(zed.at[u], z_ref.at[u], zsem.at[u]).wait()


def backward_body(
    flag, g_ref, own1, own2, peer1, peer2, vec_ref, z_ref, store_in,
    out_ref, store, cols, run, zed, held, sems, zsem,
):
    @pl.when(flag[0] == 1)
    def _():
        sources = ((own1, own2), (peer1, peer2))
        start_weights(flag[1], sources, held, sems, ((1, 1), (1, 0), (0, 1), (0, 0)))
        for u in (1, 0):
            pltpu.make_async_copy(z_ref.at[u], zed.at[u], zsem.at[u]).start()
        clear_border(cols)
        keep = keep_columns(ROWS)
        for i in range(2):
            run[i] = g_ref[i].astype(jnp.float32)

        def one(step, carry):
            u = 1 - step
            vec = vec_ref[u]
            for i in range(2):
                build(run[i], cols.at[2 * i])
            pltpu.make_async_copy(own2, held.at[u, 1], sems.at[u, 1]).wait()
            pltpu.make_async_copy(z_ref.at[u], zed.at[u], zsem.at[u]).wait()
            for i in range(2):
                pre = zed[u, i * ROWS : (i + 1) * ROWS]
                leak = vec[2:3]
                slope = leak + (1.0 - leak) / (1.0 + jnp.exp(-4.0 * pre))
                hidden = conv(cols.at[2 * i], held.at[u, 1]) * slope * vec[0:1]
                build(jnp.where(keep, hidden, 0.0), cols.at[2 * i + 1])
            pltpu.make_async_copy(own1, held.at[u, 0], sems.at[u, 0]).wait()
            for i in range(2):
                result = run[i] + conv(cols.at[2 * i + 1], held.at[u, 0])
                result = jnp.where(keep, result, 0.0).astype(jnp.bfloat16)
                run[i] = result.astype(jnp.float32)
                store[u, i] = result
            return carry

        lax.fori_loop(0, 2, one, 0)
        for i in range(2):
            out_ref[i] = run[i].astype(jnp.bfloat16)


def in_hbm(*arrays):
    return [pltpu.with_memory_space_constraint(a, pltpu.HBM) for a in arrays]


CONV_COST = pl.CostEstimate(flops=4 * 2 * 448 * 2304 * 256, bytes_accessed=6_000_000, transcendentals=500_000)


def stage_scratch(images):
    return [
        pltpu.VMEM((2 * images, ROWS + 2 * WIDE, 3 * C), jnp.bfloat16),
        pltpu.VMEM((images, ROWS, C), jnp.float32),
        pltpu.VMEM((2, images * ROWS, C), jnp.float32),
        pltpu.VMEM((2, 2, 9 * C, C), jnp.bfloat16),
        pltpu.SemaphoreType.DMA((2, 2)),
        pltpu.SemaphoreType.DMA((2,)),
    ]


def forward_stage(flag, x, weights, vec):
    images = x.shape[0]
    return pl.pallas_call(
        forward_body,
        in_specs=[SM, VM, HB, HB, HB, HB, VM],
        out_specs=[VM, HB],
        out_shape=[
            jax.ShapeDtypeStruct(x.shape, jnp.bfloat16),
            pltpu.HBM((2, images * ROWS, C), jnp.float32),
        ],
        scratch_shapes=stage_scratch(images),
        compiler_params=pltpu.CompilerParams(vmem_limit_bytes=LIMIT),
        cost_estimate=CONV_COST,
        name="forward_stage",
    )(flag, x, *in_hbm(*weights), vec)


def backward_stage(flag, g, weights, vec, z, store):
    images = g.shape[0]
    return pl.pallas_call(
        backward_body,
        in_specs=[SM, VM, HB, HB, HB, HB, VM, HB, VM],
        out_specs=[VM, VM],
        out_shape=[
            jax.ShapeDtypeStruct(g.shape, jnp.bfloat16),
            jax.ShapeDtypeStruct(store.shape, store.dtype),
        ],
        scratch_shapes=stage_scratch(images),
        input_output_aliases={8: 1},
        compiler_params=pltpu.CompilerParams(vmem_limit_bytes=LIMIT),
        cost_estimate=CONV_COST,
        name="backward_stage",
    )(flag, g, *in_hbm(*weights), vec, *in_hbm(z), store)


def flip_body(*refs):
    eye = (
        lax.broadcasted_iota(jnp.int32, (C, C), 0) == lax.broadcasted_iota(jnp.int32, (C, C), 1)
    ).astype(jnp.float32).astype(jnp.bfloat16)
    half = len(refs) // 2
    for source, target in zip(refs[:half], refs[half:]):
        turned = lax.dot_general(
            eye, source[...], (((1,), (1,)), ((), ())), preferred_element_type=jnp.float32
        )
        target[...] = turned.astype(jnp.bfloat16)


def flip_all(weights):
    count = len(weights)
    return pl.pallas_call(
        flip_body,
        grid=(9,),
        in_specs=[pl.BlockSpec((C, C), lambda t: (t, 0))] * count,
        out_specs=[pl.BlockSpec((C, C), lambda t: (8 - t, 0))] * count,
        out_shape=[pltpu.HBM(w.shape, w.dtype) for w in weights],
        compiler_params=pltpu.CompilerParams(vmem_limit_bytes=LIMIT),
        cost_estimate=pl.CostEstimate(flops=36 * 2 * 256**3, bytes_accessed=9_000_000, transcendentals=0),
        name="flip_all",
    )(*in_hbm(*weights))


def unit_scale(values):
    squares = jnp.mean(values * values, axis=-1, keepdims=True)
    factor = lax.rsqrt(squares + tiny_value) / math.sqrt(values.shape[-1])
    return (values * factor, squares, factor)


def on_device(
    section_input,
    conv_one,
    conv_two,
    unit_gain,
    offset_bias,
    leak_slope,
    depthwise,
    embed_weight,
    class_centers,
    labels,
    class_offsets,
):
    sections = lax.axis_size("section")
    shards = lax.axis_size("shard")
    planes = sections // 2
    section_index = lax.axis_index("section")
    plane = section_index // 2
    core = section_index % 2
    swap = [(s, s ^ 1) for s in range(sections)]

    def stacked(own):
        peer = lax.ppermute(own, "section", swap)
        both = jnp.zeros((2, *own.shape), own.dtype)
        both = lax.dynamic_update_index_in_dim(both, own, core, 0)
        return lax.dynamic_update_index_in_dim(both, peer, 1 - core, 0)

    own = (conv_one[0], conv_two[0])
    peer = tuple(lax.ppermute(w, "section", swap) for w in own)
    weights = (*own, *peer)
    vec = stacked(jnp.concatenate([unit_gain, offset_bias, leak_slope], axis=0))
    micro = section_input.shape[0] // 2

    def widened(rows):
        grid = rows.reshape(-1, SIDE, SIDE, C)
        return jnp.pad(grid, ((0, 0), (0, 0), (0, WIDE - SIDE), (0, 0))).reshape(-1, ROWS, C)

    mine = lax.dynamic_slice_in_dim(section_input[:, 0], core * micro, micro, 0)
    x = widened(mine)
    pool_weight = widened(depthwise)[0].astype(jnp.float32)
    flags = [jnp.stack([(plane == s).astype(jnp.int32), core]) for s in range(planes)]
    flips = flip_all(weights)
    saved = []
    for s in range(planes):
        x, z = forward_stage(flags[s], x, weights, vec)
        saved.append(z)
        if s < planes - 1:
            x = lax.ppermute(x, "section", [(2 * s + c, 2 * s + 2 + c) for c in range(2)])

    pooled = jnp.sum(x.astype(jnp.float32) * pool_weight[None], axis=1).astype(jnp.bfloat16)
    embedded = jnp.dot(pooled, embed_weight, preferred_element_type=jnp.float32)
    normed, squares, factor = unit_scale(embedded)
    sent = jnp.broadcast_to(normed.astype(jnp.bfloat16)[None], (shards, *normed.shape))
    unit_half = lax.all_to_all(sent, "shard", 0, 0, tiled=True).reshape(shards * micro, -1)
    centres_unit = unit_scale(class_centers.astype(jnp.float32))[0].astype(jnp.bfloat16)
    class_ids = class_offsets[0] + jnp.arange(class_centers.shape[0], dtype=jnp.int32)
    my_labels = lax.dynamic_slice_in_dim(labels, core * micro, micro, 0).T.reshape(-1)
    label_hits = my_labels[:, None] == class_ids[None, :]
    cosines = lax.dot_general(
        unit_half, centres_unit, (((1,), (1,)), ((), ())), preferred_element_type=jnp.float32
    )
    logits = scale_value * (cosines - margin_value * label_hits.astype(jnp.float32))
    exp_logits = jnp.exp(logits)
    weighted = jnp.dot(
        exp_logits.astype(jnp.bfloat16), centres_unit, preferred_element_type=jnp.float32
    )
    chosen = jnp.dot(
        label_hits.astype(jnp.bfloat16), centres_unit, preferred_element_type=jnp.float32
    )
    totals = jnp.sum(exp_logits, axis=1, keepdims=True)
    sums = jnp.concatenate([weighted, chosen, totals], axis=1).astype(jnp.bfloat16)
    sums = lax.all_to_all(sums.reshape(shards, micro, -1), "shard", 0, 0, tiled=True)
    sums = jnp.sum(sums.astype(jnp.float32), axis=0)
    width = embedded.shape[-1]
    grad_unit = scale_value * (
        sums[:, :width] / sums[:, 2 * width :] - sums[:, width : 2 * width]
    )
    inner = jnp.sum(embedded * grad_unit, axis=-1, keepdims=True)
    grad_embed = factor * (grad_unit - embedded * inner / (width * (squares + tiny_value)))
    grad_pooled = lax.dot_general(
        grad_embed.astype(jnp.bfloat16),
        embed_weight,
        (((1,), (1,)), ((), ())),
        preferred_element_type=jnp.float32,
    )
    g = (grad_pooled[:, None, :] * pool_weight[None]).astype(jnp.bfloat16)

    store = jnp.zeros((2, micro, ROWS, C), jnp.bfloat16)
    for s in reversed(range(planes)):
        g, store = backward_stage(flags[s], g, flips, vec, saved[s], store)
        if s > 0:
            g = lax.ppermute(g, "section", [(2 * s + c, 2 * s - 2 + c) for c in range(2)])

    def narrowed(rows):
        return rows.reshape(-1, SIDE, WIDE, C)[:, :, :SIDE].reshape(-1, SIDE * SIDE, C)

    kept = narrowed(lax.dynamic_index_in_dim(store, core, 0, keepdims=False))
    given = narrowed(lax.dynamic_index_in_dim(store, 1 - core, 0, keepdims=False))
    taken = lax.ppermute(given, "section", swap)
    first = jnp.where(core == 0, kept, taken)
    second = jnp.where(core == 0, taken, kept)
    return jnp.concatenate([first, second], axis=0)[None, :, None]


def solution(mesh):
    placed = (
        P(None, "shard", None, None),
        P("section", None, None),
        P("section", None, None),
        P("section", None),
        P("section", None),
        P("section", None),
        P(),
        P(),
        P("shard", None),
        P(),
        P("shard"),
    )
    return jax.shard_map(
        on_device,
        mesh=mesh,
        in_specs=placed,
        out_specs=P("section", None, "shard", None, None),
        check_vma=False,
    )
```

time: 196 us -> 172 us (0.88)
  local copies, waits for them, and re-layouts: 25.8 us -> 3.97 us
  matrix products: 8.21 us -> 2.58 us
  Pallas kernels: 21.6 us -> 24.3 us
    unnamed x47 -> x15, local copies, waits for them, and re-layouts: 13.7 us -> 1.68 us
    ppermute x3 -> x1, starting transfers between devices: 13.2 us -> 2.39 us  [stacked(): peer = lax.ppermute(own, 'section', swap)]
    ppermute x0 -> x2, starting transfers between devices: none -> 10.8 us  [on_device(): peer = tuple((lax.ppermute(w, 'section', swap) for w in own))]
    dynamic_update_slice x3 -> x1, local copies, waits for them, and re-layouts: 3.76 us -> 0.01 us  [stacked(): return lax.dynamic_update_index_in_dim(both, peer, 1 - core, 0)]
    all_to_all x1, waiting for transfers between devices: 10.2 us -> 13.4 us  [on_device(): lax.all_to_all(sent, 'shard', 0, 0, tiled=True).reshape(shards * micro, -1)]
    pallas_call x9, Pallas kernels: 21.6 us -> 24.3 us  [the longest x1 8.51 us: flip_all(): pl.pallas_call(flip_body, grid=(9,), in_specs=[pl.BlockSpec((C, C), lambd...]
    concatenate x3, local copies, waits for them, and re-layouts: 2.81 us -> 0.34 us  [on_device(): jnp.concatenate([weighted, chosen, totals], axis=1).astype(jnp.bfloat16)]
    all_to_all x1, waiting for transfers between devices: 13.3 us -> 11 us  [on_device(): lax.all_to_all(sums.reshape(shards, micro, -1), 'shard', 0, 0, tiled=True)]
  transfers between devices with their start and end apart: 12 -> 12, of which waited for: 5 -> 5; matrix products, arithmetic and copies ran while one was open for 6% -> 2% of each run, Pallas kernels for 2% -> 5%
where the time goes in v2:
time: 172 us
  waiting for transfers between devices  84.8 us (49%)
  starting transfers between devices  49.6 us (29%)
  Pallas kernels  24.3 us (14%)
  other arithmetic  5.37 us (3%)
  local copies, waits for them, and re-layouts  3.97 us (2%)
  matrix products  2.58 us (2%)
    ppermute x3, waiting for transfers between devices, on_device(): lax.ppermute(g, 'section', [(2 * s + c, 2 * s - 2 + c) for c in range(2)])  55.1 us
    all_to_all x1, waiting for transfers between devices, on_device(): lax.all_to_all(sent, 'shard', 0, 0, tiled=True).reshape(shards * micro, -1)  13.4 us
    all_to_all x1, starting transfers between devices, on_device(): lax.all_to_all(sent, 'shard', 0, 0, tiled=True).reshape(shards * micro, -1)  12.9 us
    all_to_all x1, waiting for transfers between devices, on_device(): lax.all_to_all(sums.reshape(shards, micro, -1), 'shard', 0, 0, tiled=True)  11 us
    ppermute x2, starting transfers between devices, on_device(): peer = tuple((lax.ppermute(w, 'section', swap) for w in own))  10.8 us
    ppermute x1, starting transfers between devices, on_device(): taken = lax.ppermute(given, 'section', swap)  10.7 us
    pallas_call x1, Pallas kernels, flip_all(): pl.pallas_call(flip_body, grid=(9,), in_specs=[pl.BlockSpec((C, C), lambd...  8.51 us
    pallas_call x4, Pallas kernels, backward_stage(): pl.pallas_call(backward_body, in_specs=[SM, VM, HB, HB, HB, HB, VM, HB, V...  8.35 us
  transfers between devices with their start and end apart: 12, of which 5 were waited for; matrix products, arithmetic and copies ran while one was open for 2% of the time, Pallas kernels for 5%

profile of v2, /device:TPU:1, one launch (start us, length us, event | category | flops | bytes accessed | tf_op | source)
XLA Modules:
  0.0 171.7 jit_solution(4265247705027254090)
XLA Ops:
  0.0 8.9 %collective-permute-start = (bf16[2304,256]{1,0:T(8,128)(2,1)}, bf16[2304,256]{1,0:T(8,128)(2,1)S(1)}, u32[]{:S(2)}, u32[]{:S(2)}) collective-permute-start(bf16[2304,256]{1,0:T(8,128)(2,1)} %bitcast.36), channel_id=1, source_target_pairs={{0,64},{64,0},{128,192},{192,128},{256,320},{320,256},{384,448},{4... | collective-permute-start | bytes 3538952 | tf_op jit(solution)/shard_map/ppermute | solution.py:263
  8.9 1.9 %collective-permute-start.1 = (bf16[2304,256]{1,0:T(8,128)(2,1)}, bf16[2304,256]{1,0:T(8,128)(2,1)S(1)}, u32[]{:S(2)}, u32[]{:S(2)}) collective-permute-start(bf16[2304,256]{1,0:T(8,128)(2,1)} %bitcast.42), channel_id=1, source_target_pairs={{0,64},{64,0},{128,192},{192,128},{256,320},{320,256},{384,448},{4... | collective-permute-start | bytes 3538952 | tf_op jit(solution)/shard_map/ppermute | solution.py:263
  10.8 0.7 pad_maximum_fusion.1
  11.5 2.4 %collective-permute-start.2 = (f32[3,256]{1,0:T(4,128)S(1)}, f32[3,256]{1,0:T(4,128)S(1)}, u32[]{:S(2)}, u32[]{:S(2)}) collective-permute-start(f32[3,256]{1,0:T(4,128)S(1)} %pad_maximum_fusion.1), channel_id=1, source_target_pairs={{0,64},{64,0},{128,192},{192,128},{256,320},{320,256},{384,448},{4... | collective-permute-start | bytes 9224 | tf_op jit(solution)/shard_map/ppermute | solution.py:257
  14.0 0.7 bitcast_dynamic-update-slice_fusion.1
  14.7 0.2 constant_dynamic-slice_fusion.3
  14.9 0.1 pad_add_fusion.flag
  15.1 0.0 collective-permute-done.2
  15.1 0.0 collective-permute-done.1.peer2.refs_3_
  15.2 1.0 copy-done.2
  16.2 0.4 copy-done.3
  16.6 5.6 %forward_stage.4 = (bf16[2,224,256]{2,1,0:T(8,128)(2,1)S(1)}, f32[2,448,256]{2,1,0:T(8,128)}) custom-call(s32[2]{0:T(128)S(1)} %pad_add_fusion.flag, bf16[2,224,256]{2,1,0:T(8,128)(2,1)S(1)} %bitcast.35, bf16[2304,256]{1,0:T(8,128)(2,1)} %bitcast.37, bf16[2304,256]{1,0:T(8,128)(2,1)} %bitcast.43, bf16[2304,256]{1,0:T(8,128)(2,1)} %copy-done.2, ...), custom_call_target="tpu_custom_call" | custom-call | flops 2113929216 | bytes 6000000 | tf_op jit(solution)/shard_map/forward_stage/pallas_call | solution.py:170
  22.2 1.3 collective-permute-start.3
  23.5 0.1 pad_add_fusion.1.flag
  24.2 0.1 pad_add_fusion.2.flag
  24.3 4.4 %collective-permute-done.3.x_ref = bf16[2,224,256]{2,1,0:T(8,128)(2,1)S(1)} collective-permute-done((bf16[2,224,256]{2,1,0:T(8,128)(2,1)S(1)}, bf16[2,224,256]{2,1,0:T(8,128)(2,1)S(1)}, u32[]{:S(2)}, u32[]{:S(2)}) %collective-permute-start.3) | collective-permute-done | bytes 229408 | tf_op jit(solution)/shard_map/ppermute | solution.py:282
  28.7 0.6 forward_stage.5
  29.3 0.7 collective-permute-start.4
  30.0 0.1 pad_add_fusion.3.flag
  30.1 0.4 fusion
  30.6 0.0 collective-permute-done.4.x_ref
  30.6 0.6 forward_stage.6
  31.2 0.7 collective-permute-start.5
  31.9 0.0 copy-start.4
  31.9 0.0 copy-start.6
  31.9 0.6 forward_stage.7
  32.5 0.1 multiply_reduce_fusion
  32.6 0.2 copy-done.4
  32.8 0.3 multiply_reduce_fusion.2
  33.1 0.1 multiply_convert_fusion.2
  33.2 0.7 broadcast_in_dim.33
  33.9 12.9 %all-to-all-start = ((bf16[64,2,512]{2,1,0:T(2,128)(2,1)}), bf16[64,2,512]{2,1,0:T(2,128)(2,1)S(1)}, u32[]{:S(2)}, u32[]{:S(2)}) async-start(bf16[64,2,512]{2,1,0:T(2,128)(2,1)} %broadcast_in_dim.33), calls=%async_computation | async-start | bytes 262144 | tf_op jit(solution)/shard_map/all_to_all | solution.py:288
  46.9 0.1 copy.25
  47.0 0.1 eq.38
  47.1 0.6 convolution_convert_fusion
  47.8 0.1 concatenate.19
  47.8 13.4 %all-to-all-done = bf16[64,2,512]{2,1,0:T(2,128)(2,1)S(1)} async-done(((bf16[64,2,512]{2,1,0:T(2,128)(2,1)}), bf16[64,2,512]{2,1,0:T(2,128)(2,1)S(1)}, u32[]{:S(2)}, u32[]{:S(2)}) %all-to-all-start) | async-done | bytes 131104 | tf_op jit(solution)/shard_map/all_to_all | solution.py:288
  61.2 0.1 reshape.78
  61.2 1.0 fusion.20
  62.2 0.5 convolution_convert_fusion.1
  62.8 0.1 concatenate.18
  62.9 0.2 concatenate.23
  63.1 1.0 pad_maximum_fusion
  64.1 7.4 %all-to-all-start.1 = ((bf16[64,2,1025]{2,1,0:T(2,128)(2,1)}), bf16[64,2,1025]{2,1,0:T(2,128)(2,1)S(1)}, u32[]{:S(2)}, u32[]{:S(2)}) async-start(bf16[64,2,1025]{2,1,0:T(2,128)(2,1)} %pad_maximum_fusion), calls=%async_computation.1 | async-start | bytes 589824 | tf_op jit(solution)/shard_map/all_to_all | solution.py:306
  71.5 8.5 %flip_all.1 = (bf16[2304,256]{1,0:T(8,128)(2,1)}, bf16[2304,256]{1,0:T(8,128)(2,1)}, bf16[2304,256]{1,0:T(8,128)(2,1)}, bf16[2304,256]{1,0:T(8,128)(2,1)}) custom-call(bf16[2304,256]{1,0:T(8,128)(2,1)} %bitcast.41, bf16[2304,256]{1,0:T(8,128)(2,1)} %bitcast.47, bf16[2304,256]{1,0:T(8,128)(2,1)} %copy-done.2, bf16[2304,256]{1,0:T(8,128)(2,1)} %copy-done.3), custom_call_target="tpu_custom_call" | custom-call | flops 1207959552 | bytes 9000000 | tf_op jit(solution)/shard_map/flip_all/pallas_call | solution.py:217
  80.0 11.0 %all-to-all-done.1 = bf16[64,2,1025]{2,1,0:T(2,128)(2,1)S(1)} async-done(((bf16[64,2,1025]{2,1,0:T(2,128)(2,1)}), bf16[64,2,1025]{2,1,0:T(2,128)(2,1)S(1)}, u32[]{:S(2)}, u32[]{:S(2)}) %all-to-all-start.1) | async-done | bytes 262432 | tf_op jit(solution)/shard_map/all_to_all | solution.py:306
  91.1 0.3 convert_reduce_fusion
  91.3 0.1 slice_reduce_fusion
  91.4 0.2 multiply_reduce_fusion.1
  91.6 0.2 fusion.9
  91.9 0.6 backward_stage.4
  92.5 0.7 collective-permute-start.6
  93.2 0.6 backward_stage.5
  93.8 0.7 collective-permute-start.7
  94.5 0.6 backward_stage.6
  95.1 1.3 collective-permute-start.8
  96.4 55.1 %collective-permute-done.8.g_ref = bf16[2,224,256]{2,1,0:T(8,128)(2,1)S(1)} collective-permute-done((bf16[2,224,256]{2,1,0:T(8,128)(2,1)S(1)}, bf16[2,224,256]{2,1,0:T(8,128)(2,1)S(1)}, u32[]{:S(2)}, u32[]{:S(2)}) %collective-permute-start.8) | collective-permute-done | bytes 229408 | tf_op jit(solution)/shard_map/ppermute | solution.py:326
  151.6 6.5 %backward_stage.7 = (bf16[2,224,256]{2,1,0:T(8,128)(2,1)}, bf16[2,2,224,256]{3,2,1,0:T(8,128)(2,1)S(1)}) custom-call(s32[2]{0:T(128)S(1)} %pad_add_fusion.flag, bf16[2,224,256]{2,1,0:T(8,128)(2,1)S(1)} %collective-permute-done.8.g_ref, bf16[2304,256]{1,0:T(8,128)(2,1)} %get-tuple-element.28.own1, ...), custom_call_target="tpu_custom_call", output_to_operand_aliasing={{1}: (8, {})} | custom-call | flops 2113929216 | bytes 6000000 | tf_op jit(solution)/shard_map/backward_stage/pallas_call | solution.py:187
  158.2 0.2 copy.28
  158.4 10.7 %collective-permute-start.9 = (bf16[2,196,256]{2,0,1:T(2,128)(2,1)S(1)}, bf16[2,196,256]{2,0,1:T(2,128)(2,1)S(1)}, u32[]{:S(2)}, u32[]{:S(2)}) collective-permute-start(bf16[2,196,256]{2,0,1:T(2,128)(2,1)S(1)} %bitcast.51), channel_id=1, source_target_pairs={{0,64},{64,0},{128,192},{192,128},{256,320},{320,256},{384,448},{4... | collective-permute-start | bytes 602120 | tf_op jit(solution)/shard_map/ppermute | solution.py:333
  169.1 0.2 copy.27
  169.3 0.8 collective-permute-done.9
  170.2 0.3 broadcast_select_fusion.1
  170.5 1.2 maximum_bitcast_fusion
  (27 shorter events, 0.3 us)
Async XLA Ops:
  0.0 14.7 %copy-start = (bf16[4,1,196,256]{3,0,2,1:T(4,128)(2,1)S(1)}, bf16[4,1,196,256]{3,0,2,1:T(4,128)(2,1)}, u32[]{:S(2)}) copy-start(bf16[4,1,196,256]{3,0,2,1:T(4,128)(2,1)} %param.11) | copy-start | bytes 1204228
  0.0 15.1 %collective-permute-start = (bf16[2304,256]{1,0:T(8,128)(2,1)}, bf16[2304,256]{1,0:T(8,128)(2,1)S(1)}, u32[]{:S(2)}, u32[]{:S(2)}) collective-permute-start(bf16[2304,256]{1,0:T(8,128)(2,1)} %bitcast.36), channel_id=1, source_target_pairs={{0,64},{64,0},{128,192},{192,128},{256,320},{320,256},{384,448},{4... | collective-permute-start | bytes 3538952 | tf_op jit(solution)/shard_map/ppermute | solution.py:263
  8.9 6.3 %collective-permute-start.1 = (bf16[2304,256]{1,0:T(8,128)(2,1)}, bf16[2304,256]{1,0:T(8,128)(2,1)S(1)}, u32[]{:S(2)}, u32[]{:S(2)}) collective-permute-start(bf16[2304,256]{1,0:T(8,128)(2,1)} %bitcast.42), channel_id=1, source_target_pairs={{0,64},{64,0},{128,192},{192,128},{256,320},{320,256},{384,448},{4... | collective-permute-start | bytes 3538952 | tf_op jit(solution)/shard_map/ppermute | solution.py:263
  11.5 3.6 %collective-permute-start.2 = (f32[3,256]{1,0:T(4,128)S(1)}, f32[3,256]{1,0:T(4,128)S(1)}, u32[]{:S(2)}, u32[]{:S(2)}) collective-permute-start(f32[3,256]{1,0:T(4,128)S(1)} %pad_maximum_fusion.1), channel_id=1, source_target_pairs={{0,64},{64,0},{128,192},{192,128},{256,320},{320,256},{384,448},{4... | collective-permute-start | bytes 9224 | tf_op jit(solution)/shard_map/ppermute | solution.py:257
  15.1 1.0 copy-start.2
  15.1 1.4 copy-start.3
  22.2 6.5 %collective-permute-start.3 = (bf16[2,224,256]{2,1,0:T(8,128)(2,1)S(1)}, bf16[2,224,256]{2,1,0:T(8,128)(2,1)S(1)}, u32[]{:S(2)}, u32[]{:S(2)}) collective-permute-start(bf16[2,224,256]{2,1,0:T(8,128)(2,1)S(1)} %get-tuple-element.24), channel_id=1, source_target_pairs={{0,128},{64,192},{1,129},{65,193},{2,130},{66,194},{3,131},{67,195... | collective-permute-start | bytes 688136 | tf_op jit(solution)/shard_map/ppermute | solution.py:282
  24.3 5.8 %copy-start.5 = (bf16[196,256]{1,0:T(8,128)(2,1)S(1)}, bf16[196,256]{1,0:T(8,128)(2,1)}, u32[]{:S(2)}) copy-start(bf16[196,256]{1,0:T(8,128)(2,1)} %param.17) | copy-start | bytes 301060
  24.3 5.8 %copy-start.1 = (bf16[1664,512]{1,0:T(8,128)(2,1)S(1)}, bf16[1664,512]{1,0:T(8,128)(2,1)}, u32[]{:S(2)}) copy-start(bf16[1664,512]{1,0:T(8,128)(2,1)} %param.19) | copy-start | bytes 5111812
  29.3 1.2 collective-permute-start.4
  31.2 0.7 collective-permute-start.5
  31.9 1.0 copy-start.4
  31.9 15.0 %copy-start.6 = (s32[4,64]{1,0:T(4,128)S(1)}, s32[4,64]{1,0:T(4,128)}, u32[]{:S(2)}) copy-start(s32[4,64]{1,0:T(4,128)} %param.20) | copy-start | bytes 3076
  33.9 27.3 %all-to-all-start = ((bf16[64,2,512]{2,1,0:T(2,128)(2,1)}), bf16[64,2,512]{2,1,0:T(2,128)(2,1)S(1)}, u32[]{:S(2)}, u32[]{:S(2)}) async-start(bf16[64,2,512]{2,1,0:T(2,128)(2,1)} %broadcast_in_dim.33), calls=%async_computation | async-start | bytes 262144 | tf_op jit(solution)/shard_map/all_to_all | solution.py:288
  64.1 27.0 %all-to-all-start.1 = ((bf16[64,2,1025]{2,1,0:T(2,128)(2,1)}), bf16[64,2,1025]{2,1,0:T(2,128)(2,1)S(1)}, u32[]{:S(2)}, u32[]{:S(2)}) async-start(bf16[64,2,1025]{2,1,0:T(2,128)(2,1)} %pad_maximum_fusion), calls=%async_computation.1 | async-start | bytes 589824 | tf_op jit(solution)/shard_map/all_to_all | solution.py:306
  92.5 0.7 collective-permute-start.6
  93.8 0.7 collective-permute-start.7
  95.1 56.4 %collective-permute-start.8 = (bf16[2,224,256]{2,1,0:T(8,128)(2,1)S(1)}, bf16[2,224,256]{2,1,0:T(8,128)(2,1)S(1)}, u32[]{:S(2)}, u32[]{:S(2)}) collective-permute-start(bf16[2,224,256]{2,1,0:T(8,128)(2,1)S(1)} %get-tuple-element.39), channel_id=1, source_target_pairs={{128,0},{192,64},{129,1},{193,65},{130,2},{194,66},{131,3},{195,67... | collective-permute-start | bytes 688136 | tf_op jit(solution)/shard_map/ppermute | solution.py:326
  158.4 11.8 %collective-permute-start.9 = (bf16[2,196,256]{2,0,1:T(2,128)(2,1)S(1)}, bf16[2,196,256]{2,0,1:T(2,128)(2,1)S(1)}, u32[]{:S(2)}, u32[]{:S(2)}) collective-permute-start(bf16[2,196,256]{2,0,1:T(2,128)(2,1)S(1)} %bitcast.51), channel_id=1, source_target_pairs={{0,64},{64,0},{128,192},{192,128},{256,320},{320,256},{384,448},{4... | collective-permute-start | bytes 602120 | tf_op jit(solution)/shard_map/ppermute | solution.py:333

commit v3 on v2

v3 whole, which is shorter than its diff:
```python
import functools
import math

import jax
import jax.numpy as jnp
from jax import lax
from jax.experimental import pallas as pl
from jax.experimental.pallas import tpu as pltpu
from jax.sharding import PartitionSpec as P

SIDE = 14
WIDE = 16
ROWS = SIDE * WIDE
C = 256

margin_value = 0.4
scale_value = 64.0
tiny_value = 1e-06

VM = pl.BlockSpec(memory_space=pltpu.VMEM)
HB = pl.BlockSpec(memory_space=pltpu.HBM)
SM = pl.BlockSpec(memory_space=pltpu.SMEM)
LIMIT = 20 * 1024 * 1024


def keep_columns(rows):
    return (lax.broadcasted_iota(jnp.int32, (rows, C), 0) % WIDE) < SIDE


HALF = ROWS // 2


def build(value, cols, base):
    rows = value.shape[0]
    parts = (pltpu.roll(value, 1, 0), value, pltpu.roll(value, rows - 1, 0))
    for place, part in enumerate(parts):
        cols[WIDE + base : WIDE + base + rows, place * C : (place + 1) * C] = part.astype(jnp.bfloat16)


def conv(cols, weights, base):
    acc = None
    for step in range(3):
        part = jnp.dot(
            cols[base + WIDE * step : base + WIDE * step + HALF, :],
            weights[step * 3 * C : (step + 1) * 3 * C, :],
            preferred_element_type=jnp.float32,
        )
        acc = part if acc is None else acc + part
    return acc


def clear_border(cols):
    for i in range(2):
        cols[i, 0:WIDE, :] = jnp.zeros((WIDE, 3 * C), jnp.bfloat16)
        cols[i, WIDE + ROWS :, :] = jnp.zeros((WIDE, 3 * C), jnp.bfloat16)


HALVES = tuple(slice(h * HALF, (h + 1) * HALF) for h in range(2))


def load_body(flag, own1, own2, peer1, peer2, *rest):
    held, sems = rest[-2:]
    for k, source in enumerate((own1, own2)):
        pltpu.make_async_copy(source, held.at[flag[0], k], sems.at[0, k]).start()
    for k, source in enumerate((peer1, peer2)):
        pltpu.make_async_copy(source, held.at[1 - flag[0], k], sems.at[1, k]).start()
    for k, source in enumerate((own1, own2)):
        pltpu.make_async_copy(source, held.at[flag[0], k], sems.at[0, k]).wait()
    for k, source in enumerate((peer1, peer2)):
        pltpu.make_async_copy(source, held.at[1 - flag[0], k], sems.at[1, k]).wait()


def forward_body(flag, x_ref, held, vec_ref, out_ref, z_ref, cols, run, zed, zsem):
    @pl.when(flag[0] == 1)
    def _():
        clear_border(cols)
        keep = keep_columns(HALF)
        run[...] = x_ref[0].astype(jnp.float32)

        def one(u, carry):
            vec = vec_ref[u]
            for h in HALVES:
                build(run[h], cols.at[0], h.start)
            for h in HALVES:
                pre = conv(cols.at[0], held.at[u, 0], h.start) * vec[0:1] + vec[1:2]
                zed[u, h] = pre.astype(jnp.bfloat16)
                leak = vec[2:3]
                rest = jnp.log(1.0 + jnp.exp(-4.0 * jnp.abs(pre)))
                active = pre * jnp.where(pre < 0.0, leak, 1.0) + (0.25 * (1.0 - leak)) * rest
                build(jnp.where(keep, active, 0.0), cols.at[1], h.start)
            pltpu.make_async_copy(zed.at[u], z_ref.at[u], zsem.at[u]).start()
            for h in HALVES:
                result = run[h] + conv(cols.at[1], held.at[u, 1], h.start)
                result = jnp.where(keep, result, 0.0).astype(jnp.bfloat16)
                run[h] = result.astype(jnp.float32)
            return carry

        lax.fori_loop(0, 2, one, 0)
        out_ref[0] = run[...].astype(jnp.bfloat16)
        for u in range(2):
            pltpu.make_async_copy(zed.at[u], z_ref.at[u], zsem.at[u]).wait()


def backward_body(flag, g_ref, held, vec_ref, z_ref, store_in, out_ref, store, cols, run, zed, zsem):
    @pl.when(flag[0] == 1)
    def _():
        for u in (1, 0):
            pltpu.make_async_copy(z_ref.at[u], zed.at[u], zsem.at[u]).start()
        clear_border(cols)
        keep = keep_columns(HALF)
        run[...] = g_ref[0].astype(jnp.float32)

        def one(step, carry):
            u = 1 - step
            vec = vec_ref[u]
            for h in HALVES:
                build(run[h], cols.at[0], h.start)
            pltpu.make_async_copy(z_ref.at[u], zed.at[u], zsem.at[u]).wait()
            for h in HALVES:
                pre = zed[u, h].astype(jnp.float32)
                half = 0.5 * vec[0:1]
                slope = half * (1.0 + vec[2:3]) + half * (1.0 - vec[2:3]) * jnp.tanh(2.0 * pre)
                hidden = conv(cols.at[0], held.at[u, 1], h.start) * slope
                build(jnp.where(keep, hidden, 0.0), cols.at[1], h.start)
            for h in HALVES:
                result = run[h] + conv(cols.at[1], held.at[u, 0], h.start)
                result = jnp.where(keep, result, 0.0).astype(jnp.bfloat16)
                run[h] = result.astype(jnp.float32)
                store[u, h] = result
            return carry

        lax.fori_loop(0, 2, one, 0)
        out_ref[0] = run[...].astype(jnp.bfloat16)


def in_hbm(*arrays):
    return [pltpu.with_memory_space_constraint(a, pltpu.HBM) for a in arrays]


CONV_COST = pl.CostEstimate(flops=4 * 2 * 224 * 2304 * 256, bytes_accessed=6_000_000, transcendentals=250_000)
STAGE_LIMIT = 8 * 1024 * 1024
STAGE_SCRATCH = [
    pltpu.VMEM((2, ROWS + 2 * WIDE, 3 * C), jnp.bfloat16),
    pltpu.VMEM((ROWS, C), jnp.float32),
    pltpu.VMEM((2, ROWS, C), jnp.bfloat16),
    pltpu.SemaphoreType.DMA((2,)),
]


def load_weights(core, weights, name, before=()):
    return pl.pallas_call(
        load_body,
        in_specs=[SM, HB, HB, HB, HB] + [pl.BlockSpec(memory_space=pl.ANY)] * len(before),
        out_specs=VM,
        out_shape=jax.ShapeDtypeStruct((2, 2, *weights[0].shape), weights[0].dtype),
        scratch_shapes=[pltpu.SemaphoreType.DMA((2, 2))],
        compiler_params=pltpu.CompilerParams(vmem_limit_bytes=STAGE_LIMIT),
        cost_estimate=pl.CostEstimate(flops=300_000_000, bytes_accessed=9_000_000, transcendentals=0),
        name=name,
    )(core, *in_hbm(*weights), *before)


def forward_stage(flag, x, held, vec):
    return pl.pallas_call(
        forward_body,
        in_specs=[SM, VM, VM, VM],
        out_specs=[VM, HB],
        out_shape=[
            jax.ShapeDtypeStruct(x.shape, jnp.bfloat16),
            pltpu.HBM((2, ROWS, C), jnp.bfloat16),
        ],
        scratch_shapes=STAGE_SCRATCH,
        compiler_params=pltpu.CompilerParams(vmem_limit_bytes=STAGE_LIMIT),
        cost_estimate=CONV_COST,
        name="forward_stage",
    )(flag, x, held, vec)


def backward_stage(flag, g, held, vec, z, store):
    return pl.pallas_call(
        backward_body,
        in_specs=[SM, VM, VM, VM, HB, VM],
        out_specs=[VM, VM],
        out_shape=[
            jax.ShapeDtypeStruct(g.shape, jnp.bfloat16),
            jax.ShapeDtypeStruct(store.shape, store.dtype),
        ],
        scratch_shapes=STAGE_SCRATCH,
        input_output_aliases={5: 1},
        compiler_params=pltpu.CompilerParams(vmem_limit_bytes=STAGE_LIMIT),
        cost_estimate=CONV_COST,
        name="backward_stage",
    )(flag, g, held, vec, *in_hbm(z), store)


def flip_body(*refs):
    eye = (
        lax.broadcasted_iota(jnp.int32, (C, C), 0) == lax.broadcasted_iota(jnp.int32, (C, C), 1)
    ).astype(jnp.float32).astype(jnp.bfloat16)
    half = len(refs) // 2
    for source, target in zip(refs[:half], refs[half:]):
        turned = lax.dot_general(
            eye, source[...], (((1,), (1,)), ((), ())), preferred_element_type=jnp.float32
        )
        target[...] = turned.astype(jnp.bfloat16)


def flip_all(weights):
    count = len(weights)
    return pl.pallas_call(
        flip_body,
        grid=(9,),
        in_specs=[pl.BlockSpec((C, C), lambda t: (t, 0))] * count,
        out_specs=[pl.BlockSpec((C, C), lambda t: (8 - t, 0))] * count,
        out_shape=[pltpu.HBM(w.shape, w.dtype) for w in weights],
        compiler_params=pltpu.CompilerParams(vmem_limit_bytes=LIMIT),
        cost_estimate=pl.CostEstimate(flops=36 * 2 * 256**3, bytes_accessed=9_000_000, transcendentals=0),
        name="flip_all",
    )(*in_hbm(*weights))


def unit_scale(values):
    squares = jnp.mean(values * values, axis=-1, keepdims=True)
    factor = lax.rsqrt(squares + tiny_value) / math.sqrt(values.shape[-1])
    return (values * factor, squares, factor)


def on_device(
    section_input,
    conv_one,
    conv_two,
    unit_gain,
    offset_bias,
    leak_slope,
    depthwise,
    embed_weight,
    class_centers,
    labels,
    class_offsets,
):
    sections = lax.axis_size("section")
    shards = lax.axis_size("shard")
    planes = sections // 2
    section_index = lax.axis_index("section")
    plane = section_index // 2
    core = section_index % 2
    swap = [(s, s ^ 1) for s in range(sections)]

    def stacked(own):
        peer = lax.ppermute(own, "section", swap)
        both = jnp.zeros((2, *own.shape), own.dtype)
        both = lax.dynamic_update_index_in_dim(both, own, core, 0)
        return lax.dynamic_update_index_in_dim(both, peer, 1 - core, 0)

    own = (conv_one[0], conv_two[0])
    peer = tuple(lax.ppermute(w, "section", swap) for w in own)
    weights = (*own, *peer)
    vec = stacked(jnp.concatenate([unit_gain, offset_bias, leak_slope], axis=0))
    micro = section_input.shape[0] // 2

    def widened(rows):
        grid = rows.reshape(-1, SIDE, SIDE, C)
        return jnp.pad(grid, ((0, 0), (0, 0), (0, WIDE - SIDE), (0, 0))).reshape(-1, ROWS, C)

    mine = lax.dynamic_slice_in_dim(section_input[:, 0], core * micro, micro, 0)
    x = widened(mine)
    flags = [(plane == s).astype(jnp.int32).reshape(1) for s in range(planes)]
    flips = flip_all(weights)
    parts = [x[m : m + 1] for m in range(micro)]
    class_ids = class_offsets[0] + jnp.arange(class_centers.shape[0], dtype=jnp.int32)
    held = load_weights(core.reshape(1), weights, "load_forward", (*parts, class_ids, *flags))
    saved = {}
    for s in range(planes):
        for m in range(micro):
            parts[m], saved[s, m] = forward_stage(flags[s], parts[m], held, vec)
            if s < planes - 1:
                parts[m] = lax.ppermute(parts[m], "section", [(2 * s + c, 2 * s + 2 + c) for c in range(2)])
    x = jnp.concatenate(parts, axis=0)
    x, depthwise, embed_weight, class_centers, labels = lax.optimization_barrier(
        (x, depthwise, embed_weight, class_centers, labels)
    )
    pool_weight = widened(depthwise)[0].astype(jnp.float32)
    pooled = jnp.sum(x.astype(jnp.float32) * pool_weight[None], axis=1).astype(jnp.bfloat16)
    embedded = jnp.dot(pooled, embed_weight, preferred_element_type=jnp.float32)
    normed, squares, factor = unit_scale(embedded)
    sent = jnp.broadcast_to(normed.astype(jnp.bfloat16)[None], (shards, *normed.shape))
    unit_half = lax.all_to_all(sent, "shard", 0, 0, tiled=True).reshape(shards * micro, -1)
    centres_unit = unit_scale(class_centers.astype(jnp.float32))[0].astype(jnp.bfloat16)
    my_labels = lax.dynamic_slice_in_dim(labels, core * micro, micro, 0).T.reshape(-1)
    label_hits = my_labels[:, None] == class_ids[None, :]
    cosines = lax.dot_general(
        unit_half, centres_unit, (((1,), (1,)), ((), ())), preferred_element_type=jnp.float32
    )
    logits = scale_value * (cosines - margin_value * label_hits.astype(jnp.float32))
    exp_logits = jnp.exp(logits)
    weighted = jnp.dot(
        exp_logits.astype(jnp.bfloat16), centres_unit, preferred_element_type=jnp.float32
    )
    chosen = jnp.dot(
        label_hits.astype(jnp.bfloat16), centres_unit, preferred_element_type=jnp.float32
    )
    totals = jnp.sum(exp_logits, axis=1, keepdims=True)
    sums = jnp.concatenate([weighted, chosen, totals], axis=1).astype(jnp.bfloat16)
    sums = lax.all_to_all(sums.reshape(shards, micro, -1), "shard", 0, 0, tiled=True)
    sums = jnp.sum(sums.astype(jnp.float32), axis=0)
    width = embedded.shape[-1]
    grad_unit = scale_value * (
        sums[:, :width] / sums[:, 2 * width :] - sums[:, width : 2 * width]
    )
    inner = jnp.sum(embedded * grad_unit, axis=-1, keepdims=True)
    grad_embed = factor * (grad_unit - embedded * inner / (width * (squares + tiny_value)))
    grad_pooled = lax.dot_general(
        grad_embed.astype(jnp.bfloat16),
        embed_weight,
        (((1,), (1,)), ((), ())),
        preferred_element_type=jnp.float32,
    )
    g = (grad_pooled[:, None, :] * pool_weight[None]).astype(jnp.bfloat16)

    flips, g = lax.optimization_barrier((flips, g))
    flips = load_weights(core.reshape(1), flips, "load_backward")
    parts = [g[m : m + 1] for m in range(micro)]
    stores = [jnp.zeros((2, ROWS, C), jnp.bfloat16) for m in range(micro)]
    for s in reversed(range(planes)):
        for m in range(micro):
            parts[m], stores[m] = backward_stage(flags[s], parts[m], flips, vec, saved[s, m], stores[m])
            if s > 0:
                parts[m] = lax.ppermute(parts[m], "section", [(2 * s + c, 2 * s - 2 + c) for c in range(2)])
    store = jnp.stack(stores, axis=1)

    def narrowed(rows):
        return rows.reshape(-1, SIDE, WIDE, C)[:, :, :SIDE].reshape(-1, SIDE * SIDE, C)

    kept = narrowed(lax.dynamic_index_in_dim(store, core, 0, keepdims=False))
    given = narrowed(lax.dynamic_index_in_dim(store, 1 - core, 0, keepdims=False))
    taken = lax.ppermute(given, "section", swap)
    first = jnp.where(core == 0, kept, taken)
    second = jnp.where(core == 0, taken, kept)
    return jnp.concatenate([first, second], axis=0)[None, :, None]


def solution(mesh):
    placed = (
        P(None, "shard", None, None),
        P("section", None, None),
        P("section", None, None),
        P("section", None),
        P("section", None),
        P("section", None),
        P(),
        P(),
        P("shard", None),
        P(),
        P("shard"),
    )
    return jax.shard_map(
        on_device,
        mesh=mesh,
        in_specs=placed,
        out_specs=P("section", None, "shard", None, None),
        check_vma=False,
    )
```

time: 172 us -> 149 us (0.87)
  waiting for transfers between devices: 84.8 us -> 55 us
  starting transfers between devices: 49.6 us -> 53.5 us
    ppermute x6 -> x12, waiting for transfers between devices: 59.5 us -> 30 us  [the longest x6 28 us: on_device(): lax.ppermute(parts[m], 'section', [(2 * s + c, 2 * s - 2 + c) for c in ra...]
    ppermute x6 -> x12, starting transfers between devices: 5.3 us -> 10.5 us  [the longest x6 5.26 us: on_device(): lax.ppermute(parts[m], 'section', [(2 * s + c, 2 * s + 2 + c) for c in ra...]
    pallas_call x8 -> x18, Pallas kernels: 15.8 us -> 17.1 us  [the longest x8 7.4 us: backward_stage(): pl.pallas_call(backward_body, in_specs=[SM, VM, VM, VM, HB, VM], out_spec...]
  transfers between devices with their start and end apart: 12 -> 18, of which waited for: 5 -> 6; matrix products, arithmetic and copies ran while one was open for 2% -> 3% of each run, Pallas kernels for 5% -> 10%
where the time goes in v3:
time: 149 us; the launch traced here: 148 us
  waiting for transfers between devices  55 us (37%)
  starting transfers between devices  53.5 us (36%)
  Pallas kernels  25.6 us (17%)
  other arithmetic  5.14 us (3%)
  local copies, waits for them, and re-layouts  4.96 us (3%)
  matrix products  2.61 us (2%)
    ppermute x6, waiting for transfers between devices, on_device(): lax.ppermute(parts[m], 'section', [(2 * s + c, 2 * s - 2 + c) for c in ra...  28 us
    all_to_all x1, starting transfers between devices, on_device(): lax.all_to_all(sent, 'shard', 0, 0, tiled=True).reshape(shards * micro, -1)  13.1 us
    all_to_all x1, waiting for transfers between devices, on_device(): lax.all_to_all(sent, 'shard', 0, 0, tiled=True).reshape(shards * micro, -1)  12.8 us
    all_to_all x1, waiting for transfers between devices, on_device(): lax.all_to_all(sums.reshape(shards, micro, -1), 'shard', 0, 0, tiled=True)  11.4 us
    ppermute x2, starting transfers between devices, on_device(): peer = tuple((lax.ppermute(w, 'section', swap) for w in own))  10.8 us
    ppermute x1, starting transfers between devices, on_device(): taken = lax.ppermute(given, 'section', swap)  9.39 us
    pallas_call x1, Pallas kernels, flip_all(): pl.pallas_call(flip_body, grid=(9,), in_specs=[pl.BlockSpec((C, C), lambd...  8.51 us
    pallas_call x8, Pallas kernels, backward_stage(): pl.pallas_call(backward_body, in_specs=[SM, VM, VM, VM, HB, VM], out_spec...  7.4 us
  transfers between devices with their start and end apart: 18, of which 6 were waited for; matrix products, arithmetic and copies ran while one was open for 3% of the time, Pallas kernels for 10%

profile of v3, /device:TPU:1, one launch (start us, length us, event | category | flops | bytes accessed | tf_op | source)
XLA Modules:
  0.0 148.2 jit_solution(564860789755203683)
XLA Ops:
  0.0 8.9 %collective-permute-start = (bf16[2304,256]{1,0:T(8,128)(2,1)}, bf16[2304,256]{1,0:T(8,128)(2,1)S(1)}, u32[]{:S(2)}, u32[]{:S(2)}) collective-permute-start(bf16[2304,256]{1,0:T(8,128)(2,1)} %bitcast.44), channel_id=1, source_target_pairs={{0,64},{64,0},{128,192},{192,128},{256,320},{320,256},{384,448},{4... | collective-permute-start | bytes 3538952 | tf_op jit(solution)/shard_map/ppermute | solution.py:256
  8.9 1.9 %collective-permute-start.1 = (bf16[2304,256]{1,0:T(8,128)(2,1)}, bf16[2304,256]{1,0:T(8,128)(2,1)S(1)}, u32[]{:S(2)}, u32[]{:S(2)}) collective-permute-start(bf16[2304,256]{1,0:T(8,128)(2,1)} %bitcast.47), channel_id=1, source_target_pairs={{0,64},{64,0},{128,192},{192,128},{256,320},{320,256},{384,448},{4... | collective-permute-start | bytes 3538952 | tf_op jit(solution)/shard_map/ppermute | solution.py:256
  10.8 0.7 pad_maximum_fusion.2
  11.5 2.4 %collective-permute-start.2 = (f32[3,256]{1,0:T(4,128)S(1)}, f32[3,256]{1,0:T(4,128)S(1)}, u32[]{:S(2)}, u32[]{:S(2)}) collective-permute-start(f32[3,256]{1,0:T(4,128)S(1)} %pad_maximum_fusion.2), channel_id=1, source_target_pairs={{0,64},{64,0},{128,192},{192,128},{256,320},{320,256},{384,448},{4... | collective-permute-start | bytes 9224 | tf_op jit(solution)/shard_map/ppermute | solution.py:250
  14.6 0.2 constant_dynamic-slice_fusion.1
  14.9 0.5 pad_slice_fusion.1
  15.3 0.7 bitcast_dynamic-update-slice_fusion.1
  16.2 1.0 copy-done.1
  17.2 0.4 copy-done.2
  17.6 2.4 %load_forward.1.held = bf16[2,2,2304,256]{3,2,1,0:T(8,128)(2,1)S(1)} custom-call(s32[1]{0:T(128)} %bitcast.7.flag, bf16[2304,256]{1,0:T(8,128)(2,1)} %bitcast.45, bf16[2304,256]{1,0:T(8,128)(2,1)} %bitcast.48, bf16[2304,256]{1,0:T(8,128)(2,1)} %copy-done.1, bf16[2304,256]{1,0:T(8,128)(2,1)} %copy-done.2, bf16[1,224,256]{2,1,0:T(8,128)(2,1)S(1)} %bitcast.42, ...), custom_call_target="tpu_custom_call" | custom-call | flops 300000000 | bytes 9000000 | tf_op jit(solution)/shard_map/load_forward/pallas_call | solution.py:151
  20.0 2.4 %forward_stage.8 = (bf16[1,224,256]{2,1,0:T(8,128)(2,1)S(1)}, bf16[2,224,256]{2,1,0:T(8,128)(2,1)}) custom-call(s32[1]{0:T(128)} %bitcast.rest_3_.flag, bf16[1,224,256]{2,1,0:T(8,128)(2,1)S(1)} %bitcast.43, bf16[2,2,2304,256]{3,2,1,0:T(8,128)(2,1)S(1)} %load_forward.1.held, f32[2,3,256]{2,1,0:T(4,128)S(1)} %bitcast_dynamic-update-slice_fusion.vec_ref), custom_call_target="tpu_custom_call" | custom-call | flops 1056964608 | bytes 6000000 | tf_op jit(solution)/shard_map/forward_stage/pallas_call | solution.py:164
  22.4 1.3 collective-permute-start.3
  23.7 2.4 %forward_stage.12 = (bf16[1,224,256]{2,1,0:T(8,128)(2,1)S(1)}, bf16[2,224,256]{2,1,0:T(8,128)(2,1)}) custom-call(s32[1]{0:T(128)} %bitcast.rest_3_.flag, bf16[1,224,256]{2,1,0:T(8,128)(2,1)S(1)} %bitcast.41, bf16[2,2,2304,256]{3,2,1,0:T(8,128)(2,1)S(1)} %load_forward.1.held, f32[2,3,256]{2,1,0:T(4,128)S(1)} %bitcast_dynamic-update-slice_fusion.vec_ref), custom_call_target="tpu_custom_call" | custom-call | flops 1056964608 | bytes 6000000 | tf_op jit(solution)/shard_map/forward_stage/pallas_call | solution.py:164
  26.1 1.3 collective-permute-start.6
  27.5 0.7 collective-permute-start.4
  28.1 2.0 %collective-permute-done.6.x_ref = bf16[1,224,256]{2,1,0:T(8,128)(2,1)S(1)} collective-permute-done((bf16[1,224,256]{2,1,0:T(8,128)(2,1)S(1)}, bf16[1,224,256]{2,1,0:T(8,128)(2,1)S(1)}, u32[]{:S(2)}, u32[]{:S(2)}) %collective-permute-start.6) | collective-permute-done | bytes 114720 | tf_op jit(solution)/shard_map/ppermute | solution.py:277
  30.2 0.7 collective-permute-start.7
  30.9 0.7 collective-permute-start.5
  31.6 0.7 collective-permute-start.8
  32.3 0.0 copy-start.5
  32.4 0.0 copy-start.4
  32.5 0.8 copy-done.5
  33.4 0.1 multiply_reduce_fusion
  33.4 0.3 multiply_reduce_fusion.2
  33.7 0.1 multiply_convert_fusion.2
  33.8 0.7 broadcast_in_dim.30
  34.5 13.1 %all-to-all-start = ((bf16[64,2,512]{2,1,0:T(2,128)(2,1)}), bf16[64,2,512]{2,1,0:T(2,128)(2,1)S(1)}, u32[]{:S(2)}, u32[]{:S(2)}) async-start(bf16[64,2,512]{2,1,0:T(2,128)(2,1)} %broadcast_in_dim.30), calls=%async_computation | async-start | bytes 262144 | tf_op jit(solution)/shard_map/all_to_all | solution.py:287
  47.6 0.4 fusion
  48.1 0.1 copy.27
  48.2 0.1 eq.38
  48.3 0.6 convolution_convert_fusion
  48.9 0.1 concatenate.23
  49.0 12.8 %all-to-all-done = bf16[64,2,512]{2,1,0:T(2,128)(2,1)S(1)} async-done(((bf16[64,2,512]{2,1,0:T(2,128)(2,1)}), bf16[64,2,512]{2,1,0:T(2,128)(2,1)S(1)}, u32[]{:S(2)}, u32[]{:S(2)}) %all-to-all-start) | async-done | bytes 131104 | tf_op jit(solution)/shard_map/all_to_all | solution.py:287
  61.8 0.1 reshape.110
  61.8 1.0 fusion.23
  62.9 0.6 convolution_convert_fusion.1
  63.4 0.1 concatenate.22
  63.5 0.2 concatenate.27
  63.7 1.0 pad_maximum_fusion
  64.7 7.3 %all-to-all-start.1 = ((bf16[64,2,1025]{2,1,0:T(2,128)(2,1)}), bf16[64,2,1025]{2,1,0:T(2,128)(2,1)S(1)}, u32[]{:S(2)}, u32[]{:S(2)}) async-start(bf16[64,2,1025]{2,1,0:T(2,128)(2,1)} %pad_maximum_fusion), calls=%async_computation.1 | async-start | bytes 589824 | tf_op jit(solution)/shard_map/all_to_all | solution.py:304
  72.0 8.5 %flip_all.1 = (bf16[2304,256]{1,0:T(8,128)(2,1)}, bf16[2304,256]{1,0:T(8,128)(2,1)}, bf16[2304,256]{1,0:T(8,128)(2,1)}, bf16[2304,256]{1,0:T(8,128)(2,1)}) custom-call(bf16[2304,256]{1,0:T(8,128)(2,1)} %bitcast.46, bf16[2304,256]{1,0:T(8,128)(2,1)} %bitcast.49, bf16[2304,256]{1,0:T(8,128)(2,1)} %copy-done.1, bf16[2304,256]{1,0:T(8,128)(2,1)} %copy-done.2), custom_call_target="tpu_custom_call" | custom-call | flops 1207959552 | bytes 9000000 | tf_op jit(solution)/shard_map/flip_all/pallas_call | solution.py:210
  80.5 11.4 %all-to-all-done.1 = bf16[64,2,1025]{2,1,0:T(2,128)(2,1)S(1)} async-done(((bf16[64,2,1025]{2,1,0:T(2,128)(2,1)}), bf16[64,2,1025]{2,1,0:T(2,128)(2,1)S(1)}, u32[]{:S(2)}, u32[]{:S(2)}) %all-to-all-start.1) | async-done | bytes 262432 | tf_op jit(solution)/shard_map/all_to_all | solution.py:304
  91.9 0.3 convert_reduce_fusion
  92.2 0.1 slice_reduce_fusion
  92.3 0.2 multiply_reduce_fusion.1
  92.5 0.2 fusion.11
  92.8 2.4 %load_backward.1.held = bf16[2,2,2304,256]{3,2,1,0:T(8,128)(2,1)S(1)} custom-call(s32[1]{0:T(128)} %bitcast.7.flag, bf16[2304,256]{1,0:T(8,128)(2,1)} %get-tuple-element.67.own1, bf16[2304,256]{1,0:T(8,128)(2,1)} %get-tuple-element.68.own2, bf16[2304,256]{1,0:T(8,128)(2,1)} %get-tuple-element.69.peer1, bf16[2304,256]{1,0:T(8,128)(2,1)} %get-tuple-element.70.peer2), custom_call_target="tpu_custom_call" | custom-call | flops 300000000 | bytes 9000000 | tf_op jit(solution)/shard_map/load_backward/pallas_call | solution.py:151
  95.2 0.7 collective-permute-start.12
  95.9 0.7 collective-permute-start.9
  96.7 0.7 collective-permute-start.13
  97.4 0.7 collective-permute-start.10
  98.1 1.3 collective-permute-start.14
  99.5 1.3 collective-permute-start.11
  100.8 26.8 %collective-permute-done.14.g_ref = bf16[1,224,256]{2,1,0:T(8,128)(2,1)S(1)} collective-permute-done((bf16[1,224,256]{2,1,0:T(8,128)(2,1)S(1)}, bf16[1,224,256]{2,1,0:T(8,128)(2,1)S(1)}, u32[]{:S(2)}, u32[]{:S(2)}) %collective-permute-start.14) | collective-permute-done | bytes 114720 | tf_op jit(solution)/shard_map/ppermute | solution.py:328
  127.6 3.6 %backward_stage.15 = (bf16[1,224,256]{2,1,0:T(8,128)(2,1)}, bf16[2,224,256]{2,1,0:T(8,128)(2,1)S(1)}) custom-call(s32[1]{0:T(128)} %bitcast.rest_3_.flag, bf16[1,224,256]{2,1,0:T(8,128)(2,1)S(1)} %collective-permute-done.14.g_ref, bf16[2,2,2304,256]{3,2,1,0:T(8,128)(2,1)S(1)} %load_backward.1.held, ...), custom_call_target="tpu_custom_call", output_to_operand_aliasing={{1}: (5, {})} | custom-call | flops 1056964608 | bytes 6000000 | tf_op jit(solution)/shard_map/backward_stage/pallas_call | solution.py:180
  131.2 1.2 collective-permute-done.11.g_ref
  132.4 3.6 %backward_stage.11 = (bf16[1,224,256]{2,1,0:T(8,128)(2,1)}, bf16[2,224,256]{2,1,0:T(8,128)(2,1)S(1)}) custom-call(s32[1]{0:T(128)} %bitcast.rest_3_.flag, bf16[1,224,256]{2,1,0:T(8,128)(2,1)S(1)} %collective-permute-done.11.g_ref, bf16[2,2,2304,256]{3,2,1,0:T(8,128)(2,1)S(1)} %load_backward.1.held, ...), custom_call_target="tpu_custom_call", output_to_operand_aliasing={{1}: (5, {})} | custom-call | flops 1056964608 | bytes 6000000 | tf_op jit(solution)/shard_map/backward_stage/pallas_call | solution.py:180
  136.0 0.1 fusion.9
  136.1 0.2 copy.30
  136.3 9.4 %collective-permute-start.15 = (bf16[2,196,256]{2,0,1:T(2,128)(2,1)S(1)}, bf16[2,196,256]{2,0,1:T(2,128)(2,1)S(1)}, u32[]{:S(2)}, u32[]{:S(2)}) collective-permute-start(bf16[2,196,256]{2,0,1:T(2,128)(2,1)S(1)} %bitcast.53), channel_id=1, source_target_pairs={{0,64},{64,0},{128,192},{192,128},{256,320},{320,256},{384,448},{4... | collective-permute-start | bytes 602120 | tf_op jit(solution)/shard_map/ppermute | solution.py:336
  145.7 0.2 copy.29
  145.9 0.8 collective-permute-done.15
  146.7 0.3 broadcast_select_fusion.1
  147.1 1.2 maximum_bitcast_fusion
  (49 shorter events, 0.7 us)
Async XLA Ops:
  0.0 14.6 %copy-start = (bf16[4,1,196,256]{3,0,2,1:T(4,128)(2,1)S(1)}, bf16[4,1,196,256]{3,0,2,1:T(4,128)(2,1)}, u32[]{:S(2)}) copy-start(bf16[4,1,196,256]{3,0,2,1:T(4,128)(2,1)} %param.11) | copy-start | bytes 1204228
  0.0 16.2 %collective-permute-start = (bf16[2304,256]{1,0:T(8,128)(2,1)}, bf16[2304,256]{1,0:T(8,128)(2,1)S(1)}, u32[]{:S(2)}, u32[]{:S(2)}) collective-permute-start(bf16[2304,256]{1,0:T(8,128)(2,1)} %bitcast.44), channel_id=1, source_target_pairs={{0,64},{64,0},{128,192},{192,128},{256,320},{320,256},{384,448},{4... | collective-permute-start | bytes 3538952 | tf_op jit(solution)/shard_map/ppermute | solution.py:256
  8.9 7.3 %collective-permute-start.1 = (bf16[2304,256]{1,0:T(8,128)(2,1)}, bf16[2304,256]{1,0:T(8,128)(2,1)S(1)}, u32[]{:S(2)}, u32[]{:S(2)}) collective-permute-start(bf16[2304,256]{1,0:T(8,128)(2,1)} %bitcast.47), channel_id=1, source_target_pairs={{0,64},{64,0},{128,192},{192,128},{256,320},{320,256},{384,448},{4... | collective-permute-start | bytes 3538952 | tf_op jit(solution)/shard_map/ppermute | solution.py:256
  11.5 4.6 %collective-permute-start.2 = (f32[3,256]{1,0:T(4,128)S(1)}, f32[3,256]{1,0:T(4,128)S(1)}, u32[]{:S(2)}, u32[]{:S(2)}) collective-permute-start(f32[3,256]{1,0:T(4,128)S(1)} %pad_maximum_fusion.2), channel_id=1, source_target_pairs={{0,64},{64,0},{128,192},{192,128},{256,320},{320,256},{384,448},{4... | collective-permute-start | bytes 9224 | tf_op jit(solution)/shard_map/ppermute | solution.py:250
  16.2 1.0 copy-start.1
  16.2 1.4 copy-start.2
  22.4 5.0 %collective-permute-start.3 = (bf16[1,224,256]{2,1,0:T(8,128)(2,1)S(1)}, bf16[1,224,256]{2,1,0:T(8,128)(2,1)S(1)}, u32[]{:S(2)}, u32[]{:S(2)}) collective-permute-start(bf16[1,224,256]{2,1,0:T(8,128)(2,1)S(1)} %get-tuple-element.53), channel_id=1, source_target_pairs={{0,128},{64,192},{1,129},{65,193},{2,130},{66,194},{3,131},{67,195... | collective-permute-start | bytes 344072 | tf_op jit(solution)/shard_map/ppermute | solution.py:277
  26.1 4.1 %collective-permute-start.6 = (bf16[1,224,256]{2,1,0:T(8,128)(2,1)S(1)}, bf16[1,224,256]{2,1,0:T(8,128)(2,1)S(1)}, u32[]{:S(2)}, u32[]{:S(2)}) collective-permute-start(bf16[1,224,256]{2,1,0:T(8,128)(2,1)S(1)} %get-tuple-element.57), channel_id=1, source_target_pairs={{0,128},{64,192},{1,129},{65,193},{2,130},{66,194},{3,131},{67,195... | collective-permute-start | bytes 344072 | tf_op jit(solution)/shard_map/ppermute | solution.py:277
  27.5 3.4 %collective-permute-start.4 = (bf16[1,224,256]{2,1,0:T(8,128)(2,1)S(1)}, bf16[1,224,256]{2,1,0:T(8,128)(2,1)S(1)}, u32[]{:S(2)}, u32[]{:S(2)}) collective-permute-start(bf16[1,224,256]{2,1,0:T(8,128)(2,1)S(1)} %get-tuple-element.54), channel_id=1, source_target_pairs={{128,256},{192,320},{129,257},{193,321},{130,258},{194,322},{131,2... | collective-permute-start | bytes 344072 | tf_op jit(solution)/shard_map/ppermute | solution.py:277
  30.2 1.4 collective-permute-start.7
  30.9 1.4 collective-permute-start.5
  31.6 0.7 collective-permute-start.8
  32.3 0.9 copy-start.5
  32.4 1.1 copy-start.4
  32.4 15.2 %copy-start.3 = (bf16[1664,512]{1,0:T(8,128)(2,1)S(1)}, bf16[1664,512]{1,0:T(8,128)(2,1)}, u32[]{:S(2)}) copy-start(bf16[1664,512]{1,0:T(8,128)(2,1)} %param.19) | copy-start | bytes 5111812
  33.3 14.8 %copy-start.6 = (s32[4,64]{1,0:T(4,128)S(1)}, s32[4,64]{1,0:T(4,128)}, u32[]{:S(2)}) copy-start(s32[4,64]{1,0:T(4,128)} %param.20) | copy-start | bytes 3076
  34.5 27.3 %all-to-all-start = ((bf16[64,2,512]{2,1,0:T(2,128)(2,1)}), bf16[64,2,512]{2,1,0:T(2,128)(2,1)S(1)}, u32[]{:S(2)}, u32[]{:S(2)}) async-start(bf16[64,2,512]{2,1,0:T(2,128)(2,1)} %broadcast_in_dim.30), calls=%async_computation | async-start | bytes 262144 | tf_op jit(solution)/shard_map/all_to_all | solution.py:287
  64.7 27.2 %all-to-all-start.1 = ((bf16[64,2,1025]{2,1,0:T(2,128)(2,1)}), bf16[64,2,1025]{2,1,0:T(2,128)(2,1)S(1)}, u32[]{:S(2)}, u32[]{:S(2)}) async-start(bf16[64,2,1025]{2,1,0:T(2,128)(2,1)} %pad_maximum_fusion), calls=%async_computation.1 | async-start | bytes 589824 | tf_op jit(solution)/shard_map/all_to_all | solution.py:304
  95.2 1.4 collective-permute-start.12
  95.9 1.4 collective-permute-start.9
  96.7 1.4 collective-permute-start.13
  97.4 2.0 %collective-permute-start.10 = (bf16[1,224,256]{2,1,0:T(8,128)(2,1)S(1)}, bf16[1,224,256]{2,1,0:T(8,128)(2,1)S(1)}, u32[]{:S(2)}, u32[]{:S(2)}) collective-permute-start(bf16[1,224,256]{2,1,0:T(8,128)(2,1)S(1)} %get-tuple-element.75), channel_id=1, source_target_pairs={{256,128},{320,192},{257,129},{321,193},{258,130},{322,194},{259,1... | collective-permute-start | bytes 344072 | tf_op jit(solution)/shard_map/ppermute | solution.py:328
  98.1 29.5 %collective-permute-start.14 = (bf16[1,224,256]{2,1,0:T(8,128)(2,1)S(1)}, bf16[1,224,256]{2,1,0:T(8,128)(2,1)S(1)}, u32[]{:S(2)}, u32[]{:S(2)}) collective-permute-start(bf16[1,224,256]{2,1,0:T(8,128)(2,1)S(1)} %get-tuple-element.89), channel_id=1, source_target_pairs={{128,0},{192,64},{129,1},{193,65},{130,2},{194,66},{131,3},{195,67... | collective-permute-start | bytes 344072 | tf_op jit(solution)/shard_map/ppermute | solution.py:328
  99.5 32.9 %collective-permute-start.11 = (bf16[1,224,256]{2,1,0:T(8,128)(2,1)S(1)}, bf16[1,224,256]{2,1,0:T(8,128)(2,1)S(1)}, u32[]{:S(2)}, u32[]{:S(2)}) collective-permute-start(bf16[1,224,256]{2,1,0:T(8,128)(2,1)S(1)} %get-tuple-element.78), channel_id=1, source_target_pairs={{128,0},{192,64},{129,1},{193,65},{130,2},{194,66},{131,3},{195,67... | collective-permute-start | bytes 344072 | tf_op jit(solution)/shard_map/ppermute | solution.py:328
  136.3 10.4 %collective-permute-start.15 = (bf16[2,196,256]{2,0,1:T(2,128)(2,1)S(1)}, bf16[2,196,256]{2,0,1:T(2,128)(2,1)S(1)}, u32[]{:S(2)}, u32[]{:S(2)}) collective-permute-start(bf16[2,196,256]{2,0,1:T(2,128)(2,1)S(1)} %bitcast.53), channel_id=1, source_target_pairs={{0,64},{64,0},{128,192},{192,128},{256,320},{320,256},{384,448},{4... | collective-permute-start | bytes 602120 | tf_op jit(solution)/shard_map/ppermute | solution.py:336

commit v4 on v3

--- a/solution.py
+++ b/solution.py
@@ -18,6 +18,7 @@
 tiny_value = 1e-06
 
 VM = pl.BlockSpec(memory_space=pltpu.VMEM)
+AN = pl.BlockSpec(memory_space=pl.ANY)
 HB = pl.BlockSpec(memory_space=pltpu.HBM)
 SM = pl.BlockSpec(memory_space=pltpu.SMEM)
 LIMIT = 20 * 1024 * 1024
@@ -101,11 +102,9 @@
             pltpu.make_async_copy(zed.at[u], z_ref.at[u], zsem.at[u]).wait()
 
 
-def backward_body(flag, g_ref, held, vec_ref, z_ref, store_in, out_ref, store, cols, run, zed, zsem):
+def backward_body(image, flag, g_ref, held, vec_ref, z_ref, store_in, out_ref, store, cols, run):
     @pl.when(flag[0] == 1)
     def _():
-        for u in (1, 0):
-            pltpu.make_async_copy(z_ref.at[u], zed.at[u], zsem.at[u]).start()
         clear_border(cols)
         keep = keep_columns(HALF)
         run[...] = g_ref[0].astype(jnp.float32)
@@ -113,13 +112,13 @@
         def one(step, carry):
             u = 1 - step
             vec = vec_ref[u]
+            half = 0.5 * vec[0:1]
+            base = half * (1.0 + vec[2:3])
+            gain = half * (1.0 - vec[2:3])
             for h in HALVES:
                 build(run[h], cols.at[0], h.start)
-            pltpu.make_async_copy(z_ref.at[u], zed.at[u], zsem.at[u]).wait()
-            for h in HALVES:
-                pre = zed[u, h].astype(jnp.float32)
-                half = 0.5 * vec[0:1]
-                slope = half * (1.0 + vec[2:3]) + half * (1.0 - vec[2:3]) * jnp.tanh(2.0 * pre)
+            for h in HALVES:
+                slope = base + gain * jnp.tanh(2.0 * z_ref[image, u, h].astype(jnp.float32))
                 hidden = conv(cols.at[0], held.at[u, 1], h.start) * slope
                 build(jnp.where(keep, hidden, 0.0), cols.at[1], h.start)
             for h in HALVES:
@@ -131,6 +130,66 @@
 
         lax.fori_loop(0, 2, one, 0)
         out_ref[0] = run[...].astype(jnp.bfloat16)
+
+
+def tail_body(
+    flag, sums_ref, chosen_ref, embedded_ref, embed_ref, pool_ref, own1, own2, peer1, peer2, *rest
+):
+    saved, (g_ref, held, zbuf, sems, zsems) = rest[:-5], rest[-5:]
+    images = zbuf.shape[0]
+    core, plane = flag[0], flag[1]
+    copies = [
+        pltpu.make_async_copy(source, held.at[place, k], sems.at[side, k])
+        for side, place, pair in ((0, core, (own1, own2)), (1, 1 - core, (peer1, peer2)))
+        for k, source in enumerate(pair)
+    ]
+    for copy in copies:
+        copy.start()
+    for s in range(len(saved) // images):
+
+        @pl.when(plane == s)
+        def _():
+            for m in range(images):
+                pltpu.make_async_copy(saved[s * images + m], zbuf.at[m], zsems.at[m]).start()
+
+    embedded = embedded_ref[...]
+    width = embedded.shape[1]
+    squares = jnp.sum(embedded * embedded, axis=1, keepdims=True) / width
+    factor = lax.rsqrt(squares + tiny_value) / math.sqrt(width)
+    total = sums_ref[:, width : width + 1]
+    grad_unit = scale_value * (sums_ref[:, :width] / total - chosen_ref[...].astype(jnp.float32))
+    inner = jnp.sum(embedded * grad_unit, axis=1, keepdims=True)
+    grad_embed = factor * (grad_unit - embedded * inner / (width * (squares + tiny_value)))
+    grad_pooled = lax.dot_general(
+        grad_embed.astype(jnp.bfloat16),
+        embed_ref[...],
+        (((1,), (1,)), ((), ())),
+        preferred_element_type=jnp.float32,
+    )
+    for m in range(images):
+        g_ref[m] = (grad_pooled[m : m + 1] * pool_ref[...]).astype(jnp.bfloat16)
+    for copy in copies:
+        copy.wait()
+    for m in range(images):
+        pltpu.make_async_copy(saved[m], zbuf.at[m], zsems.at[m]).wait()
+
+
+def tail(flag, sums, chosen, embedded, embed_weight, pool_weight, weights, saved):
+    images = sums.shape[0]
+    return pl.pallas_call(
+        tail_body,
+        in_specs=[SM, VM, VM, VM, VM, VM] + [HB] * (len(weights) + len(saved)),
+        out_specs=[VM, VM, VM],
+        out_shape=[
+            jax.ShapeDtypeStruct((images, ROWS, C), jnp.bfloat16),
+            jax.ShapeDtypeStruct((2, 2, *weights[0].shape), weights[0].dtype),
+            jax.ShapeDtypeStruct((images, 2, ROWS, C), jnp.bfloat16),
+        ],
+        scratch_shapes=[pltpu.SemaphoreType.DMA((2, 2)), pltpu.SemaphoreType.DMA((images,))],
+        compiler_params=pltpu.CompilerParams(vmem_limit_bytes=STAGE_LIMIT),
+        cost_estimate=pl.CostEstimate(flops=300_000_000, bytes_accessed=9_000_000, transcendentals=0),
+        name="tail",
+    )(flag, sums, chosen, embedded, embed_weight, pool_weight, *in_hbm(*weights), *in_hbm(*saved))
 
 
 def in_hbm(*arrays):
@@ -150,14 +209,14 @@
 def load_weights(core, weights, name, before=()):
     return pl.pallas_call(
         load_body,
-        in_specs=[SM, HB, HB, HB, HB] + [pl.BlockSpec(memory_space=pl.ANY)] * len(before),
+        in_specs=[SM, HB, HB, AN, AN] + [AN] * len(before),
         out_specs=VM,
         out_shape=jax.ShapeDtypeStruct((2, 2, *weights[0].shape), weights[0].dtype),
         scratch_shapes=[pltpu.SemaphoreType.DMA((2, 2))],
         compiler_params=pltpu.CompilerParams(vmem_limit_bytes=STAGE_LIMIT),
         cost_estimate=pl.CostEstimate(flops=300_000_000, bytes_accessed=9_000_000, transcendentals=0),
         name=name,
-    )(core, *in_hbm(*weights), *before)
+    )(core, *in_hbm(*weights[:2]), *weights[2:], *before)
 
 
 def forward_stage(flag, x, held, vec):
@@ -176,21 +235,21 @@
     )(flag, x, held, vec)
 
 
-def backward_stage(flag, g, held, vec, z, store):
+def backward_stage(image, flag, g, held, vec, z, store):
     return pl.pallas_call(
-        backward_body,
-        in_specs=[SM, VM, VM, VM, HB, VM],
+        functools.partial(backward_body, image),
+        in_specs=[SM, VM, VM, VM, VM, VM],
         out_specs=[VM, VM],
         out_shape=[
             jax.ShapeDtypeStruct(g.shape, jnp.bfloat16),
             jax.ShapeDtypeStruct(store.shape, store.dtype),
         ],
-        scratch_shapes=STAGE_SCRATCH,
+        scratch_shapes=STAGE_SCRATCH[:2],
         input_output_aliases={5: 1},
         compiler_params=pltpu.CompilerParams(vmem_limit_bytes=STAGE_LIMIT),
         cost_estimate=CONV_COST,
         name="backward_stage",
-    )(flag, g, held, vec, *in_hbm(z), store)
+    )(flag, g, held, vec, z, store)
 
 
 def flip_body(*refs):
@@ -282,11 +341,26 @@
     pool_weight = widened(depthwise)[0].astype(jnp.float32)
     pooled = jnp.sum(x.astype(jnp.float32) * pool_weight[None], axis=1).astype(jnp.bfloat16)
     embedded = jnp.dot(pooled, embed_weight, preferred_element_type=jnp.float32)
-    normed, squares, factor = unit_scale(embedded)
-    sent = jnp.broadcast_to(normed.astype(jnp.bfloat16)[None], (shards, *normed.shape))
-    unit_half = lax.all_to_all(sent, "shard", 0, 0, tiled=True).reshape(shards * micro, -1)
-    centres_unit = unit_scale(class_centers.astype(jnp.float32))[0].astype(jnp.bfloat16)
+    normed = unit_scale(embedded)[0]
+    width = embedded.shape[-1]
     my_labels = lax.dynamic_slice_in_dim(labels, core * micro, micro, 0).T.reshape(-1)
+
+    def scaled_centres():
+        return unit_scale(class_centers.astype(jnp.float32))[0].astype(jnp.bfloat16)
+
+    def label_rows():
+        hits = my_labels[:, None] == class_ids[None, :]
+        rows = jnp.dot(
+            hits.astype(jnp.bfloat16), scaled_centres(), preferred_element_type=jnp.float32
+        ).astype(jnp.bfloat16)
+        rows = lax.all_to_all(rows.reshape(shards, micro, width), "shard", 0, 0, tiled=True)
+        return jnp.sum(rows.astype(jnp.float32), axis=0).astype(jnp.bfloat16)
+
+    chosen = lax.cond(plane == 0, label_rows, lambda: jnp.zeros((micro, width), jnp.bfloat16))
+    chosen = lax.ppermute(chosen, "section", [(c, sections - 2 + c) for c in range(2)])
+    sent = jnp.broadcast_to(normed.astype(jnp.bfloat16)[None], (shards, micro, width))
+    unit_half = lax.all_to_all(sent, "shard", 0, 0, tiled=True).reshape(shards * micro, width)
+    centres_unit = scaled_centres()
     label_hits = my_labels[:, None] == class_ids[None, :]
     cosines = lax.dot_general(
         unit_half, centres_unit, (((1,), (1,)), ((), ())), preferred_element_type=jnp.float32
@@ -296,34 +370,19 @@
     weighted = jnp.dot(
         exp_logits.astype(jnp.bfloat16), centres_unit, preferred_element_type=jnp.float32
     )
-    chosen = jnp.dot(
-        label_hits.astype(jnp.bfloat16), centres_unit, preferred_element_type=jnp.float32
-    )
     totals = jnp.sum(exp_logits, axis=1, keepdims=True)
-    sums = jnp.concatenate([weighted, chosen, totals], axis=1).astype(jnp.bfloat16)
+    sums = jnp.concatenate([weighted, totals], axis=1).astype(jnp.bfloat16)
     sums = lax.all_to_all(sums.reshape(shards, micro, -1), "shard", 0, 0, tiled=True)
     sums = jnp.sum(sums.astype(jnp.float32), axis=0)
-    width = embedded.shape[-1]
-    grad_unit = scale_value * (
-        sums[:, :width] / sums[:, 2 * width :] - sums[:, width : 2 * width]
-    )
-    inner = jnp.sum(embedded * grad_unit, axis=-1, keepdims=True)
-    grad_embed = factor * (grad_unit - embedded * inner / (width * (squares + tiny_value)))
-    grad_pooled = lax.dot_general(
-        grad_embed.astype(jnp.bfloat16),
-        embed_weight,
-        (((1,), (1,)), ((), ())),
-        preferred_element_type=jnp.float32,
-    )
-    g = (grad_pooled[:, None, :] * pool_weight[None]).astype(jnp.bfloat16)
-
-    flips, g = lax.optimization_barrier((flips, g))
-    flips = load_weights(core.reshape(1), flips, "load_backward")
+    g, flips, zbuf = tail(
+        jnp.stack([core, plane]), sums, chosen, embedded, embed_weight, pool_weight, flips,
+        [saved[s, m] for s in range(planes) for m in range(micro)],
+    )
     parts = [g[m : m + 1] for m in range(micro)]
     stores = [jnp.zeros((2, ROWS, C), jnp.bfloat16) for m in range(micro)]
     for s in reversed(range(planes)):
         for m in range(micro):
-            parts[m], stores[m] = backward_stage(flags[s], parts[m], flips, vec, saved[s, m], stores[m])
+            parts[m], stores[m] = backward_stage(m, flags[s], parts[m], flips, vec, zbuf, stores[m])
             if s > 0:
                 parts[m] = lax.ppermute(parts[m], "section", [(2 * s + c, 2 * s - 2 + c) for c in range(2)])
     store = jnp.stack(stores, axis=1)

time: 149 us -> 146 us (0.980)
  blocking collectives: 0 us -> 27.1 us
  waiting for transfers between devices: 55 us -> 35 us
  starting transfers between devices: 53.5 us -> 45.4 us
    all_to_all x0 -> x1, blocking collectives: none -> 27.1 us  [label_rows(): lax.all_to_all(rows.reshape(shards, micro, width), 'shard', 0, 0, tiled=T...]
    ppermute x6, waiting for transfers between devices: 28 us -> 13.6 us  [on_device(): lax.ppermute(parts[m], 'section', [(2 * s + c, 2 * s - 2 + c) for c in ra...]
    all_to_all x1, waiting for transfers between devices: 11.4 us -> 5.08 us  [on_device(): lax.all_to_all(sums.reshape(shards, micro, -1), 'shard', 0, 0, tiled=True)]
    all_to_all x1, starting transfers between devices: 13.1 us -> 7.27 us  [on_device(): lax.all_to_all(sent, 'shard', 0, 0, tiled=True)]
    ppermute x1, starting transfers between devices: 9.39 us -> 5.67 us  [on_device(): taken = lax.ppermute(given, 'section', swap)]
  transfers between devices with their start and end apart: 18 -> 19, of which waited for: 6 -> 6; matrix products, arithmetic and copies ran while one was open for 3% -> 2% of each run, Pallas kernels for 10% -> 10%
where the time goes in v4:
time: 146 us; the launch traced here: 145 us
  starting transfers between devices  45.4 us (31%)
  waiting for transfers between devices  35 us (24%)
  blocking collectives  27.1 us (19%)
  Pallas kernels  24.6 us (17%)
  other arithmetic  5.27 us (4%)
  local copies, waits for them, and re-layouts  3.75 us (3%)
  matrix products  2.42 us (2%)
    all_to_all x1, blocking collectives, label_rows(): lax.all_to_all(rows.reshape(shards, micro, width), 'shard', 0, 0, tiled=T...  27.1 us
    ppermute x6, waiting for transfers between devices, on_device(): lax.ppermute(parts[m], 'section', [(2 * s + c, 2 * s - 2 + c) for c in ra...  13.6 us
    all_to_all x1, waiting for transfers between devices, on_device(): lax.all_to_all(sent, 'shard', 0, 0, tiled=True)  13.4 us
    ppermute x2, starting transfers between devices, on_device(): peer = tuple((lax.ppermute(w, 'section', swap) for w in own))  10.8 us
    pallas_call x1, Pallas kernels, flip_all(): pl.pallas_call(flip_body, grid=(9,), in_specs=[pl.BlockSpec((C, C), lambd...  8.48 us
    all_to_all x1, starting transfers between devices, on_device(): lax.all_to_all(sums.reshape(shards, micro, -1), 'shard', 0, 0, tiled=True)  7.44 us
    all_to_all x1, starting transfers between devices, on_device(): lax.all_to_all(sent, 'shard', 0, 0, tiled=True)  7.27 us
    ppermute x1, starting transfers between devices, on_device(): taken = lax.ppermute(given, 'section', swap)  5.67 us
  transfers between devices with their start and end apart: 19, of which 6 were waited for; matrix products, arithmetic and copies ran while one was open for 2% of the time, Pallas kernels for 10%

profile of v4, /device:TPU:1, one launch (start us, length us, event | category | flops | bytes accessed | tf_op | source)
XLA Modules:
  0.0 144.9 jit_solution(2895127072469345902)
XLA Ops:
  0.0 8.9 %collective-permute-start = (bf16[2304,256]{1,0:T(8,128)(2,1)}, bf16[2304,256]{1,0:T(8,128)(2,1)S(1)}, u32[]{:S(2)}, u32[]{:S(2)}) collective-permute-start(bf16[2304,256]{1,0:T(8,128)(2,1)} %bitcast.44), channel_id=1, source_target_pairs={{0,64},{64,0},{128,192},{192,128},{256,320},{320,256},{384,448},{4... | collective-permute-start | bytes 3538952 | tf_op jit(solution)/shard_map/ppermute | solution.py:315
  8.9 1.9 %collective-permute-start.1 = (bf16[2304,256]{1,0:T(8,128)(2,1)}, bf16[2304,256]{1,0:T(8,128)(2,1)S(1)}, u32[]{:S(2)}, u32[]{:S(2)}) collective-permute-start(bf16[2304,256]{1,0:T(8,128)(2,1)} %bitcast.47), channel_id=1, source_target_pairs={{0,64},{64,0},{128,192},{192,128},{256,320},{320,256},{384,448},{4... | collective-permute-start | bytes 3538952 | tf_op jit(solution)/shard_map/ppermute | solution.py:315
  10.8 0.7 pad_maximum_fusion.2
  11.5 2.4 %collective-permute-start.2 = (f32[3,256]{1,0:T(4,128)S(1)}, f32[3,256]{1,0:T(4,128)S(1)}, u32[]{:S(2)}, u32[]{:S(2)}) collective-permute-start(f32[3,256]{1,0:T(4,128)S(1)} %pad_maximum_fusion.2), channel_id=1, source_target_pairs={{0,64},{64,0},{128,192},{192,128},{256,320},{320,256},{384,448},{4... | collective-permute-start | bytes 9224 | tf_op jit(solution)/shard_map/ppermute | solution.py:309
  14.6 0.2 constant_dynamic-slice_fusion
  14.9 0.5 pad_slice_fusion.1
  15.3 0.7 bitcast_dynamic-update-slice_fusion.1
  16.2 2.5 %load_forward.1.held = bf16[2,2,2304,256]{3,2,1,0:T(8,128)(2,1)S(1)} custom-call(s32[1]{0:T(128)} %bitcast.4.flag, bf16[2304,256]{1,0:T(8,128)(2,1)} %bitcast.45, bf16[2304,256]{1,0:T(8,128)(2,1)} %bitcast.48, bf16[2304,256]{1,0:T(8,128)(2,1)S(1)} %collective-permute-done.peer1.refs_2_, bf16[2304,256]{1,0:T(8,128)(2,1)S(1)} %collective-permute-done.1.peer2.refs_3_, ...), custom_call_target="tpu_custom_call" | custom-call | flops 300000000 | bytes 9000000 | tf_op jit(solution)/shard_map/load_forward/pallas_call | solution.py:210
  18.8 2.4 %forward_stage.8 = (bf16[1,224,256]{2,1,0:T(8,128)(2,1)S(1)}, bf16[2,224,256]{2,1,0:T(8,128)(2,1)}) custom-call(s32[1]{0:T(128)} %bitcast.rest_3_.flag, bf16[1,224,256]{2,1,0:T(8,128)(2,1)S(1)} %bitcast.43, bf16[2,2,2304,256]{3,2,1,0:T(8,128)(2,1)S(1)} %load_forward.1.held, f32[2,3,256]{2,1,0:T(4,128)S(1)} %bitcast_dynamic-update-slice_fusion.vec_ref), custom_call_target="tpu_custom_call" | custom-call | flops 1056964608 | bytes 6000000 | tf_op jit(solution)/shard_map/forward_stage/pallas_call | solution.py:223
  21.2 1.3 collective-permute-start.3
  22.5 2.4 %forward_stage.12 = (bf16[1,224,256]{2,1,0:T(8,128)(2,1)S(1)}, bf16[2,224,256]{2,1,0:T(8,128)(2,1)}) custom-call(s32[1]{0:T(128)} %bitcast.rest_3_.flag, bf16[1,224,256]{2,1,0:T(8,128)(2,1)S(1)} %bitcast.41, bf16[2,2,2304,256]{3,2,1,0:T(8,128)(2,1)S(1)} %load_forward.1.held, f32[2,3,256]{2,1,0:T(4,128)S(1)} %bitcast_dynamic-update-slice_fusion.vec_ref), custom_call_target="tpu_custom_call" | custom-call | flops 1056964608 | bytes 6000000 | tf_op jit(solution)/shard_map/forward_stage/pallas_call | solution.py:223
  24.9 1.3 collective-permute-start.6
  26.2 0.7 collective-permute-start.4
  26.9 2.0 %collective-permute-done.6.x_ref = bf16[1,224,256]{2,1,0:T(8,128)(2,1)S(1)} collective-permute-done((bf16[1,224,256]{2,1,0:T(8,128)(2,1)S(1)}, bf16[1,224,256]{2,1,0:T(8,128)(2,1)S(1)}, u32[]{:S(2)}, u32[]{:S(2)}) %collective-permute-start.6) | collective-permute-done | bytes 114720 | tf_op jit(solution)/shard_map/ppermute | solution.py:336
  29.0 0.7 collective-permute-start.7
  29.7 0.7 collective-permute-start.5
  30.4 0.7 collective-permute-start.8
  31.2 0.6 copy-done.6
  31.8 0.1 copy.27
  31.9 0.1 dynamic-slice_bitcast_fusion
  32.1 0.1 multiply_reduce_fusion
  32.2 0.3 multiply_reduce_fusion.1
  32.5 0.3 copy-done.4
  32.8 28.5 %conditional.1 = (bf16[2,512]{1,0:T(2,128)(2,1)S(1)}) conditional(s32[]{:T(128)} %convert_element_type.52, () %tuple.13, (s32[64,2]{1,0:T(8,128)S(1)}, s32[1664]{0:T(1024)S(1)}, bf16[1664,512]{1,0:T(8,128)(2,1)S(1)}) %tuple.24), branch_computations={%region_5.6_spmd, %region_6.9_spmd} | conditional | flops 223561984 | bytes 4231178 | solution.py:359
  32.8 0.4 fusion
  33.2 0.1 eq.9
  33.3 0.6 fusion.5
  33.9 0.1 reshape.86
  34.0 27.1 %all_to_all.14 = bf16[64,2,512]{2,1,0:T(2,128)(2,1)S(1)} all-to-all(bf16[64,2,512]{2,1,0:T(2,128)(2,1)S(1)} %reshape.86), channel_id=1, replica_groups=mesh['section'=8,'shard'=64] {'shard'}, dimensions={0} | all-to-all | bytes 262144 | tf_op jit(solution)/shard_map/cond/branch_1_fun/all_to_all | solution.py:356
  61.1 0.1 reduce_sum.60
  61.3 0.1 multiply_convert_fusion
  61.3 0.7 broadcast_in_dim.29
  62.1 7.3 %all-to-all-start.1 = ((bf16[64,2,512]{2,1,0:T(2,128)(2,1)}), bf16[64,2,512]{2,1,0:T(2,128)(2,1)S(1)}, u32[]{:S(2)}, u32[]{:S(2)}) async-start(bf16[64,2,512]{2,1,0:T(2,128)(2,1)} %broadcast_in_dim.29), calls=%async_computation.1 | async-start | bytes 262144 | tf_op jit(solution)/shard_map/all_to_all | solution.py:362
  69.3 0.1 eq.54
  69.5 0.4 fusion.11
  69.9 13.4 %all-to-all-done.1 = bf16[64,2,512]{2,1,0:T(2,128)(2,1)S(1)} async-done(((bf16[64,2,512]{2,1,0:T(2,128)(2,1)}), bf16[64,2,512]{2,1,0:T(2,128)(2,1)S(1)}, u32[]{:S(2)}, u32[]{:S(2)}) %all-to-all-start.1) | async-done | bytes 131104 | tf_op jit(solution)/shard_map/all_to_all | solution.py:362
  83.4 1.0 fusion.23
  84.4 0.5 convolution_convert_fusion
  84.9 0.1 concatenate.20
  85.0 0.2 concatenate.24
  85.2 0.8 pad_maximum_fusion.1
  86.1 7.4 %all-to-all-start.2 = ((bf16[64,2,513]{2,1,0:T(2,128)(2,1)}), bf16[64,2,513]{2,1,0:T(2,128)(2,1)S(1)}, u32[]{:S(2)}, u32[]{:S(2)}) async-start(bf16[64,2,513]{2,1,0:T(2,128)(2,1)} %pad_maximum_fusion.1), calls=%async_computation.2 | async-start | bytes 327680 | tf_op jit(solution)/shard_map/all_to_all | solution.py:375
  93.5 0.1 pad_add_fusion.flag
  93.6 8.5 %flip_all.1 = (bf16[2304,256]{1,0:T(8,128)(2,1)}, bf16[2304,256]{1,0:T(8,128)(2,1)}, bf16[2304,256]{1,0:T(8,128)(2,1)}, bf16[2304,256]{1,0:T(8,128)(2,1)}) custom-call(bf16[2304,256]{1,0:T(8,128)(2,1)} %bitcast.46, bf16[2304,256]{1,0:T(8,128)(2,1)} %bitcast.49, bf16[2304,256]{1,0:T(8,128)(2,1)} %copy-done.1, bf16[2304,256]{1,0:T(8,128)(2,1)} %copy-done.2), custom_call_target="tpu_custom_call" | custom-call | flops 1207959552 | bytes 9000000 | tf_op jit(solution)/shard_map/flip_all/pallas_call | solution.py:269
  102.1 1.3 collective-permute-start.9
  103.4 5.1 %all-to-all-done.2 = bf16[64,2,513]{2,1,0:T(2,128)(2,1)S(1)} async-done(((bf16[64,2,513]{2,1,0:T(2,128)(2,1)}), bf16[64,2,513]{2,1,0:T(2,128)(2,1)S(1)}, u32[]{:S(2)}, u32[]{:S(2)}) %all-to-all-start.2) | async-done | bytes 131360 | tf_op jit(solution)/shard_map/all_to_all | solution.py:375
  108.4 0.2 convert_reduce_fusion.sums_ref
  108.6 3.2 %tail.1 = (bf16[2,224,256]{2,1,0:T(8,128)(2,1)S(1)}, bf16[2,2,2304,256]{3,2,1,0:T(8,128)(2,1)S(1)}, bf16[2,2,224,256]{3,2,1,0:T(8,128)(2,1)S(1)}) custom-call(s32[2]{0:T(128)S(1)} %pad_add_fusion.flag, f32[2,513]{1,0:T(2,128)S(1)} %convert_reduce_fusion.sums_ref, bf16[2,512]{1,0:T(2,128)(2,1)S(1)} %collective-permute-done.9.chosen_ref, ...), custom_call_target="tpu_custom_call" | custom-call | flops 300000000 | bytes 9000000 | tf_op jit(solution)/shard_map/tail/pallas_call | solution.py:179
  111.9 0.7 collective-permute-start.13
  112.6 0.7 collective-permute-start.10
  113.3 0.7 collective-permute-start.14
  114.0 0.7 collective-permute-start.11
  114.7 1.3 collective-permute-start.15
  116.1 1.3 collective-permute-start.12
  117.4 10.2 %collective-permute-done.15.g_ref = bf16[1,224,256]{2,1,0:T(8,128)(2,1)S(1)} collective-permute-done((bf16[1,224,256]{2,1,0:T(8,128)(2,1)S(1)}, bf16[1,224,256]{2,1,0:T(8,128)(2,1)S(1)}, u32[]{:S(2)}, u32[]{:S(2)}) %collective-permute-start.15) | collective-permute-done | bytes 114720 | tf_op jit(solution)/shard_map/ppermute | solution.py:387
  127.5 2.7 %backward_stage.15 = (bf16[1,224,256]{2,1,0:T(8,128)(2,1)}, bf16[2,224,256]{2,1,0:T(8,128)(2,1)S(1)}) custom-call(s32[1]{0:T(128)} %bitcast.rest_3_.flag, bf16[1,224,256]{2,1,0:T(8,128)(2,1)S(1)} %collective-permute-done.15.g_ref, bf16[2,2,2304,256]{3,2,1,0:T(8,128)(2,1)S(1)} %get-tuple-element.85.held, ...), custom_call_target="tpu_custom_call", output_to_operand_aliasing={{1}: (5, {})} | custom-call | flops 1056964608 | bytes 6000000 | tf_op jit(solution)/shard_map/backward_stage/pallas_call | solution.py:239
  130.2 3.5 %collective-permute-done.12.g_ref = bf16[1,224,256]{2,1,0:T(8,128)(2,1)S(1)} collective-permute-done((bf16[1,224,256]{2,1,0:T(8,128)(2,1)S(1)}, bf16[1,224,256]{2,1,0:T(8,128)(2,1)S(1)}, u32[]{:S(2)}, u32[]{:S(2)}) %collective-permute-start.12) | collective-permute-done | bytes 114720 | tf_op jit(solution)/shard_map/ppermute | solution.py:387
  133.7 2.7 %backward_stage.11 = (bf16[1,224,256]{2,1,0:T(8,128)(2,1)}, bf16[2,224,256]{2,1,0:T(8,128)(2,1)S(1)}) custom-call(s32[1]{0:T(128)} %bitcast.rest_3_.flag, bf16[1,224,256]{2,1,0:T(8,128)(2,1)S(1)} %collective-permute-done.12.g_ref, bf16[2,2,2304,256]{3,2,1,0:T(8,128)(2,1)S(1)} %get-tuple-element.85.held, ...), custom_call_target="tpu_custom_call", output_to_operand_aliasing={{1}: (5, {})} | custom-call | flops 1056964608 | bytes 6000000 | tf_op jit(solution)/shard_map/backward_stage/pallas_call | solution.py:239
  136.4 0.2 copy.30
  136.7 5.7 %collective-permute-start.16 = (bf16[2,196,256]{2,0,1:T(2,128)(2,1)S(1)}, bf16[2,196,256]{2,0,1:T(2,128)(2,1)S(1)}, u32[]{:S(2)}, u32[]{:S(2)}) collective-permute-start(bf16[2,196,256]{2,0,1:T(2,128)(2,1)S(1)} %bitcast.53), channel_id=1, source_target_pairs={{0,64},{64,0},{128,192},{192,128},{256,320},{320,256},{384,448},{4... | collective-permute-start | bytes 602120 | tf_op jit(solution)/shard_map/ppermute | solution.py:395
  142.3 0.2 copy.29
  142.6 0.8 collective-permute-done.16
  143.4 0.3 broadcast_select_fusion.1
  143.7 1.2 maximum_bitcast_fusion
  (54 shorter events, 0.7 us)
Async XLA Ops:
  0.0 14.6 %copy-start = (bf16[4,1,196,256]{3,0,2,1:T(4,128)(2,1)S(1)}, bf16[4,1,196,256]{3,0,2,1:T(4,128)(2,1)}, u32[]{:S(2)}) copy-start(bf16[4,1,196,256]{3,0,2,1:T(4,128)(2,1)} %param.13) | copy-start | bytes 1204228
  0.0 16.2 %collective-permute-start = (bf16[2304,256]{1,0:T(8,128)(2,1)}, bf16[2304,256]{1,0:T(8,128)(2,1)S(1)}, u32[]{:S(2)}, u32[]{:S(2)}) collective-permute-start(bf16[2304,256]{1,0:T(8,128)(2,1)} %bitcast.44), channel_id=1, source_target_pairs={{0,64},{64,0},{128,192},{192,128},{256,320},{320,256},{384,448},{4... | collective-permute-start | bytes 3538952 | tf_op jit(solution)/shard_map/ppermute | solution.py:315
  8.9 7.3 %collective-permute-start.1 = (bf16[2304,256]{1,0:T(8,128)(2,1)}, bf16[2304,256]{1,0:T(8,128)(2,1)S(1)}, u32[]{:S(2)}, u32[]{:S(2)}) collective-permute-start(bf16[2304,256]{1,0:T(8,128)(2,1)} %bitcast.47), channel_id=1, source_target_pairs={{0,64},{64,0},{128,192},{192,128},{256,320},{320,256},{384,448},{4... | collective-permute-start | bytes 3538952 | tf_op jit(solution)/shard_map/ppermute | solution.py:315
  11.5 4.6 %collective-permute-start.2 = (f32[3,256]{1,0:T(4,128)S(1)}, f32[3,256]{1,0:T(4,128)S(1)}, u32[]{:S(2)}, u32[]{:S(2)}) collective-permute-start(f32[3,256]{1,0:T(4,128)S(1)} %pad_maximum_fusion.2), channel_id=1, source_target_pairs={{0,64},{64,0},{128,192},{192,128},{256,320},{320,256},{384,448},{4... | collective-permute-start | bytes 9224 | tf_op jit(solution)/shard_map/ppermute | solution.py:309
  16.2 2.5 %copy-start.1 = (bf16[2304,256]{1,0:T(8,128)(2,1)}, bf16[2304,256]{1,0:T(8,128)(2,1)S(1)}, u32[]{:S(2)}) copy-start(bf16[2304,256]{1,0:T(8,128)(2,1)S(1)} %collective-permute-done.peer1.refs_2_) | copy-start | bytes 3538948
  16.2 2.5 %copy-start.2 = (bf16[2304,256]{1,0:T(8,128)(2,1)}, bf16[2304,256]{1,0:T(8,128)(2,1)S(1)}, u32[]{:S(2)}) copy-start(bf16[2304,256]{1,0:T(8,128)(2,1)S(1)} %collective-permute-done.1.peer2.refs_3_) | copy-start | bytes 3538948
  21.2 5.0 %collective-permute-start.3 = (bf16[1,224,256]{2,1,0:T(8,128)(2,1)S(1)}, bf16[1,224,256]{2,1,0:T(8,128)(2,1)S(1)}, u32[]{:S(2)}, u32[]{:S(2)}) collective-permute-start(bf16[1,224,256]{2,1,0:T(8,128)(2,1)S(1)} %get-tuple-element.59), channel_id=1, source_target_pairs={{0,128},{64,192},{1,129},{65,193},{2,130},{66,194},{3,131},{67,195... | collective-permute-start | bytes 344072 | tf_op jit(solution)/shard_map/ppermute | solution.py:336
  24.9 4.0 %collective-permute-start.6 = (bf16[1,224,256]{2,1,0:T(8,128)(2,1)S(1)}, bf16[1,224,256]{2,1,0:T(8,128)(2,1)S(1)}, u32[]{:S(2)}, u32[]{:S(2)}) collective-permute-start(bf16[1,224,256]{2,1,0:T(8,128)(2,1)S(1)} %get-tuple-element.63), channel_id=1, source_target_pairs={{0,128},{64,192},{1,129},{65,193},{2,130},{66,194},{3,131},{67,195... | collective-permute-start | bytes 344072 | tf_op jit(solution)/shard_map/ppermute | solution.py:336
  26.2 3.4 %collective-permute-start.4 = (bf16[1,224,256]{2,1,0:T(8,128)(2,1)S(1)}, bf16[1,224,256]{2,1,0:T(8,128)(2,1)S(1)}, u32[]{:S(2)}, u32[]{:S(2)}) collective-permute-start(bf16[1,224,256]{2,1,0:T(8,128)(2,1)S(1)} %get-tuple-element.60), channel_id=1, source_target_pairs={{128,256},{192,320},{129,257},{193,321},{130,258},{194,322},{131,2... | collective-permute-start | bytes 344072 | tf_op jit(solution)/shard_map/ppermute | solution.py:336
  29.0 1.4 collective-permute-start.7
  29.7 1.4 collective-permute-start.5
  30.4 0.7 collective-permute-start.8
  31.1 0.7 copy-start.6
  31.1 0.9 copy-start.5
  31.2 1.0 copy-start.3
  31.2 1.6 %copy-start.4 = (bf16[1664,512]{1,0:T(8,128)(2,1)S(1)}, bf16[1664,512]{1,0:T(8,128)(2,1)}, u32[]{:S(2)}) copy-start(bf16[1664,512]{1,0:T(8,128)(2,1)} %param.21) | copy-start | bytes 5111812
  62.1 21.2 %all-to-all-start.1 = ((bf16[64,2,512]{2,1,0:T(2,128)(2,1)}), bf16[64,2,512]{2,1,0:T(2,128)(2,1)S(1)}, u32[]{:S(2)}, u32[]{:S(2)}) async-start(bf16[64,2,512]{2,1,0:T(2,128)(2,1)} %broadcast_in_dim.29), calls=%async_computation.1 | async-start | bytes 262144 | tf_op jit(solution)/shard_map/all_to_all | solution.py:362
  86.1 22.4 %all-to-all-start.2 = ((bf16[64,2,513]{2,1,0:T(2,128)(2,1)}), bf16[64,2,513]{2,1,0:T(2,128)(2,1)S(1)}, u32[]{:S(2)}, u32[]{:S(2)}) async-start(bf16[64,2,513]{2,1,0:T(2,128)(2,1)} %pad_maximum_fusion.1), calls=%async_computation.2 | async-start | bytes 327680 | tf_op jit(solution)/shard_map/all_to_all | solution.py:375
  102.1 6.5 %collective-permute-start.9 = (bf16[2,512]{1,0:T(2,128)(2,1)S(1)}, bf16[2,512]{1,0:T(2,128)(2,1)S(1)}, u32[]{:S(2)}, u32[]{:S(2)}) collective-permute-start(bf16[2,512]{1,0:T(2,128)(2,1)S(1)} %get-tuple-element.115), channel_id=1, source_target_pairs={{0,384},{64,448},{1,385},{65,449},{2,386},{66,450},{3,387},{67,451... | collective-permute-start | bytes 6152 | tf_op jit(solution)/shard_map/ppermute | solution.py:360
  111.9 1.4 collective-permute-start.13
  112.6 1.4 collective-permute-start.10
  113.3 1.4 collective-permute-start.14
  114.0 2.0 %collective-permute-start.11 = (bf16[1,224,256]{2,1,0:T(8,128)(2,1)S(1)}, bf16[1,224,256]{2,1,0:T(8,128)(2,1)S(1)}, u32[]{:S(2)}, u32[]{:S(2)}) collective-permute-start(bf16[1,224,256]{2,1,0:T(8,128)(2,1)S(1)} %get-tuple-element.89), channel_id=1, source_target_pairs={{256,128},{320,192},{257,129},{321,193},{258,130},{322,194},{259,1... | collective-permute-start | bytes 344072 | tf_op jit(solution)/shard_map/ppermute | solution.py:387
  114.7 12.8 %collective-permute-start.15 = (bf16[1,224,256]{2,1,0:T(8,128)(2,1)S(1)}, bf16[1,224,256]{2,1,0:T(8,128)(2,1)S(1)}, u32[]{:S(2)}, u32[]{:S(2)}) collective-permute-start(bf16[1,224,256]{2,1,0:T(8,128)(2,1)S(1)} %get-tuple-element.98), channel_id=1, source_target_pairs={{128,0},{192,64},{129,1},{193,65},{130,2},{194,66},{131,3},{195,67... | collective-permute-start | bytes 344072 | tf_op jit(solution)/shard_map/ppermute | solution.py:387
  116.1 17.6 %collective-permute-start.12 = (bf16[1,224,256]{2,1,0:T(8,128)(2,1)S(1)}, bf16[1,224,256]{2,1,0:T(8,128)(2,1)S(1)}, u32[]{:S(2)}, u32[]{:S(2)}) collective-permute-start(bf16[1,224,256]{2,1,0:T(8,128)(2,1)S(1)} %get-tuple-element.91), channel_id=1, source_target_pairs={{128,0},{192,64},{129,1},{193,65},{130,2},{194,66},{131,3},{195,67... | collective-permute-start | bytes 344072 | tf_op jit(solution)/shard_map/ppermute | solution.py:387
  136.7 6.7 %collective-permute-start.16 = (bf16[2,196,256]{2,0,1:T(2,128)(2,1)S(1)}, bf16[2,196,256]{2,0,1:T(2,128)(2,1)S(1)}, u32[]{:S(2)}, u32[]{:S(2)}) collective-permute-start(bf16[2,196,256]{2,0,1:T(2,128)(2,1)S(1)} %bitcast.53), channel_id=1, source_target_pairs={{0,64},{64,0},{128,192},{192,128},{256,320},{320,256},{384,448},{4... | collective-permute-start | bytes 602120 | tf_op jit(solution)/shard_map/ppermute | solution.py:395

commit v5 on v4

--- a/solution.py
+++ b/solution.py
@@ -59,16 +59,74 @@
 HALVES = tuple(slice(h * HALF, (h + 1) * HALF) for h in range(2))
 
 
-def load_body(flag, own1, own2, peer1, peer2, *rest):
-    held, sems = rest[-2:]
-    for k, source in enumerate((own1, own2)):
-        pltpu.make_async_copy(source, held.at[flag[0], k], sems.at[0, k]).start()
-    for k, source in enumerate((peer1, peer2)):
-        pltpu.make_async_copy(source, held.at[1 - flag[0], k], sems.at[1, k]).start()
-    for k, source in enumerate((own1, own2)):
-        pltpu.make_async_copy(source, held.at[flag[0], k], sems.at[0, k]).wait()
-    for k, source in enumerate((peer1, peer2)):
-        pltpu.make_async_copy(source, held.at[1 - flag[0], k], sems.at[1, k]).wait()
+def load_body(flag, own1, own2, peer1, peer2, own_vec, peer_vec, pool, embed, *rest):
+    held, vec, pool_out, embed_out, sems, more = rest[-6:]
+    core = flag[0]
+    copies = [
+        pltpu.make_async_copy(source, held.at[place, k], sems.at[side, k])
+        for side, place, pair in ((0, core, (own1, own2)), (1, 1 - core, (peer1, peer2)))
+        for k, source in enumerate(pair)
+    ] + [
+        pltpu.make_async_copy(pool, pool_out, more.at[0]),
+        pltpu.make_async_copy(embed, embed_out, more.at[1]),
+    ]
+    for copy in copies:
+        copy.start()
+    vec[core] = own_vec[...]
+    vec[1 - core] = peer_vec[...]
+    for copy in copies:
+        copy.wait()
+
+
+def pool_body(first, second, pool_ref, embed_ref, embedded_ref, sent_ref):
+    pooled = []
+    for image in (first, second):
+        total = jnp.zeros((SIDE, C), jnp.float32)
+        for i in range(SIDE):
+            rows = image[0, WIDE * i : WIDE * i + SIDE, :].astype(jnp.float32)
+            total += rows * pool_ref[SIDE * i : SIDE * i + SIDE, :].astype(jnp.float32)
+        pooled.append(jnp.sum(total, axis=0, keepdims=True))
+    pooled = jnp.concatenate(pooled, axis=0).astype(jnp.bfloat16)
+    embedded = jnp.dot(pooled, embed_ref[...], preferred_element_type=jnp.float32)
+    embedded_ref[...] = embedded
+    normed = unit_scale(embedded)[0].astype(jnp.bfloat16)
+    sent_ref[...] = jnp.broadcast_to(normed[None], sent_ref.shape)
+
+
+def pool_and_embed(parts, pool, embed, shards):
+    width = embed.shape[1]
+    return pl.pallas_call(
+        pool_body,
+        in_specs=[VM] * 4,
+        out_specs=[VM, VM],
+        out_shape=[
+            jax.ShapeDtypeStruct((2, width), jnp.float32),
+            jax.ShapeDtypeStruct((shards, 2, width), jnp.bfloat16),
+        ],
+        compiler_params=pltpu.CompilerParams(vmem_limit_bytes=STAGE_LIMIT),
+        cost_estimate=pl.CostEstimate(flops=100_000_000, bytes_accessed=1_000_000, transcendentals=0),
+        name="pool_and_embed",
+    )(*parts, pool, embed)
+
+
+def centres_body(centres_ref, after, out_ref):
+    values = centres_ref[...].astype(jnp.float32)
+    out_ref[...] = unit_scale(values)[0].astype(jnp.bfloat16)
+
+
+def unit_centres(centres, after):
+    rows, width = centres.shape
+    block = pl.BlockSpec((128, width), lambda i: (i, 0))
+    return pl.pallas_call(
+        centres_body,
+        grid=(rows // 128,),
+        in_specs=[block, AN],
+        out_specs=block,
+        out_shape=jax.ShapeDtypeStruct(centres.shape, jnp.bfloat16),
+        compiler_params=pltpu.CompilerParams(vmem_limit_bytes=STAGE_LIMIT),
+        cost_estimate=pl.CostEstimate(flops=100_000_000, bytes_accessed=3_000_000, transcendentals=0),
+        name="unit_centres",
+    )(*in_hbm(centres), after)
 
 
 def forward_body(flag, x_ref, held, vec_ref, out_ref, z_ref, cols, run, zed, zsem):
@@ -102,7 +160,9 @@
             pltpu.make_async_copy(zed.at[u], z_ref.at[u], zsem.at[u]).wait()
 
 
-def backward_body(image, flag, g_ref, held, vec_ref, z_ref, store_in, out_ref, store, cols, run):
+def backward_body(image, flag, g_ref, held, vec_ref, z_ref, store_in, *rest):
+    store, cols, run = rest[-3:]
+
     @pl.when(flag[0] == 1)
     def _():
         clear_border(cols)
@@ -129,7 +189,8 @@
             return carry
 
         lax.fori_loop(0, 2, one, 0)
-        out_ref[0] = run[...].astype(jnp.bfloat16)
+        if rest[0].ndim == 3:
+            rest[0][0] = run[...].astype(jnp.bfloat16)
 
 
 def tail_body(
@@ -206,17 +267,22 @@
 ]
 
 
-def load_weights(core, weights, name, before=()):
+def load_weights(core, weights, own_vec, peer_vec, pool, embed, before):
     return pl.pallas_call(
         load_body,
-        in_specs=[SM, HB, HB, AN, AN] + [AN] * len(before),
-        out_specs=VM,
-        out_shape=jax.ShapeDtypeStruct((2, 2, *weights[0].shape), weights[0].dtype),
-        scratch_shapes=[pltpu.SemaphoreType.DMA((2, 2))],
+        in_specs=[SM, HB, HB, AN, AN, VM, VM, HB, HB] + [AN] * len(before),
+        out_specs=[VM] * 4,
+        out_shape=[
+            jax.ShapeDtypeStruct((2, 2, *weights[0].shape), weights[0].dtype),
+            jax.ShapeDtypeStruct((2, *own_vec.shape), own_vec.dtype),
+            jax.ShapeDtypeStruct(pool.shape, pool.dtype),
+            jax.ShapeDtypeStruct(embed.shape, embed.dtype),
+        ],
+        scratch_shapes=[pltpu.SemaphoreType.DMA((2, 2)), pltpu.SemaphoreType.DMA((2,))],
         compiler_params=pltpu.CompilerParams(vmem_limit_bytes=STAGE_LIMIT),
         cost_estimate=pl.CostEstimate(flops=300_000_000, bytes_accessed=9_000_000, transcendentals=0),
-        name=name,
-    )(core, *in_hbm(*weights[:2]), *weights[2:], *before)
+        name="load_weights",
+    )(core, *in_hbm(*weights[:2]), *weights[2:], own_vec, peer_vec, *in_hbm(pool, embed), *before)
 
 
 def forward_stage(flag, x, held, vec):
@@ -235,21 +301,20 @@
     )(flag, x, held, vec)
 
 
-def backward_stage(image, flag, g, held, vec, z, store):
-    return pl.pallas_call(
+def backward_stage(image, last, flag, g, held, vec, z, store):
+    passed = [jax.ShapeDtypeStruct((16, 128) if last else g.shape, jnp.bfloat16)]
+    outs = pl.pallas_call(
         functools.partial(backward_body, image),
         in_specs=[SM, VM, VM, VM, VM, VM],
-        out_specs=[VM, VM],
-        out_shape=[
-            jax.ShapeDtypeStruct(g.shape, jnp.bfloat16),
-            jax.ShapeDtypeStruct(store.shape, store.dtype),
-        ],
+        out_specs=[VM] * (len(passed) + 1),
+        out_shape=passed + [jax.ShapeDtypeStruct(store.shape, store.dtype)],
         scratch_shapes=STAGE_SCRATCH[:2],
-        input_output_aliases={5: 1},
+        input_output_aliases={5: len(passed)},
         compiler_params=pltpu.CompilerParams(vmem_limit_bytes=STAGE_LIMIT),
         cost_estimate=CONV_COST,
         name="backward_stage",
     )(flag, g, held, vec, z, store)
+    return outs[0], outs[-1]
 
 
 def flip_body(*refs):
@@ -305,16 +370,11 @@
     core = section_index % 2
     swap = [(s, s ^ 1) for s in range(sections)]
 
-    def stacked(own):
-        peer = lax.ppermute(own, "section", swap)
-        both = jnp.zeros((2, *own.shape), own.dtype)
-        both = lax.dynamic_update_index_in_dim(both, own, core, 0)
-        return lax.dynamic_update_index_in_dim(both, peer, 1 - core, 0)
-
     own = (conv_one[0], conv_two[0])
     peer = tuple(lax.ppermute(w, "section", swap) for w in own)
     weights = (*own, *peer)
-    vec = stacked(jnp.concatenate([unit_gain, offset_bias, leak_slope], axis=0))
+    own_vec = jnp.concatenate([unit_gain, offset_bias, leak_slope], axis=0)
+    peer_vec = lax.ppermute(own_vec, "section", swap)
     micro = section_input.shape[0] // 2
 
     def widened(rows):
@@ -326,42 +386,42 @@
     flags = [(plane == s).astype(jnp.int32).reshape(1) for s in range(planes)]
     flips = flip_all(weights)
     parts = [x[m : m + 1] for m in range(micro)]
+    mine_at, other_at = core.astype(jnp.uint32), (1 - core).astype(jnp.uint32)
     class_ids = class_offsets[0] + jnp.arange(class_centers.shape[0], dtype=jnp.int32)
-    held = load_weights(core.reshape(1), weights, "load_forward", (*parts, class_ids, *flags))
+    held, vec, pool_compact, embed_ready = load_weights(
+        core.reshape(1), weights, own_vec, peer_vec, depthwise, embed_weight, (*parts, class_ids, *flags, mine_at.reshape(1), other_at.reshape(1))
+    )
     saved = {}
     for s in range(planes):
         for m in range(micro):
             parts[m], saved[s, m] = forward_stage(flags[s], parts[m], held, vec)
             if s < planes - 1:
                 parts[m] = lax.ppermute(parts[m], "section", [(2 * s + c, 2 * s + 2 + c) for c in range(2)])
-    x = jnp.concatenate(parts, axis=0)
-    x, depthwise, embed_weight, class_centers, labels = lax.optimization_barrier(
-        (x, depthwise, embed_weight, class_centers, labels)
+    embedded, sent = pool_and_embed(parts, pool_compact, embed_ready, shards)
+    width = embedded.shape[-1]
+    embedded, depthwise, embed_weight, labels = lax.optimization_barrier(
+        (embedded, depthwise, embed_weight, labels)
     )
     pool_weight = widened(depthwise)[0].astype(jnp.float32)
-    pooled = jnp.sum(x.astype(jnp.float32) * pool_weight[None], axis=1).astype(jnp.bfloat16)
-    embedded = jnp.dot(pooled, embed_weight, preferred_element_type=jnp.float32)
-    normed = unit_scale(embedded)[0]
-    width = embedded.shape[-1]
-    my_labels = lax.dynamic_slice_in_dim(labels, core * micro, micro, 0).T.reshape(-1)
-
-    def scaled_centres():
-        return unit_scale(class_centers.astype(jnp.float32))[0].astype(jnp.bfloat16)
+
+    def find_hits():
+        mine = lax.dynamic_slice_in_dim(labels, core * micro, micro, 0).T.reshape(-1)
+        return mine[:, None] == class_ids[None, :]
 
     def label_rows():
-        hits = my_labels[:, None] == class_ids[None, :]
         rows = jnp.dot(
-            hits.astype(jnp.bfloat16), scaled_centres(), preferred_element_type=jnp.float32
+            find_hits().astype(jnp.bfloat16),
+            unit_centres(class_centers, class_ids),
+            preferred_element_type=jnp.float32,
         ).astype(jnp.bfloat16)
         rows = lax.all_to_all(rows.reshape(shards, micro, width), "shard", 0, 0, tiled=True)
         return jnp.sum(rows.astype(jnp.float32), axis=0).astype(jnp.bfloat16)
 
     chosen = lax.cond(plane == 0, label_rows, lambda: jnp.zeros((micro, width), jnp.bfloat16))
     chosen = lax.ppermute(chosen, "section", [(c, sections - 2 + c) for c in range(2)])
-    sent = jnp.broadcast_to(normed.astype(jnp.bfloat16)[None], (shards, micro, width))
     unit_half = lax.all_to_all(sent, "shard", 0, 0, tiled=True).reshape(shards * micro, width)
-    centres_unit = scaled_centres()
-    label_hits = my_labels[:, None] == class_ids[None, :]
+    centres_unit = unit_centres(class_centers, chosen)
+    label_hits = find_hits()
     cosines = lax.dot_general(
         unit_half, centres_unit, (((1,), (1,)), ((), ())), preferred_element_type=jnp.float32
     )
@@ -382,7 +442,7 @@
     stores = [jnp.zeros((2, ROWS, C), jnp.bfloat16) for m in range(micro)]
     for s in reversed(range(planes)):
         for m in range(micro):
-            parts[m], stores[m] = backward_stage(m, flags[s], parts[m], flips, vec, zbuf, stores[m])
+            parts[m], stores[m] = backward_stage(m, s == 0, flags[s], parts[m], flips, vec, zbuf, stores[m])
             if s > 0:
                 parts[m] = lax.ppermute(parts[m], "section", [(2 * s + c, 2 * s - 2 + c) for c in range(2)])
     store = jnp.stack(stores, axis=1)
@@ -390,11 +450,11 @@
     def narrowed(rows):
         return rows.reshape(-1, SIDE, WIDE, C)[:, :, :SIDE].reshape(-1, SIDE * SIDE, C)
 
-    kept = narrowed(lax.dynamic_index_in_dim(store, core, 0, keepdims=False))
-    given = narrowed(lax.dynamic_index_in_dim(store, 1 - core, 0, keepdims=False))
+    kept = narrowed(lax.dynamic_index_in_dim(store, mine_at, 0, keepdims=False))
+    given = narrowed(lax.dynamic_index_in_dim(store, other_at, 0, keepdims=False))
     taken = lax.ppermute(given, "section", swap)
-    first = jnp.where(core == 0, kept, taken)
-    second = jnp.where(core == 0, taken, kept)
+    first = jnp.where(mine_at == 0, kept, taken)
+    second = jnp.where(mine_at == 0, taken, kept)
     return jnp.concatenate([first, second], axis=0)[None, :, None]
 
 

time: 146 us -> 157 us (1.075)
  Pallas kernels: 24.6 us -> 40.3 us
  waiting for transfers between devices: 35 us -> 29.1 us
  starting transfers between devices: 45.4 us -> 50.9 us
  other arithmetic: 5.27 us -> 3.52 us
  local copies, waits for them, and re-layouts: 3.75 us -> 2.1 us
    pallas_call x1 -> x4, Pallas kernels: 2.51 us -> 18 us  [the longest x2 14.4 us: unit_centres(): pl.pallas_call(centres_body, grid=(rows // 128,), in_specs=[block, AN], o...]
    all_to_all x1, waiting for transfers between devices: 13.4 us -> 4.71 us  [on_device(): lax.all_to_all(sent, 'shard', 0, 0, tiled=True)]
    ppermute x1, starting transfers between devices: 5.67 us -> 8.53 us  [on_device(): taken = lax.ppermute(given, 'section', swap)]
    all_to_all x1, starting transfers between devices: 7.44 us -> 9.87 us  [on_device(): lax.all_to_all(sums.reshape(shards, micro, -1), 'shard', 0, 0, tiled=True)]
    ppermute x6, waiting for transfers between devices: 13.6 us -> 15.9 us  [on_device(): lax.ppermute(parts[m], 'section', [(2 * s + c, 2 * s - 2 + c) for c in ra...]
  transfers between devices with their start and end apart: 19 -> 19, of which waited for: 6 -> 7; matrix products, arithmetic and copies ran while one was open for 2% -> 1% of each run, Pallas kernels for 10% -> 14%
where the time goes in v5:
time: 157 us; the launch traced here: 156 us
  starting transfers between devices  50.9 us (32%)
  Pallas kernels  40.3 us (26%)
  waiting for transfers between devices  29.1 us (19%)
  blocking collectives  27 us (17%)
  other arithmetic  3.52 us (2%)
  local copies, waits for them, and re-layouts  2.1 us (1%)
  matrix products  1.64 us (1%)
    all_to_all x1, blocking collectives, label_rows(): lax.all_to_all(rows.reshape(shards, micro, width), 'shard', 0, 0, tiled=T...  27 us
    ppermute x6, waiting for transfers between devices, on_device(): lax.ppermute(parts[m], 'section', [(2 * s + c, 2 * s - 2 + c) for c in ra...  15.9 us
    pallas_call x2, Pallas kernels, unit_centres(): pl.pallas_call(centres_body, grid=(rows // 128,), in_specs=[block, AN], o...  14.4 us
    ppermute x2, starting transfers between devices, on_device(): peer = tuple((lax.ppermute(w, 'section', swap) for w in own))  10.8 us
    all_to_all x1, starting transfers between devices, on_device(): lax.all_to_all(sums.reshape(shards, micro, -1), 'shard', 0, 0, tiled=True)  9.87 us
    pallas_call x1, Pallas kernels, flip_all(): pl.pallas_call(flip_body, grid=(9,), in_specs=[pl.BlockSpec((C, C), lambd...  8.66 us
    ppermute x1, starting transfers between devices, on_device(): taken = lax.ppermute(given, 'section', swap)  8.53 us
    all_to_all x1, starting transfers between devices, on_device(): lax.all_to_all(sent, 'shard', 0, 0, tiled=True)  7.32 us
  transfers between devices with their start and end apart: 19, of which 7 were waited for; matrix products, arithmetic and copies ran while one was open for 1% of the time, Pallas kernels for 14%

profile of v5, /device:TPU:1, one launch (start us, length us, event | category | flops | bytes accessed | tf_op | source)
XLA Modules:
  0.0 155.8 jit_solution(2477142867606522851)
XLA Ops:
  0.0 8.9 %collective-permute-start = (bf16[2304,256]{1,0:T(8,128)(2,1)}, bf16[2304,256]{1,0:T(8,128)(2,1)S(1)}, u32[]{:S(2)}, u32[]{:S(2)}) collective-permute-start(bf16[2304,256]{1,0:T(8,128)(2,1)} %bitcast.45), channel_id=1, source_target_pairs={{0,64},{64,0},{128,192},{192,128},{256,320},{320,256},{384,448},{4... | collective-permute-start | bytes 3538952 | tf_op jit(solution)/shard_map/ppermute | solution.py:374
  8.9 1.9 %collective-permute-start.1 = (bf16[2304,256]{1,0:T(8,128)(2,1)}, bf16[2304,256]{1,0:T(8,128)(2,1)S(1)}, u32[]{:S(2)}, u32[]{:S(2)}) collective-permute-start(bf16[2304,256]{1,0:T(8,128)(2,1)} %bitcast.48), channel_id=1, source_target_pairs={{0,64},{64,0},{128,192},{192,128},{256,320},{320,256},{384,448},{4... | collective-permute-start | bytes 3538952 | tf_op jit(solution)/shard_map/ppermute | solution.py:374
  10.8 0.7 pad_maximum_fusion.1.own_vec
  11.5 2.4 %collective-permute-start.2 = (f32[3,256]{1,0:T(4,128)S(1)}, f32[3,256]{1,0:T(4,128)S(1)}, u32[]{:S(2)}, u32[]{:S(2)}) collective-permute-start(f32[3,256]{1,0:T(4,128)S(1)} %pad_maximum_fusion.1.own_vec), channel_id=1, source_target_pairs={{0,64},{64,0},{128,192},{192,128},{256,320},{320,256},{384,448},{4... | collective-permute-start | bytes 9224 | tf_op jit(solution)/shard_map/ppermute | solution.py:377
  14.6 0.2 constant_dynamic-slice_fusion
  14.8 0.3 pad_slice_fusion
  15.3 0.0 collective-permute-done.1.peer2.refs_3_
  15.3 2.6 %load_weights.1 = (bf16[2,2,2304,256]{3,2,1,0:T(8,128)(2,1)S(1)}, f32[2,3,256]{2,1,0:T(4,128)S(1)}, bf16[196,256]{1,0:T(8,128)(2,1)S(1)}, bf16[256,512]{1,0:T(8,128)(2,1)S(1)}) custom-call(s32[1]{0:T(128)} %bitcast.5.flag, bf16[2304,256]{1,0:T(8,128)(2,1)} %bitcast.46, bf16[2304,256]{1,0:T(8,128)(2,1)} %bitcast.49, ...), custom_call_target="tpu_custom_call" | custom-call | flops 300000000 | bytes 9000000 | tf_op jit(solution)/shard_map/load_weights/pallas_call | solution.py:271
  18.0 2.4 %forward_stage.12 = (bf16[1,224,256]{2,1,0:T(8,128)(2,1)S(1)}, bf16[2,224,256]{2,1,0:T(8,128)(2,1)}) custom-call(s32[1]{0:T(128)} %bitcast.1.rest_3_.flag, bf16[1,224,256]{2,1,0:T(8,128)(2,1)S(1)} %bitcast.44, bf16[2,2,2304,256]{3,2,1,0:T(8,128)(2,1)S(1)} %get-tuple-element.67.held, f32[2,3,256]{2,1,0:T(4,128)S(1)} %get-tuple-element.68.vec_ref), custom_call_target="tpu_custom_call" | custom-call | flops 1056964608 | bytes 6000000 | tf_op jit(solution)/shard_map/forward_stage/pallas_call | solution.py:289
  20.4 1.3 collective-permute-start.6
  21.7 2.4 %forward_stage.8 = (bf16[1,224,256]{2,1,0:T(8,128)(2,1)S(1)}, bf16[2,224,256]{2,1,0:T(8,128)(2,1)}) custom-call(s32[1]{0:T(128)} %bitcast.1.rest_3_.flag, bf16[1,224,256]{2,1,0:T(8,128)(2,1)S(1)} %bitcast.42, bf16[2,2,2304,256]{3,2,1,0:T(8,128)(2,1)S(1)} %get-tuple-element.67.held, f32[2,3,256]{2,1,0:T(4,128)S(1)} %get-tuple-element.68.vec_ref), custom_call_target="tpu_custom_call" | custom-call | flops 1056964608 | bytes 6000000 | tf_op jit(solution)/shard_map/forward_stage/pallas_call | solution.py:289
  24.1 1.3 collective-permute-start.3
  25.4 0.0 collective-permute-done.6.x_ref
  25.5 0.7 collective-permute-start.7
  26.2 2.0 %collective-permute-done.3.x_ref = bf16[1,224,256]{2,1,0:T(8,128)(2,1)S(1)} collective-permute-done((bf16[1,224,256]{2,1,0:T(8,128)(2,1)S(1)}, bf16[1,224,256]{2,1,0:T(8,128)(2,1)S(1)}, u32[]{:S(2)}, u32[]{:S(2)}) %collective-permute-start.3) | collective-permute-done | bytes 114720 | tf_op jit(solution)/shard_map/ppermute | solution.py:399
  28.2 0.7 collective-permute-start.4
  28.9 0.7 collective-permute-start.8
  29.7 0.7 collective-permute-start.5
  30.4 0.0 copy-start.5
  30.4 1.0 pool_and_embed.1
  31.4 35.2 %conditional.1 = (bf16[2,512]{1,0:T(2,128)(2,1)S(1)}) conditional(s32[]{:T(128)} %convert_element_type.38, () %tuple.12, (s32[]{:T(128)}, s32[4,64]{1,0:T(4,128)S(1)}, s32[1664]{0:T(1024)S(1)}, bf16[1664,512]{1,0:T(8,128)(2,1)}) %tuple.26), branch_computations={%region_0.1_spmd, %region_1.3_spmd} | conditional | flops 318446848 | bytes 5503740 | solution.py:420
  31.4 0.1 copy.29
  31.5 0.1 dynamic-slice_bitcast_fusion
  31.6 0.1 eq.6
  31.8 7.2 %unit_centres.2 = bf16[1664,512]{1,0:T(8,128)(2,1)S(1)} custom-call(bf16[1664,512]{1,0:T(8,128)(2,1)} %get-tuple-element.19.centres_ref, s32[1664]{0:T(1024)S(1)} %get-tuple-element.18.after), custom_call_target="tpu_custom_call" | custom-call | flops 100000000 | bytes 3000000 | tf_op jit(solution)/shard_map/cond/branch_1_fun/unit_centres/pallas_call | solution.py:120
  39.0 0.4 convolution_convert_fusion
  39.4 0.1 reshape.55
  39.5 27.0 %all_to_all.14 = bf16[64,2,512]{2,1,0:T(2,128)(2,1)S(1)} all-to-all(bf16[64,2,512]{2,1,0:T(2,128)(2,1)S(1)} %reshape.55), channel_id=1, replica_groups=mesh['section'=8,'shard'=64] {'shard'}, dimensions={0} | all-to-all | bytes 262144 | tf_op jit(solution)/shard_map/cond/branch_1_fun/all_to_all | solution.py:417
  66.5 0.1 reduce_sum.27
  66.6 7.3 %all-to-all-start.1 = ((bf16[64,2,512]{2,1,0:T(2,128)(2,1)}), bf16[64,2,512]{2,1,0:T(2,128)(2,1)S(1)}, u32[]{:S(2)}, u32[]{:S(2)}) async-start(bf16[64,2,512]{2,1,0:T(2,128)(2,1)} %get-tuple-element.79), calls=%async_computation.1 | async-start | bytes 262144 | tf_op jit(solution)/shard_map/all_to_all | solution.py:422
  73.9 1.5 collective-permute-start.9
  75.4 0.1 copy.30
  75.5 0.1 eq.54
  75.7 0.3 collective-permute-done.9.after.chosen_ref
  76.0 7.2 %unit_centres.3 = bf16[1664,512]{1,0:T(8,128)(2,1)S(1)} custom-call(bf16[1664,512]{1,0:T(8,128)(2,1)} %centres_ref.1, bf16[2,512]{1,0:T(2,128)(2,1)S(1)} %collective-permute-done.9.after.chosen_ref), custom_call_target="tpu_custom_call" | custom-call | flops 100000000 | bytes 3000000 | tf_op jit(solution)/shard_map/unit_centres/pallas_call | solution.py:120
  83.2 4.7 %all-to-all-done.1 = bf16[64,2,512]{2,1,0:T(2,128)(2,1)S(1)} async-done(((bf16[64,2,512]{2,1,0:T(2,128)(2,1)}), bf16[64,2,512]{2,1,0:T(2,128)(2,1)S(1)}, u32[]{:S(2)}, u32[]{:S(2)}) %all-to-all-start.1) | async-done | bytes 131104 | tf_op jit(solution)/shard_map/all_to_all | solution.py:422
  87.9 0.1 reshape.82
  88.0 0.8 fusion.9
  88.7 0.4 convolution_convert_fusion.1
  89.2 0.1 concatenate.16
  89.2 0.2 concatenate.20
  89.5 0.8 pad_maximum_fusion
  90.3 9.9 %all-to-all-start.2 = ((bf16[64,2,513]{2,1,0:T(2,128)(2,1)}), bf16[64,2,513]{2,1,0:T(2,128)(2,1)S(1)}, u32[]{:S(2)}, u32[]{:S(2)}) async-start(bf16[64,2,513]{2,1,0:T(2,128)(2,1)} %pad_maximum_fusion), calls=%async_computation.2 | async-start | bytes 327680 | tf_op jit(solution)/shard_map/all_to_all | solution.py:435
  100.2 0.1 pad_add_fusion.flag
  100.3 8.7 %flip_all.1 = (bf16[2304,256]{1,0:T(8,128)(2,1)}, bf16[2304,256]{1,0:T(8,128)(2,1)}, bf16[2304,256]{1,0:T(8,128)(2,1)}, bf16[2304,256]{1,0:T(8,128)(2,1)}) custom-call(bf16[2304,256]{1,0:T(8,128)(2,1)} %bitcast.47, bf16[2304,256]{1,0:T(8,128)(2,1)} %bitcast.50, bf16[2304,256]{1,0:T(8,128)(2,1)} %copy-done.1, bf16[2304,256]{1,0:T(8,128)(2,1)} %copy-done.2), custom_call_target="tpu_custom_call" | custom-call | flops 1207959552 | bytes 9000000 | tf_op jit(solution)/shard_map/flip_all/pallas_call | solution.py:334
  109.0 5.3 %all-to-all-done.2 = bf16[64,2,513]{2,1,0:T(2,128)(2,1)S(1)} async-done(((bf16[64,2,513]{2,1,0:T(2,128)(2,1)}), bf16[64,2,513]{2,1,0:T(2,128)(2,1)S(1)}, u32[]{:S(2)}, u32[]{:S(2)}) %all-to-all-start.2) | async-done | bytes 131360 | tf_op jit(solution)/shard_map/all_to_all | solution.py:435
  114.4 0.2 convert_reduce_fusion.sums_ref
  114.5 3.2 %tail.1 = (bf16[2,224,256]{2,1,0:T(8,128)(2,1)S(1)}, bf16[2,2,2304,256]{3,2,1,0:T(8,128)(2,1)S(1)}, bf16[2,2,224,256]{3,2,1,0:T(8,128)(2,1)S(1)}) custom-call(s32[2]{0:T(128)S(1)} %pad_add_fusion.flag, f32[2,513]{1,0:T(2,128)S(1)} %convert_reduce_fusion.sums_ref, bf16[2,512]{1,0:T(2,128)(2,1)S(1)} %collective-permute-done.9.after.chosen_ref, ...), custom_call_target="tpu_custom_call" | custom-call | flops 300000000 | bytes 9000000 | tf_op jit(solution)/shard_map/tail/pallas_call | solution.py:240
  117.8 0.7 collective-permute-start.13
  118.5 0.7 collective-permute-start.10
  119.2 0.7 collective-permute-start.14
  120.0 0.7 collective-permute-start.11
  120.7 1.3 collective-permute-start.15
  122.0 1.3 collective-permute-start.12
  123.3 14.7 %collective-permute-done.15.g_ref = bf16[1,224,256]{2,1,0:T(8,128)(2,1)S(1)} collective-permute-done((bf16[1,224,256]{2,1,0:T(8,128)(2,1)S(1)}, bf16[1,224,256]{2,1,0:T(8,128)(2,1)S(1)}, u32[]{:S(2)}, u32[]{:S(2)}) %collective-permute-start.15) | collective-permute-done | bytes 114720 | tf_op jit(solution)/shard_map/ppermute | solution.py:447
  138.0 2.7 %backward_stage.15 = (bf16[16,128]{1,0:T(8,128)(2,1)}, bf16[2,224,256]{2,1,0:T(8,128)(2,1)S(1)}) custom-call(s32[1]{0:T(128)} %bitcast.1.rest_3_.flag, bf16[1,224,256]{2,1,0:T(8,128)(2,1)S(1)} %collective-permute-done.15.g_ref, bf16[2,2,2304,256]{3,2,1,0:T(8,128)(2,1)S(1)} %get-tuple-element.98.held, ...), custom_call_target="tpu_custom_call", output_to_operand_aliasing={{1}: (5, {})} | custom-call | flops 1056964608 | bytes 6000000 | tf_op jit(solution)/shard_map/backward_stage/pallas_call | solution.py:306
  140.6 1.2 collective-permute-done.12.g_ref
  141.8 2.7 %backward_stage.11 = (bf16[16,128]{1,0:T(8,128)(2,1)}, bf16[2,224,256]{2,1,0:T(8,128)(2,1)S(1)}) custom-call(s32[1]{0:T(128)} %bitcast.1.rest_3_.flag, bf16[1,224,256]{2,1,0:T(8,128)(2,1)S(1)} %collective-permute-done.12.g_ref, bf16[2,2,2304,256]{3,2,1,0:T(8,128)(2,1)S(1)} %get-tuple-element.98.held, ...), custom_call_target="tpu_custom_call", output_to_operand_aliasing={{1}: (5, {})} | custom-call | flops 1056964608 | bytes 6000000 | tf_op jit(solution)/shard_map/backward_stage/pallas_call | solution.py:306
  144.5 0.2 copy.33
  144.7 8.5 %collective-permute-start.16 = (bf16[2,196,256]{2,0,1:T(2,128)(2,1)S(1)}, bf16[2,196,256]{2,0,1:T(2,128)(2,1)S(1)}, u32[]{:S(2)}, u32[]{:S(2)}) collective-permute-start(bf16[2,196,256]{2,0,1:T(2,128)(2,1)S(1)} %bitcast.54), channel_id=1, source_target_pairs={{0,64},{64,0},{128,192},{192,128},{256,320},{320,256},{384,448},{4... | collective-permute-start | bytes 602120 | tf_op jit(solution)/shard_map/ppermute | solution.py:455
  153.3 0.2 copy.32
  153.5 0.8 collective-permute-done.16
  154.3 0.3 broadcast_select_fusion.1
  154.7 1.2 maximum_bitcast_fusion
  (44 shorter events, 0.5 us)
Async XLA Ops:
  0.0 14.6 %copy-start = (bf16[4,1,196,256]{3,0,2,1:T(4,128)(2,1)S(1)}, bf16[4,1,196,256]{3,0,2,1:T(4,128)(2,1)}, u32[]{:S(2)}) copy-start(bf16[4,1,196,256]{3,0,2,1:T(4,128)(2,1)} %param.13) | copy-start | bytes 1204228
  0.0 15.3 %collective-permute-start = (bf16[2304,256]{1,0:T(8,128)(2,1)}, bf16[2304,256]{1,0:T(8,128)(2,1)S(1)}, u32[]{:S(2)}, u32[]{:S(2)}) collective-permute-start(bf16[2304,256]{1,0:T(8,128)(2,1)} %bitcast.45), channel_id=1, source_target_pairs={{0,64},{64,0},{128,192},{192,128},{256,320},{320,256},{384,448},{4... | collective-permute-start | bytes 3538952 | tf_op jit(solution)/shard_map/ppermute | solution.py:374
  8.9 6.5 %collective-permute-start.1 = (bf16[2304,256]{1,0:T(8,128)(2,1)}, bf16[2304,256]{1,0:T(8,128)(2,1)S(1)}, u32[]{:S(2)}, u32[]{:S(2)}) collective-permute-start(bf16[2304,256]{1,0:T(8,128)(2,1)} %bitcast.48), channel_id=1, source_target_pairs={{0,64},{64,0},{128,192},{192,128},{256,320},{320,256},{384,448},{4... | collective-permute-start | bytes 3538952 | tf_op jit(solution)/shard_map/ppermute | solution.py:374
  11.5 3.8 %collective-permute-start.2 = (f32[3,256]{1,0:T(4,128)S(1)}, f32[3,256]{1,0:T(4,128)S(1)}, u32[]{:S(2)}, u32[]{:S(2)}) collective-permute-start(f32[3,256]{1,0:T(4,128)S(1)} %pad_maximum_fusion.1.own_vec), channel_id=1, source_target_pairs={{0,64},{64,0},{128,192},{192,128},{256,320},{320,256},{384,448},{4... | collective-permute-start | bytes 9224 | tf_op jit(solution)/shard_map/ppermute | solution.py:377
  15.3 2.6 %copy-start.1 = (bf16[2304,256]{1,0:T(8,128)(2,1)}, bf16[2304,256]{1,0:T(8,128)(2,1)S(1)}, u32[]{:S(2)}) copy-start(bf16[2304,256]{1,0:T(8,128)(2,1)S(1)} %collective-permute-done.peer1.refs_2_) | copy-start | bytes 3538948
  15.3 2.6 %copy-start.2 = (bf16[2304,256]{1,0:T(8,128)(2,1)}, bf16[2304,256]{1,0:T(8,128)(2,1)S(1)}, u32[]{:S(2)}) copy-start(bf16[2304,256]{1,0:T(8,128)(2,1)S(1)} %collective-permute-done.1.peer2.refs_3_) | copy-start | bytes 3538948
  20.4 5.0 %collective-permute-start.6 = (bf16[1,224,256]{2,1,0:T(8,128)(2,1)S(1)}, bf16[1,224,256]{2,1,0:T(8,128)(2,1)S(1)}, u32[]{:S(2)}, u32[]{:S(2)}) collective-permute-start(bf16[1,224,256]{2,1,0:T(8,128)(2,1)S(1)} %get-tuple-element.73), channel_id=1, source_target_pairs={{0,128},{64,192},{1,129},{65,193},{2,130},{66,194},{3,131},{67,195... | collective-permute-start | bytes 344072 | tf_op jit(solution)/shard_map/ppermute | solution.py:399
  24.1 4.0 %collective-permute-start.3 = (bf16[1,224,256]{2,1,0:T(8,128)(2,1)S(1)}, bf16[1,224,256]{2,1,0:T(8,128)(2,1)S(1)}, u32[]{:S(2)}, u32[]{:S(2)}) collective-permute-start(bf16[1,224,256]{2,1,0:T(8,128)(2,1)S(1)} %get-tuple-element.69), channel_id=1, source_target_pairs={{0,128},{64,192},{1,129},{65,193},{2,130},{66,194},{3,131},{67,195... | collective-permute-start | bytes 344072 | tf_op jit(solution)/shard_map/ppermute | solution.py:399
  25.5 3.4 %collective-permute-start.7 = (bf16[1,224,256]{2,1,0:T(8,128)(2,1)S(1)}, bf16[1,224,256]{2,1,0:T(8,128)(2,1)S(1)}, u32[]{:S(2)}, u32[]{:S(2)}) collective-permute-start(bf16[1,224,256]{2,1,0:T(8,128)(2,1)S(1)} %get-tuple-element.74), channel_id=1, source_target_pairs={{128,256},{192,320},{129,257},{193,321},{130,258},{194,322},{131,2... | collective-permute-start | bytes 344072 | tf_op jit(solution)/shard_map/ppermute | solution.py:399
  28.2 1.4 collective-permute-start.4
  28.9 1.4 collective-permute-start.8
  29.7 0.7 collective-permute-start.5
  30.4 1.1 copy-start.5
  66.6 21.3 %all-to-all-start.1 = ((bf16[64,2,512]{2,1,0:T(2,128)(2,1)}), bf16[64,2,512]{2,1,0:T(2,128)(2,1)S(1)}, u32[]{:S(2)}, u32[]{:S(2)}) async-start(bf16[64,2,512]{2,1,0:T(2,128)(2,1)} %get-tuple-element.79), calls=%async_computation.1 | async-start | bytes 262144 | tf_op jit(solution)/shard_map/all_to_all | solution.py:422
  73.9 2.0 %collective-permute-start.9 = (bf16[2,512]{1,0:T(2,128)(2,1)S(1)}, bf16[2,512]{1,0:T(2,128)(2,1)S(1)}, u32[]{:S(2)}, u32[]{:S(2)}) collective-permute-start(bf16[2,512]{1,0:T(2,128)(2,1)S(1)} %get-tuple-element.138), channel_id=1, source_target_pairs={{0,384},{64,448},{1,385},{65,449},{2,386},{66,450},{3,387},{67,451... | collective-permute-start | bytes 6152 | tf_op jit(solution)/shard_map/ppermute | solution.py:421
  90.3 24.1 %all-to-all-start.2 = ((bf16[64,2,513]{2,1,0:T(2,128)(2,1)}), bf16[64,2,513]{2,1,0:T(2,128)(2,1)S(1)}, u32[]{:S(2)}, u32[]{:S(2)}) async-start(bf16[64,2,513]{2,1,0:T(2,128)(2,1)} %pad_maximum_fusion), calls=%async_computation.2 | async-start | bytes 327680 | tf_op jit(solution)/shard_map/all_to_all | solution.py:435
  100.2 8.7 %copy-start.4 = (bf16[196,256]{1,0:T(8,128)(2,1)S(1)}, bf16[196,256]{1,0:T(8,128)(2,1)}, u32[]{:S(2)}) copy-start(bf16[196,256]{1,0:T(8,128)(2,1)} %pool.1) | copy-start | bytes 301060
  100.3 14.3 %copy-start.3 = (bf16[256,512]{1,0:T(8,128)(2,1)S(1)}, bf16[256,512]{1,0:T(8,128)(2,1)}, u32[]{:S(2)}) copy-start(bf16[256,512]{1,0:T(8,128)(2,1)} %embed_ref) | copy-start | bytes 786436
  117.8 1.4 collective-permute-start.13
  118.5 1.4 collective-permute-start.10
  119.2 1.4 collective-permute-start.14
  120.0 2.0 %collective-permute-start.11 = (bf16[1,224,256]{2,1,0:T(8,128)(2,1)S(1)}, bf16[1,224,256]{2,1,0:T(8,128)(2,1)S(1)}, u32[]{:S(2)}, u32[]{:S(2)}) collective-permute-start(bf16[1,224,256]{2,1,0:T(8,128)(2,1)S(1)} %get-tuple-element.102), channel_id=1, source_target_pairs={{256,128},{320,192},{257,129},{321,193},{258,130},{322,194},{259,1... | collective-permute-start | bytes 344072 | tf_op jit(solution)/shard_map/ppermute | solution.py:447
  120.7 17.3 %collective-permute-start.15 = (bf16[1,224,256]{2,1,0:T(8,128)(2,1)S(1)}, bf16[1,224,256]{2,1,0:T(8,128)(2,1)S(1)}, u32[]{:S(2)}, u32[]{:S(2)}) collective-permute-start(bf16[1,224,256]{2,1,0:T(8,128)(2,1)S(1)} %get-tuple-element.111), channel_id=1, source_target_pairs={{128,0},{192,64},{129,1},{193,65},{130,2},{194,66},{131,3},{195,67... | collective-permute-start | bytes 344072 | tf_op jit(solution)/shard_map/ppermute | solution.py:447
  122.0 19.8 %collective-permute-start.12 = (bf16[1,224,256]{2,1,0:T(8,128)(2,1)S(1)}, bf16[1,224,256]{2,1,0:T(8,128)(2,1)S(1)}, u32[]{:S(2)}, u32[]{:S(2)}) collective-permute-start(bf16[1,224,256]{2,1,0:T(8,128)(2,1)S(1)} %get-tuple-element.104), channel_id=1, source_target_pairs={{128,0},{192,64},{129,1},{193,65},{130,2},{194,66},{131,3},{195,67... | collective-permute-start | bytes 344072 | tf_op jit(solution)/shard_map/ppermute | solution.py:447
  144.7 9.6 %collective-permute-start.16 = (bf16[2,196,256]{2,0,1:T(2,128)(2,1)S(1)}, bf16[2,196,256]{2,0,1:T(2,128)(2,1)S(1)}, u32[]{:S(2)}, u32[]{:S(2)}) collective-permute-start(bf16[2,196,256]{2,0,1:T(2,128)(2,1)S(1)} %bitcast.54), channel_id=1, source_target_pairs={{0,64},{64,0},{128,192},{192,128},{256,320},{320,256},{384,448},{4... | collective-permute-start | bytes 602120 | tf_op jit(solution)/shard_map/ppermute | solution.py:455

commit v6 on v5

--- a/solution.py
+++ b/solution.py
@@ -109,24 +109,36 @@
     )(*parts, pool, embed)
 
 
-def centres_body(centres_ref, after, out_ref):
-    values = centres_ref[...].astype(jnp.float32)
-    out_ref[...] = unit_scale(values)[0].astype(jnp.bfloat16)
-
-
-def unit_centres(centres, after):
-    rows, width = centres.shape
-    block = pl.BlockSpec((128, width), lambda i: (i, 0))
-    return pl.pallas_call(
-        centres_body,
-        grid=(rows // 128,),
-        in_specs=[block, AN],
-        out_specs=block,
-        out_shape=jax.ShapeDtypeStruct(centres.shape, jnp.bfloat16),
-        compiler_params=pltpu.CompilerParams(vmem_limit_bytes=STAGE_LIMIT),
-        cost_estimate=pl.CostEstimate(flops=100_000_000, bytes_accessed=3_000_000, transcendentals=0),
-        name="unit_centres",
-    )(*in_hbm(centres), after)
+def head_body(unit_ref, centres_ref, scale_ref, labels_ref, ids_ref, *rest):
+    out_ref = rest[-1]
+    faces = unit_ref.shape[0]
+    width = centres_ref.shape[1]
+    centres = centres_ref[...]
+    scale = scale_ref[...]
+    cosines = lax.dot_general(
+        unit_ref[...], centres, (((1,), (1,)), ((), ())), preferred_element_type=jnp.float32
+    )
+    hits = (labels_ref[...] == ids_ref[...]).astype(jnp.float32)
+    weights = jnp.exp(scale_value * (cosines * scale - margin_value * hits))
+    totals = jnp.sum(weights, axis=1, keepdims=True)
+    weighted = jnp.dot(
+        (weights * scale).astype(jnp.bfloat16), centres, preferred_element_type=jnp.float32
+    )
+    out_ref[:, :width] = weighted.astype(jnp.bfloat16)
+    out_ref[:, width:] = jnp.broadcast_to(totals, (faces, 128)).astype(jnp.bfloat16)
+
+
+def class_sums(unit_half, centres, scale, labels, ids, after):
+    faces, width = unit_half.shape
+    return pl.pallas_call(
+        head_body,
+        in_specs=[VM] * 5 + [AN] * len(after),
+        out_specs=VM,
+        out_shape=jax.ShapeDtypeStruct((faces, width + 128), jnp.bfloat16),
+        compiler_params=pltpu.CompilerParams(vmem_limit_bytes=STAGE_LIMIT),
+        cost_estimate=pl.CostEstimate(flops=450_000_000, bytes_accessed=2_000_000, transcendentals=220_000),
+        name="class_sums",
+    )(unit_half, centres, scale, labels, ids, *in_hbm(*after))
 
 
 def forward_body(flag, x_ref, held, vec_ref, out_ref, z_ref, cols, run, zed, zsem):
@@ -189,7 +201,7 @@
             return carry
 
         lax.fori_loop(0, 2, one, 0)
-        if rest[0].ndim == 3:
+        if len(rest) == 4:
             rest[0][0] = run[...].astype(jnp.bfloat16)
 
 
@@ -302,7 +314,7 @@
 
 
 def backward_stage(image, last, flag, g, held, vec, z, store):
-    passed = [jax.ShapeDtypeStruct((16, 128) if last else g.shape, jnp.bfloat16)]
+    passed = [] if last else [jax.ShapeDtypeStruct(g.shape, jnp.bfloat16)]
     outs = pl.pallas_call(
         functools.partial(backward_body, image),
         in_specs=[SM, VM, VM, VM, VM, VM],
@@ -404,14 +416,14 @@
     )
     pool_weight = widened(depthwise)[0].astype(jnp.float32)
 
-    def find_hits():
-        mine = lax.dynamic_slice_in_dim(labels, core * micro, micro, 0).T.reshape(-1)
-        return mine[:, None] == class_ids[None, :]
+    def my_labels():
+        return lax.dynamic_slice_in_dim(labels, core * micro, micro, 0).T.reshape(-1, 1)
 
     def label_rows():
+        centres_unit = unit_scale(class_centers.astype(jnp.float32))[0].astype(jnp.bfloat16)
         rows = jnp.dot(
-            find_hits().astype(jnp.bfloat16),
-            unit_centres(class_centers, class_ids),
+            (my_labels() == class_ids[None, :]).astype(jnp.bfloat16),
+            centres_unit,
             preferred_element_type=jnp.float32,
         ).astype(jnp.bfloat16)
         rows = lax.all_to_all(rows.reshape(shards, micro, width), "shard", 0, 0, tiled=True)
@@ -420,18 +432,8 @@
     chosen = lax.cond(plane == 0, label_rows, lambda: jnp.zeros((micro, width), jnp.bfloat16))
     chosen = lax.ppermute(chosen, "section", [(c, sections - 2 + c) for c in range(2)])
     unit_half = lax.all_to_all(sent, "shard", 0, 0, tiled=True).reshape(shards * micro, width)
-    centres_unit = unit_centres(class_centers, chosen)
-    label_hits = find_hits()
-    cosines = lax.dot_general(
-        unit_half, centres_unit, (((1,), (1,)), ((), ())), preferred_element_type=jnp.float32
-    )
-    logits = scale_value * (cosines - margin_value * label_hits.astype(jnp.float32))
-    exp_logits = jnp.exp(logits)
-    weighted = jnp.dot(
-        exp_logits.astype(jnp.bfloat16), centres_unit, preferred_element_type=jnp.float32
-    )
-    totals = jnp.sum(exp_logits, axis=1, keepdims=True)
-    sums = jnp.concatenate([weighted, totals], axis=1).astype(jnp.bfloat16)
+    scale = unit_scale(class_centers.astype(jnp.float32))[2].reshape(1, -1)
+    sums = class_sums(unit_half, class_centers, scale, my_labels(), class_ids[None, :], flips)
     sums = lax.all_to_all(sums.reshape(shards, micro, -1), "shard", 0, 0, tiled=True)
     sums = jnp.sum(sums.astype(jnp.float32), axis=0)
     g, flips, zbuf = tail(

time: 157 us -> 140 us (0.89)
  Pallas kernels: 40.3 us -> 25.4 us
    pallas_call x2 -> x1, Pallas kernels: 14.4 us -> 0.97 us  [class_sums(): pl.pallas_call(head_body, in_specs=[VM] * 5 + [AN] * len(after), out_spec...]
    ppermute x6, waiting for transfers between devices: 15.9 us -> 7.04 us  [on_device(): lax.ppermute(parts[m], 'section', [(2 * s + c, 2 * s - 2 + c) for c in ra...]
    all_to_all x1, waiting for transfers between devices: 5.34 us -> 13 us  [on_device(): lax.all_to_all(sums.reshape(shards, micro, -1), 'shard', 0, 0, tiled=True)]
  transfers between devices with their start and end apart: 19 -> 19, of which waited for: 7 -> 6; matrix products, arithmetic and copies ran while one was open for 1% -> 2% of each run, Pallas kernels for 14% -> 9%
where the time goes in v6:
time: 140 us; the launch traced here: 139 us
  starting transfers between devices  50.1 us (36%)
  waiting for transfers between devices  28.1 us (20%)
  blocking collectives  27.1 us (19%)
  Pallas kernels  25.4 us (18%)
  other arithmetic  3.54 us (3%)
  local copies, waits for them, and re-layouts  2.62 us (2%)
    all_to_all x1, blocking collectives, label_rows(): lax.all_to_all(rows.reshape(shards, micro, width), 'shard', 0, 0, tiled=T...  27.1 us
    all_to_all x1, waiting for transfers between devices, on_device(): lax.all_to_all(sums.reshape(shards, micro, -1), 'shard', 0, 0, tiled=True)  13 us
    ppermute x2, starting transfers between devices, on_device(): peer = tuple((lax.ppermute(w, 'section', swap) for w in own))  10.8 us
    all_to_all x1, starting transfers between devices, on_device(): lax.all_to_all(sums.reshape(shards, micro, -1), 'shard', 0, 0, tiled=True)  9.32 us
    pallas_call x1, Pallas kernels, flip_all(): pl.pallas_call(flip_body, grid=(9,), in_specs=[pl.BlockSpec((C, C), lambd...  8.51 us
    ppermute x1, starting transfers between devices, on_device(): taken = lax.ppermute(given, 'section', swap)  8.44 us
    all_to_all x1, starting transfers between devices, on_device(): lax.all_to_all(sent, 'shard', 0, 0, tiled=True)  7.25 us
    ppermute x6, waiting for transfers between devices, on_device(): lax.ppermute(parts[m], 'section', [(2 * s + c, 2 * s - 2 + c) for c in ra...  7.04 us
  transfers between devices with their start and end apart: 19, of which 6 were waited for; matrix products, arithmetic and copies ran while one was open for 2% of the time, Pallas kernels for 9%

profile of v6, /device:TPU:1, one launch (start us, length us, event | category | flops | bytes accessed | tf_op | source)
XLA Modules:
  0.0 138.8 jit_solution(5626935112412339124)
XLA Ops:
  0.0 8.9 %collective-permute-start = (bf16[2304,256]{1,0:T(8,128)(2,1)}, bf16[2304,256]{1,0:T(8,128)(2,1)S(1)}, u32[]{:S(2)}, u32[]{:S(2)}) collective-permute-start(bf16[2304,256]{1,0:T(8,128)(2,1)} %bitcast.41), channel_id=1, source_target_pairs={{0,64},{64,0},{128,192},{192,128},{256,320},{320,256},{384,448},{4... | collective-permute-start | bytes 3538952 | tf_op jit(solution)/shard_map/ppermute | solution.py:386
  8.9 1.9 %collective-permute-start.1 = (bf16[2304,256]{1,0:T(8,128)(2,1)}, bf16[2304,256]{1,0:T(8,128)(2,1)S(1)}, u32[]{:S(2)}, u32[]{:S(2)}) collective-permute-start(bf16[2304,256]{1,0:T(8,128)(2,1)} %bitcast.44), channel_id=1, source_target_pairs={{0,64},{64,0},{128,192},{192,128},{256,320},{320,256},{384,448},{4... | collective-permute-start | bytes 3538952 | tf_op jit(solution)/shard_map/ppermute | solution.py:386
  10.8 0.7 pad_maximum_fusion.own_vec
  11.5 2.4 %collective-permute-start.2 = (f32[3,256]{1,0:T(4,128)S(1)}, f32[3,256]{1,0:T(4,128)S(1)}, u32[]{:S(2)}, u32[]{:S(2)}) collective-permute-start(f32[3,256]{1,0:T(4,128)S(1)} %pad_maximum_fusion.own_vec), channel_id=1, source_target_pairs={{0,64},{64,0},{128,192},{192,128},{256,320},{320,256},{384,448},{4... | collective-permute-start | bytes 9224 | tf_op jit(solution)/shard_map/ppermute | solution.py:389
  14.6 0.2 constant_dynamic-slice_fusion
  14.8 0.5 pad_slice_fusion
  15.4 0.0 collective-permute-done.peer1.refs_2_
  15.4 0.0 collective-permute-done.1.peer2.refs_3_
  15.5 2.6 %load_weights.1 = (bf16[2,2,2304,256]{3,2,1,0:T(8,128)(2,1)S(1)}, f32[2,3,256]{2,1,0:T(4,128)S(1)}, bf16[196,256]{1,0:T(8,128)(2,1)S(1)}, bf16[256,512]{1,0:T(8,128)(2,1)S(1)}) custom-call(s32[1]{0:T(128)} %bitcast.5.flag, bf16[2304,256]{1,0:T(8,128)(2,1)} %bitcast.42, bf16[2304,256]{1,0:T(8,128)(2,1)} %bitcast.45, ...), custom_call_target="tpu_custom_call" | custom-call | flops 300000000 | bytes 9000000 | tf_op jit(solution)/shard_map/load_weights/pallas_call | solution.py:283
  18.1 2.4 %forward_stage.12 = (bf16[1,224,256]{2,1,0:T(8,128)(2,1)S(1)}, bf16[2,224,256]{2,1,0:T(8,128)(2,1)}) custom-call(s32[1]{0:T(128)} %bitcast.1.rest_3_.flag, bf16[1,224,256]{2,1,0:T(8,128)(2,1)S(1)} %bitcast.40, bf16[2,2,2304,256]{3,2,1,0:T(8,128)(2,1)S(1)} %get-tuple-element.65.held, f32[2,3,256]{2,1,0:T(4,128)S(1)} %get-tuple-element.66.vec_ref), custom_call_target="tpu_custom_call" | custom-call | flops 1056964608 | bytes 6000000 | tf_op jit(solution)/shard_map/forward_stage/pallas_call | solution.py:301
  20.5 1.3 collective-permute-start.6
  21.8 2.4 %forward_stage.8 = (bf16[1,224,256]{2,1,0:T(8,128)(2,1)S(1)}, bf16[2,224,256]{2,1,0:T(8,128)(2,1)}) custom-call(s32[1]{0:T(128)} %bitcast.1.rest_3_.flag, bf16[1,224,256]{2,1,0:T(8,128)(2,1)S(1)} %bitcast.38, bf16[2,2,2304,256]{3,2,1,0:T(8,128)(2,1)S(1)} %get-tuple-element.65.held, f32[2,3,256]{2,1,0:T(4,128)S(1)} %get-tuple-element.66.vec_ref), custom_call_target="tpu_custom_call" | custom-call | flops 1056964608 | bytes 6000000 | tf_op jit(solution)/shard_map/forward_stage/pallas_call | solution.py:301
  24.2 1.3 collective-permute-start.3
  25.6 0.7 collective-permute-start.7
  26.2 2.0 %collective-permute-done.3.x_ref = bf16[1,224,256]{2,1,0:T(8,128)(2,1)S(1)} collective-permute-done((bf16[1,224,256]{2,1,0:T(8,128)(2,1)S(1)}, bf16[1,224,256]{2,1,0:T(8,128)(2,1)S(1)}, u32[]{:S(2)}, u32[]{:S(2)}) %collective-permute-start.3) | collective-permute-done | bytes 114720 | tf_op jit(solution)/shard_map/ppermute | solution.py:411
  28.3 0.7 collective-permute-start.4
  29.0 0.0 copy-start.4
  29.0 0.8 collective-permute-start.8
  29.9 0.7 collective-permute-start.5
  30.5 0.4 multiply_reduce_fusion
  31.0 0.0 copy-start.6
  31.1 1.0 pool_and_embed.1
  32.1 28.6 %conditional.1 = (bf16[2,512]{1,0:T(2,128)(2,1)S(1)}) conditional(s32[]{:T(128)} %convert_element_type.41, () %tuple.13, (s32[]{:T(128)}, s32[4,64]{1,0:T(4,128)S(1)}, s32[1664]{0:T(1024)S(1)}, bf16[1664,512]{1,0:T(8,128)(2,1)S(1)}) %tuple.25), branch_computations={%region_2.3_spmd, %region_3.6_spmd} | conditional | flops 223561984 | bytes 4234300 | solution.py:432
  32.1 0.1 copy.31
  32.2 0.1 dynamic-slice_bitcast_fusion
  32.2 0.1 eq.6
  32.4 0.4 fusion
  32.8 0.6 fusion.5
  33.4 0.1 reshape.94
  33.5 27.1 %all_to_all.14 = bf16[64,2,512]{2,1,0:T(2,128)(2,1)S(1)} all-to-all(bf16[64,2,512]{2,1,0:T(2,128)(2,1)S(1)} %reshape.94), channel_id=1, replica_groups=mesh['section'=8,'shard'=64] {'shard'}, dimensions={0} | all-to-all | bytes 262144 | tf_op jit(solution)/shard_map/cond/branch_1_fun/all_to_all | solution.py:429
  60.5 0.1 reduce_sum.36
  60.7 7.2 %all-to-all-start.1 = ((bf16[64,2,512]{2,1,0:T(2,128)(2,1)}), bf16[64,2,512]{2,1,0:T(2,128)(2,1)S(1)}, u32[]{:S(2)}, u32[]{:S(2)}) async-start(bf16[64,2,512]{2,1,0:T(2,128)(2,1)} %get-tuple-element.77), calls=%async_computation.1 | async-start | bytes 262144 | tf_op jit(solution)/shard_map/all_to_all | solution.py:434
  68.0 8.5 %flip_all.1 = (bf16[2304,256]{1,0:T(8,128)(2,1)}, bf16[2304,256]{1,0:T(8,128)(2,1)}, bf16[2304,256]{1,0:T(8,128)(2,1)}, bf16[2304,256]{1,0:T(8,128)(2,1)}) custom-call(bf16[2304,256]{1,0:T(8,128)(2,1)} %bitcast.43, bf16[2304,256]{1,0:T(8,128)(2,1)} %bitcast.46, bf16[2304,256]{1,0:T(8,128)(2,1)} %copy-done.1, bf16[2304,256]{1,0:T(8,128)(2,1)} %copy-done.2), custom_call_target="tpu_custom_call" | custom-call | flops 1207959552 | bytes 9000000 | tf_op jit(solution)/shard_map/flip_all/pallas_call | solution.py:346
  76.5 0.1 copy.29
  76.6 0.1 reshape.138.labels_ref
  76.7 5.2 %all-to-all-done.1 = bf16[64,2,512]{2,1,0:T(2,128)(2,1)S(1)} async-done(((bf16[64,2,512]{2,1,0:T(2,128)(2,1)}), bf16[64,2,512]{2,1,0:T(2,128)(2,1)S(1)}, u32[]{:S(2)}, u32[]{:S(2)}) %all-to-all-start.1) | async-done | bytes 131104 | tf_op jit(solution)/shard_map/all_to_all | solution.py:434
  81.9 0.1 reshape.123.unit_ref
  82.0 0.0 copy-start.5
  82.0 1.0 class_sums.1
  82.9 0.0 copy-start.3
  83.0 0.7 reshape.125
  83.7 9.3 %all-to-all-start.2 = ((bf16[64,2,640]{2,1,0:T(2,128)(2,1)}), bf16[64,2,640]{2,1,0:T(2,128)(2,1)S(1)}, u32[]{:S(2)}, u32[]{:S(2)}) async-start(bf16[64,2,640]{2,1,0:T(2,128)(2,1)} %reshape.125), calls=%async_computation.2 | async-start | bytes 327680 | tf_op jit(solution)/shard_map/all_to_all | solution.py:437
  93.0 0.1 pad_add_fusion.flag
  93.1 1.3 collective-permute-start.9
  94.5 13.0 %all-to-all-done.2 = bf16[64,2,640]{2,1,0:T(2,128)(2,1)S(1)} async-done(((bf16[64,2,640]{2,1,0:T(2,128)(2,1)}), bf16[64,2,640]{2,1,0:T(2,128)(2,1)S(1)}, u32[]{:S(2)}, u32[]{:S(2)}) %all-to-all-start.2) | async-done | bytes 163872 | tf_op jit(solution)/shard_map/all_to_all | solution.py:437
  107.5 0.2 convert_reduce_fusion.sums_ref
  107.7 3.2 %tail.1 = (bf16[2,224,256]{2,1,0:T(8,128)(2,1)S(1)}, bf16[2,2,2304,256]{3,2,1,0:T(8,128)(2,1)S(1)}, bf16[2,2,224,256]{3,2,1,0:T(8,128)(2,1)S(1)}) custom-call(s32[2]{0:T(128)S(1)} %pad_add_fusion.flag, f32[2,640]{1,0:T(2,128)S(1)} %convert_reduce_fusion.sums_ref, bf16[2,512]{1,0:T(2,128)(2,1)S(1)} %collective-permute-done.9.chosen_ref, ...), custom_call_target="tpu_custom_call" | custom-call | flops 300000000 | bytes 9000000 | tf_op jit(solution)/shard_map/tail/pallas_call | solution.py:252
  111.0 0.7 collective-permute-start.13
  111.7 0.7 collective-permute-start.10
  112.4 0.7 collective-permute-start.14
  113.1 0.7 collective-permute-start.11
  113.8 1.3 collective-permute-start.15
  115.1 1.3 collective-permute-start.12
  116.4 5.2 %collective-permute-done.15.g_ref = bf16[1,224,256]{2,1,0:T(8,128)(2,1)S(1)} collective-permute-done((bf16[1,224,256]{2,1,0:T(8,128)(2,1)S(1)}, bf16[1,224,256]{2,1,0:T(8,128)(2,1)S(1)}, u32[]{:S(2)}, u32[]{:S(2)}) %collective-permute-start.15) | collective-permute-done | bytes 114720 | tf_op jit(solution)/shard_map/ppermute | solution.py:449
  121.6 2.0 %backward_stage.15 = bf16[2,224,256]{2,1,0:T(8,128)(2,1)S(1)} custom-call(s32[1]{0:T(128)} %bitcast.1.rest_3_.flag, bf16[1,224,256]{2,1,0:T(8,128)(2,1)S(1)} %collective-permute-done.15.g_ref, bf16[2,2,2304,256]{3,2,1,0:T(8,128)(2,1)S(1)} %get-tuple-element.96.held, f32[2,3,256]{2,1,0:T(4,128)S(1)} %get-tuple-element.66.vec_ref, ...), custom_call_target="tpu_custom_call", output_to_operand_aliasing={{}: (5, {})} | custom-call | flops 1056964608 | bytes 6000000 | tf_op jit(solution)/shard_map/backward_stage/pallas_call | solution.py:318
  123.6 1.9 %collective-permute-done.12.g_ref = bf16[1,224,256]{2,1,0:T(8,128)(2,1)S(1)} collective-permute-done((bf16[1,224,256]{2,1,0:T(8,128)(2,1)S(1)}, bf16[1,224,256]{2,1,0:T(8,128)(2,1)S(1)}, u32[]{:S(2)}, u32[]{:S(2)}) %collective-permute-start.12) | collective-permute-done | bytes 114720 | tf_op jit(solution)/shard_map/ppermute | solution.py:449
  125.5 2.0 %backward_stage.11 = bf16[2,224,256]{2,1,0:T(8,128)(2,1)S(1)} custom-call(s32[1]{0:T(128)} %bitcast.1.rest_3_.flag, bf16[1,224,256]{2,1,0:T(8,128)(2,1)S(1)} %collective-permute-done.12.g_ref, bf16[2,2,2304,256]{3,2,1,0:T(8,128)(2,1)S(1)} %get-tuple-element.96.held, f32[2,3,256]{2,1,0:T(4,128)S(1)} %get-tuple-element.66.vec_ref, ...), custom_call_target="tpu_custom_call", output_to_operand_aliasing={{}: (5, {})} | custom-call | flops 1056964608 | bytes 6000000 | tf_op jit(solution)/shard_map/backward_stage/pallas_call | solution.py:318
  127.6 0.1 fusion.12
  127.6 0.2 copy.33
  127.8 8.4 %collective-permute-start.16 = (bf16[2,196,256]{2,0,1:T(2,128)(2,1)S(1)}, bf16[2,196,256]{2,0,1:T(2,128)(2,1)S(1)}, u32[]{:S(2)}, u32[]{:S(2)}) collective-permute-start(bf16[2,196,256]{2,0,1:T(2,128)(2,1)S(1)} %bitcast.50), channel_id=1, source_target_pairs={{0,64},{64,0},{128,192},{192,128},{256,320},{320,256},{384,448},{4... | collective-permute-start | bytes 602120 | tf_op jit(solution)/shard_map/ppermute | solution.py:457
  136.3 0.2 copy.32
  136.5 0.8 collective-permute-done.16
  137.3 0.3 broadcast_select_fusion.1
  137.7 1.2 maximum_bitcast_fusion
  (47 shorter events, 0.5 us)
Async XLA Ops:
  0.0 14.6 %copy-start = (bf16[4,1,196,256]{3,0,2,1:T(4,128)(2,1)S(1)}, bf16[4,1,196,256]{3,0,2,1:T(4,128)(2,1)}, u32[]{:S(2)}) copy-start(bf16[4,1,196,256]{3,0,2,1:T(4,128)(2,1)} %param.13) | copy-start | bytes 1204228
  0.0 15.4 %collective-permute-start = (bf16[2304,256]{1,0:T(8,128)(2,1)}, bf16[2304,256]{1,0:T(8,128)(2,1)S(1)}, u32[]{:S(2)}, u32[]{:S(2)}) collective-permute-start(bf16[2304,256]{1,0:T(8,128)(2,1)} %bitcast.41), channel_id=1, source_target_pairs={{0,64},{64,0},{128,192},{192,128},{256,320},{320,256},{384,448},{4... | collective-permute-start | bytes 3538952 | tf_op jit(solution)/shard_map/ppermute | solution.py:386
  8.9 6.6 %collective-permute-start.1 = (bf16[2304,256]{1,0:T(8,128)(2,1)}, bf16[2304,256]{1,0:T(8,128)(2,1)S(1)}, u32[]{:S(2)}, u32[]{:S(2)}) collective-permute-start(bf16[2304,256]{1,0:T(8,128)(2,1)} %bitcast.44), channel_id=1, source_target_pairs={{0,64},{64,0},{128,192},{192,128},{256,320},{320,256},{384,448},{4... | collective-permute-start | bytes 3538952 | tf_op jit(solution)/shard_map/ppermute | solution.py:386
  11.5 3.9 %collective-permute-start.2 = (f32[3,256]{1,0:T(4,128)S(1)}, f32[3,256]{1,0:T(4,128)S(1)}, u32[]{:S(2)}, u32[]{:S(2)}) collective-permute-start(f32[3,256]{1,0:T(4,128)S(1)} %pad_maximum_fusion.own_vec), channel_id=1, source_target_pairs={{0,64},{64,0},{128,192},{192,128},{256,320},{320,256},{384,448},{4... | collective-permute-start | bytes 9224 | tf_op jit(solution)/shard_map/ppermute | solution.py:389
  15.4 2.6 %copy-start.1 = (bf16[2304,256]{1,0:T(8,128)(2,1)}, bf16[2304,256]{1,0:T(8,128)(2,1)S(1)}, u32[]{:S(2)}) copy-start(bf16[2304,256]{1,0:T(8,128)(2,1)S(1)} %collective-permute-done.peer1.refs_2_) | copy-start | bytes 3538948
  15.5 2.6 %copy-start.2 = (bf16[2304,256]{1,0:T(8,128)(2,1)}, bf16[2304,256]{1,0:T(8,128)(2,1)S(1)}, u32[]{:S(2)}) copy-start(bf16[2304,256]{1,0:T(8,128)(2,1)S(1)} %collective-permute-done.1.peer2.refs_3_) | copy-start | bytes 3538948
  20.5 5.0 %collective-permute-start.6 = (bf16[1,224,256]{2,1,0:T(8,128)(2,1)S(1)}, bf16[1,224,256]{2,1,0:T(8,128)(2,1)S(1)}, u32[]{:S(2)}, u32[]{:S(2)}) collective-permute-start(bf16[1,224,256]{2,1,0:T(8,128)(2,1)S(1)} %get-tuple-element.71), channel_id=1, source_target_pairs={{0,128},{64,192},{1,129},{65,193},{2,130},{66,194},{3,131},{67,195... | collective-permute-start | bytes 344072 | tf_op jit(solution)/shard_map/ppermute | solution.py:411
  24.2 4.0 %collective-permute-start.3 = (bf16[1,224,256]{2,1,0:T(8,128)(2,1)S(1)}, bf16[1,224,256]{2,1,0:T(8,128)(2,1)S(1)}, u32[]{:S(2)}, u32[]{:S(2)}) collective-permute-start(bf16[1,224,256]{2,1,0:T(8,128)(2,1)S(1)} %get-tuple-element.67), channel_id=1, source_target_pairs={{0,128},{64,192},{1,129},{65,193},{2,130},{66,194},{3,131},{67,195... | collective-permute-start | bytes 344072 | tf_op jit(solution)/shard_map/ppermute | solution.py:411
  25.6 3.4 %collective-permute-start.7 = (bf16[1,224,256]{2,1,0:T(8,128)(2,1)S(1)}, bf16[1,224,256]{2,1,0:T(8,128)(2,1)S(1)}, u32[]{:S(2)}, u32[]{:S(2)}) collective-permute-start(bf16[1,224,256]{2,1,0:T(8,128)(2,1)S(1)} %get-tuple-element.72), channel_id=1, source_target_pairs={{128,256},{192,320},{129,257},{193,321},{130,258},{194,322},{131,2... | collective-permute-start | bytes 344072 | tf_op jit(solution)/shard_map/ppermute | solution.py:411
  28.3 1.5 %collective-permute-start.4 = (bf16[1,224,256]{2,1,0:T(8,128)(2,1)S(1)}, bf16[1,224,256]{2,1,0:T(8,128)(2,1)S(1)}, u32[]{:S(2)}, u32[]{:S(2)}) collective-permute-start(bf16[1,224,256]{2,1,0:T(8,128)(2,1)S(1)} %get-tuple-element.68), channel_id=1, source_target_pairs={{128,256},{192,320},{129,257},{193,321},{130,258},{194,322},{131,2... | collective-permute-start | bytes 344072 | tf_op jit(solution)/shard_map/ppermute | solution.py:411
  29.0 1.5 %copy-start.4 = (bf16[1664,512]{1,0:T(8,128)(2,1)S(1)}, bf16[1664,512]{1,0:T(8,128)(2,1)}, u32[]{:S(2)}) copy-start(bf16[1664,512]{1,0:T(8,128)(2,1)} %centres_ref.1) | copy-start | bytes 5111812
  29.0 2.0 %collective-permute-start.8 = (bf16[1,224,256]{2,1,0:T(8,128)(2,1)S(1)}, bf16[1,224,256]{2,1,0:T(8,128)(2,1)S(1)}, u32[]{:S(2)}, u32[]{:S(2)}) collective-permute-start(bf16[1,224,256]{2,1,0:T(8,128)(2,1)S(1)} %get-tuple-element.73), channel_id=1, source_target_pairs={{256,384},{320,448},{257,385},{321,449},{258,386},{322,450},{259,3... | collective-permute-start | bytes 344072 | tf_op jit(solution)/shard_map/ppermute | solution.py:411
  29.9 1.2 collective-permute-start.5
  31.0 1.1 copy-start.6
  60.7 21.2 %all-to-all-start.1 = ((bf16[64,2,512]{2,1,0:T(2,128)(2,1)}), bf16[64,2,512]{2,1,0:T(2,128)(2,1)S(1)}, u32[]{:S(2)}, u32[]{:S(2)}) async-start(bf16[64,2,512]{2,1,0:T(2,128)(2,1)} %get-tuple-element.77), calls=%async_computation.1 | async-start | bytes 262144 | tf_op jit(solution)/shard_map/all_to_all | solution.py:434
  82.0 11.1 %copy-start.5 = (bf16[196,256]{1,0:T(8,128)(2,1)S(1)}, bf16[196,256]{1,0:T(8,128)(2,1)}, u32[]{:S(2)}) copy-start(bf16[196,256]{1,0:T(8,128)(2,1)} %pool.1) | copy-start | bytes 301060
  82.9 24.7 %copy-start.3 = (bf16[256,512]{1,0:T(8,128)(2,1)S(1)}, bf16[256,512]{1,0:T(8,128)(2,1)}, u32[]{:S(2)}) copy-start(bf16[256,512]{1,0:T(8,128)(2,1)} %embed_ref) | copy-start | bytes 786436
  83.7 23.8 %all-to-all-start.2 = ((bf16[64,2,640]{2,1,0:T(2,128)(2,1)}), bf16[64,2,640]{2,1,0:T(2,128)(2,1)S(1)}, u32[]{:S(2)}, u32[]{:S(2)}) async-start(bf16[64,2,640]{2,1,0:T(2,128)(2,1)} %reshape.125), calls=%async_computation.2 | async-start | bytes 327680 | tf_op jit(solution)/shard_map/all_to_all | solution.py:437
  93.1 14.5 %collective-permute-start.9 = (bf16[2,512]{1,0:T(2,128)(2,1)S(1)}, bf16[2,512]{1,0:T(2,128)(2,1)S(1)}, u32[]{:S(2)}, u32[]{:S(2)}) collective-permute-start(bf16[2,512]{1,0:T(2,128)(2,1)S(1)} %get-tuple-element.130), channel_id=1, source_target_pairs={{0,384},{64,448},{1,385},{65,449},{2,386},{66,450},{3,387},{67,451... | collective-permute-start | bytes 6152 | tf_op jit(solution)/shard_map/ppermute | solution.py:433
  111.0 1.4 %collective-permute-start.13 = (bf16[1,224,256]{2,1,0:T(8,128)(2,1)S(1)}, bf16[1,224,256]{2,1,0:T(8,128)(2,1)S(1)}, u32[]{:S(2)}, u32[]{:S(2)}) collective-permute-start(bf16[1,224,256]{2,1,0:T(8,128)(2,1)S(1)} %get-tuple-element.104), channel_id=1, source_target_pairs={{384,256},{448,320},{385,257},{449,321},{386,258},{450,322},{387,2... | collective-permute-start | bytes 344072 | tf_op jit(solution)/shard_map/ppermute | solution.py:449
  111.7 1.4 collective-permute-start.10
  112.4 1.4 collective-permute-start.14
  113.1 2.0 %collective-permute-start.11 = (bf16[1,224,256]{2,1,0:T(8,128)(2,1)S(1)}, bf16[1,224,256]{2,1,0:T(8,128)(2,1)S(1)}, u32[]{:S(2)}, u32[]{:S(2)}) collective-permute-start(bf16[1,224,256]{2,1,0:T(8,128)(2,1)S(1)} %get-tuple-element.100), channel_id=1, source_target_pairs={{256,128},{320,192},{257,129},{321,193},{258,130},{322,194},{259,1... | collective-permute-start | bytes 344072 | tf_op jit(solution)/shard_map/ppermute | solution.py:449
  113.8 7.8 %collective-permute-start.15 = (bf16[1,224,256]{2,1,0:T(8,128)(2,1)S(1)}, bf16[1,224,256]{2,1,0:T(8,128)(2,1)S(1)}, u32[]{:S(2)}, u32[]{:S(2)}) collective-permute-start(bf16[1,224,256]{2,1,0:T(8,128)(2,1)S(1)} %get-tuple-element.108), channel_id=1, source_target_pairs={{128,0},{192,64},{129,1},{193,65},{130,2},{194,66},{131,3},{195,67... | collective-permute-start | bytes 344072 | tf_op jit(solution)/shard_map/ppermute | solution.py:449
  115.1 10.4 %collective-permute-start.12 = (bf16[1,224,256]{2,1,0:T(8,128)(2,1)S(1)}, bf16[1,224,256]{2,1,0:T(8,128)(2,1)S(1)}, u32[]{:S(2)}, u32[]{:S(2)}) collective-permute-start(bf16[1,224,256]{2,1,0:T(8,128)(2,1)S(1)} %get-tuple-element.102), channel_id=1, source_target_pairs={{128,0},{192,64},{129,1},{193,65},{130,2},{194,66},{131,3},{195,67... | collective-permute-start | bytes 344072 | tf_op jit(solution)/shard_map/ppermute | solution.py:449
  127.8 9.5 %collective-permute-start.16 = (bf16[2,196,256]{2,0,1:T(2,128)(2,1)S(1)}, bf16[2,196,256]{2,0,1:T(2,128)(2,1)S(1)}, u32[]{:S(2)}, u32[]{:S(2)}) collective-permute-start(bf16[2,196,256]{2,0,1:T(2,128)(2,1)S(1)} %bitcast.50), channel_id=1, source_target_pairs={{0,64},{64,0},{128,192},{192,128},{256,320},{320,256},{384,448},{4... | collective-permute-start | bytes 602120 | tf_op jit(solution)/shard_map/ppermute | solution.py:457

commit v7 on v6

--- a/solution.py
+++ b/solution.py
@@ -7,6 +7,7 @@
 from jax.experimental import pallas as pl
 from jax.experimental.pallas import tpu as pltpu
 from jax.sharding import PartitionSpec as P
+
 
 SIDE = 14
 WIDE = 16
@@ -59,14 +60,28 @@
 HALVES = tuple(slice(h * HALF, (h + 1) * HALF) for h in range(2))
 
 
+def start_unit(core, u, own, peer, held, sems):
+    @pl.when(core == u)
+    def _():
+        for k, source in enumerate(own):
+            pltpu.make_async_copy(source, held.at[u, k], sems.at[k]).start()
+
+    @pl.when(core != u)
+    def _():
+        for k, source in enumerate(peer):
+            pltpu.make_async_copy(source, held.at[u, k], sems.at[k]).start()
+
+
+def wait_unit(u, own, held, sems):
+    for k, source in enumerate(own):
+        pltpu.make_async_copy(source, held.at[u, k], sems.at[k]).wait()
+
+
 def load_body(flag, own1, own2, peer1, peer2, own_vec, peer_vec, pool, embed, *rest):
     held, vec, pool_out, embed_out, sems, more = rest[-6:]
     core = flag[0]
+    start_unit(core, 0, (own1, own2), (peer1, peer2), held, sems)
     copies = [
-        pltpu.make_async_copy(source, held.at[place, k], sems.at[side, k])
-        for side, place, pair in ((0, core, (own1, own2)), (1, 1 - core, (peer1, peer2)))
-        for k, source in enumerate(pair)
-    ] + [
         pltpu.make_async_copy(pool, pool_out, more.at[0]),
         pltpu.make_async_copy(embed, embed_out, more.at[1]),
     ]
@@ -74,6 +89,7 @@
         copy.start()
     vec[core] = own_vec[...]
     vec[1 - core] = peer_vec[...]
+    wait_unit(0, (own1, own2), held, sems)
     for copy in copies:
         copy.wait()
 
@@ -141,7 +157,15 @@
     )(unit_half, centres, scale, labels, ids, *in_hbm(*after))
 
 
-def forward_body(flag, x_ref, held, vec_ref, out_ref, z_ref, cols, run, zed, zsem):
+def forward_body(first, flag, x_ref, held_in, vec_ref, *rest):
+    if first:
+        own, peer, held, sems = rest[0:2], rest[2:4], rest[4], rest[-1]
+        rest = rest[5:-1]
+        start_unit(flag[1], 1, own, peer, held, sems)
+    else:
+        held = held_in
+    out_ref, z_ref, cols, run, zed, zsem = rest
+
     @pl.when(flag[0] == 1)
     def _():
         clear_border(cols)
@@ -152,6 +176,8 @@
             vec = vec_ref[u]
             for h in HALVES:
                 build(run[h], cols.at[0], h.start)
+            if first:
+                pl.when(u == 1)(lambda: wait_unit(1, own, held, sems))
             for h in HALVES:
                 pre = conv(cols.at[0], held.at[u, 0], h.start) * vec[0:1] + vec[1:2]
                 zed[u, h] = pre.astype(jnp.bfloat16)
@@ -171,8 +197,20 @@
         for u in range(2):
             pltpu.make_async_copy(zed.at[u], z_ref.at[u], zsem.at[u]).wait()
 
-
-def backward_body(image, flag, g_ref, held, vec_ref, z_ref, store_in, *rest):
+    if first:
+
+        @pl.when(flag[0] != 1)
+        def _():
+            wait_unit(1, own, held, sems)
+
+
+def backward_body(image, first, flag, g_ref, held_in, vec_ref, z_ref, store_in, *rest):
+    if first:
+        own, peer, held, sems = rest[0:2], rest[2:4], rest[4], rest[-1]
+        rest = rest[5:-1]
+        start_unit(flag[1], 0, own, peer, held, sems)
+    else:
+        held = held_in
     store, cols, run = rest[-3:]
 
     @pl.when(flag[0] == 1)
@@ -189,6 +227,8 @@
             gain = half * (1.0 - vec[2:3])
             for h in HALVES:
                 build(run[h], cols.at[0], h.start)
+            if first:
+                pl.when(u == 0)(lambda: wait_unit(0, own, held, sems))
             for h in HALVES:
                 slope = base + gain * jnp.tanh(2.0 * z_ref[image, u, h].astype(jnp.float32))
                 hidden = conv(cols.at[0], held.at[u, 1], h.start) * slope
@@ -204,20 +244,20 @@
         if len(rest) == 4:
             rest[0][0] = run[...].astype(jnp.bfloat16)
 
+    if first:
+
+        @pl.when(flag[0] != 1)
+        def _():
+            wait_unit(0, own, held, sems)
+
 
 def tail_body(
     flag, sums_ref, chosen_ref, embedded_ref, embed_ref, pool_ref, own1, own2, peer1, peer2, *rest
 ):
-    saved, (g_ref, held, zbuf, sems, zsems) = rest[:-5], rest[-5:]
+    saved, (first_g, second_g, held, zbuf, sems, zsems) = rest[:-6], rest[-6:]
     images = zbuf.shape[0]
     core, plane = flag[0], flag[1]
-    copies = [
-        pltpu.make_async_copy(source, held.at[place, k], sems.at[side, k])
-        for side, place, pair in ((0, core, (own1, own2)), (1, 1 - core, (peer1, peer2)))
-        for k, source in enumerate(pair)
-    ]
-    for copy in copies:
-        copy.start()
+    start_unit(core, 1, (own1, own2), (peer1, peer2), held, sems)
     for s in range(len(saved) // images):
 
         @pl.when(plane == s)
@@ -239,10 +279,9 @@
         (((1,), (1,)), ((), ())),
         preferred_element_type=jnp.float32,
     )
-    for m in range(images):
-        g_ref[m] = (grad_pooled[m : m + 1] * pool_ref[...]).astype(jnp.bfloat16)
-    for copy in copies:
-        copy.wait()
+    for m, g_ref in enumerate((first_g, second_g)):
+        g_ref[0] = (grad_pooled[m : m + 1] * pool_ref[...]).astype(jnp.bfloat16)
+    wait_unit(1, (own1, own2), held, sems)
     for m in range(images):
         pltpu.make_async_copy(saved[m], zbuf.at[m], zsems.at[m]).wait()
 
@@ -252,13 +291,14 @@
     return pl.pallas_call(
         tail_body,
         in_specs=[SM, VM, VM, VM, VM, VM] + [HB] * (len(weights) + len(saved)),
-        out_specs=[VM, VM, VM],
+        out_specs=[VM] * 4,
         out_shape=[
-            jax.ShapeDtypeStruct((images, ROWS, C), jnp.bfloat16),
+            jax.ShapeDtypeStruct((1, ROWS, C), jnp.bfloat16),
+            jax.ShapeDtypeStruct((1, ROWS, C), jnp.bfloat16),
             jax.ShapeDtypeStruct((2, 2, *weights[0].shape), weights[0].dtype),
             jax.ShapeDtypeStruct((images, 2, ROWS, C), jnp.bfloat16),
         ],
-        scratch_shapes=[pltpu.SemaphoreType.DMA((2, 2)), pltpu.SemaphoreType.DMA((images,))],
+        scratch_shapes=[pltpu.SemaphoreType.DMA((2,)), pltpu.SemaphoreType.DMA((images,))],
         compiler_params=pltpu.CompilerParams(vmem_limit_bytes=STAGE_LIMIT),
         cost_estimate=pl.CostEstimate(flops=300_000_000, bytes_accessed=9_000_000, transcendentals=0),
         name="tail",
@@ -290,43 +330,53 @@
             jax.ShapeDtypeStruct(pool.shape, pool.dtype),
             jax.ShapeDtypeStruct(embed.shape, embed.dtype),
         ],
-        scratch_shapes=[pltpu.SemaphoreType.DMA((2, 2)), pltpu.SemaphoreType.DMA((2,))],
+        scratch_shapes=[pltpu.SemaphoreType.DMA((2,)), pltpu.SemaphoreType.DMA((2,))],
         compiler_params=pltpu.CompilerParams(vmem_limit_bytes=STAGE_LIMIT),
         cost_estimate=pl.CostEstimate(flops=300_000_000, bytes_accessed=9_000_000, transcendentals=0),
         name="load_weights",
     )(core, *in_hbm(*weights[:2]), *weights[2:], own_vec, peer_vec, *in_hbm(pool, embed), *before)
 
 
-def forward_stage(flag, x, held, vec):
-    return pl.pallas_call(
-        forward_body,
-        in_specs=[SM, VM, VM, VM],
-        out_specs=[VM, HB],
-        out_shape=[
+def forward_stage(flag, x, held, vec, weights=()):
+    first = len(weights) > 0
+    outs = pl.pallas_call(
+        functools.partial(forward_body, first),
+        in_specs=[SM, VM, VM, VM] + [HB] * len(weights),
+        out_specs=[VM] * first + [VM, HB],
+        out_shape=[jax.ShapeDtypeStruct(held.shape, held.dtype)] * first
+        + [
             jax.ShapeDtypeStruct(x.shape, jnp.bfloat16),
             pltpu.HBM((2, ROWS, C), jnp.bfloat16),
         ],
-        scratch_shapes=STAGE_SCRATCH,
+        scratch_shapes=STAGE_SCRATCH + [pltpu.SemaphoreType.DMA((2,))] * first,
+        input_output_aliases={2: 0} if first else {},
         compiler_params=pltpu.CompilerParams(vmem_limit_bytes=STAGE_LIMIT),
         cost_estimate=CONV_COST,
         name="forward_stage",
-    )(flag, x, held, vec)
-
-
-def backward_stage(image, last, flag, g, held, vec, z, store):
-    passed = [] if last else [jax.ShapeDtypeStruct(g.shape, jnp.bfloat16)]
+    )(flag, x, held, vec, *in_hbm(*weights))
+    return (outs[0] if first else held), outs[-2], outs[-1]
+
+
+def backward_stage(image, last, flag, g, held, vec, z, store, weights=()):
+    first = len(weights) > 0
+    shapes = [jax.ShapeDtypeStruct(held.shape, held.dtype)] * first
+    shapes += [] if last else [jax.ShapeDtypeStruct(g.shape, jnp.bfloat16)]
+    shapes += [jax.ShapeDtypeStruct(store.shape, store.dtype)]
+    aliases = {5: len(shapes) - 1}
+    if first:
+        aliases[2] = 0
     outs = pl.pallas_call(
-        functools.partial(backward_body, image),
-        in_specs=[SM, VM, VM, VM, VM, VM],
-        out_specs=[VM] * (len(passed) + 1),
-        out_shape=passed + [jax.ShapeDtypeStruct(store.shape, store.dtype)],
-        scratch_shapes=STAGE_SCRATCH[:2],
-        input_output_aliases={5: len(passed)},
+        functools.partial(backward_body, image, first),
+        in_specs=[SM, VM, VM, VM, VM, VM] + [HB] * len(weights),
+        out_specs=[VM] * len(shapes),
+        out_shape=shapes,
+        scratch_shapes=STAGE_SCRATCH[:2] + [pltpu.SemaphoreType.DMA((2,))] * first,
+        input_output_aliases=aliases,
         compiler_params=pltpu.CompilerParams(vmem_limit_bytes=STAGE_LIMIT),
         cost_estimate=CONV_COST,
         name="backward_stage",
-    )(flag, g, held, vec, z, store)
-    return outs[0], outs[-1]
+    )(flag, g, held, vec, z, store, *in_hbm(*weights))
+    return (outs[0] if first else held), (None if last else outs[-2]), outs[-1]
 
 
 def flip_body(*refs):
@@ -399,16 +449,22 @@
     flips = flip_all(weights)
     parts = [x[m : m + 1] for m in range(micro)]
     mine_at, other_at = core.astype(jnp.uint32), (1 - core).astype(jnp.uint32)
+    opening = jnp.stack([flags[0][0], core])
+    closing = jnp.stack([flags[planes - 1][0], core])
     class_ids = class_offsets[0] + jnp.arange(class_centers.shape[0], dtype=jnp.int32)
     held, vec, pool_compact, embed_ready = load_weights(
-        core.reshape(1), weights, own_vec, peer_vec, depthwise, embed_weight, (*parts, class_ids, *flags, mine_at.reshape(1), other_at.reshape(1))
+        core.reshape(1), weights, own_vec, peer_vec, depthwise, embed_weight, (*parts, class_ids, *flags, opening, closing, mine_at.reshape(1), other_at.reshape(1))
     )
     saved = {}
     for s in range(planes):
-        for m in range(micro):
-            parts[m], saved[s, m] = forward_stage(flags[s], parts[m], held, vec)
+        for m in reversed(range(micro)):
+            lead = s == 0 and m == micro - 1
+            held, parts[m], saved[s, m] = forward_stage(
+                opening if lead else flags[s], parts[m], held, vec, weights if lead else ()
+            )
             if s < planes - 1:
-                parts[m] = lax.ppermute(parts[m], "section", [(2 * s + c, 2 * s + 2 + c) for c in range(2)])
+                pairs = [(2 * s + c, 2 * s + 2 + c) for c in range(2)]
+                parts[m] = lax.ppermute(parts[m], "section", pairs)
     embedded, sent = pool_and_embed(parts, pool_compact, embed_ready, shards)
     width = embedded.shape[-1]
     embedded, depthwise, embed_weight, labels = lax.optimization_barrier(
@@ -436,17 +492,21 @@
     sums = class_sums(unit_half, class_centers, scale, my_labels(), class_ids[None, :], flips)
     sums = lax.all_to_all(sums.reshape(shards, micro, -1), "shard", 0, 0, tiled=True)
     sums = jnp.sum(sums.astype(jnp.float32), axis=0)
-    g, flips, zbuf = tail(
+    *parts, held, zbuf = tail(
         jnp.stack([core, plane]), sums, chosen, embedded, embed_weight, pool_weight, flips,
         [saved[s, m] for s in range(planes) for m in range(micro)],
     )
-    parts = [g[m : m + 1] for m in range(micro)]
-    stores = [jnp.zeros((2, ROWS, C), jnp.bfloat16) for m in range(micro)]
+    stores = [jnp.zeros((2, ROWS, C), jnp.bfloat16) for _ in range(micro)]
     for s in reversed(range(planes)):
-        for m in range(micro):
-            parts[m], stores[m] = backward_stage(m, s == 0, flags[s], parts[m], flips, vec, zbuf, stores[m])
+        for m in reversed(range(micro)):
+            lead = s == planes - 1 and m == micro - 1
+            held, parts[m], stores[m] = backward_stage(
+                m, s == 0, closing if lead else flags[s], parts[m], held, vec, zbuf, stores[m],
+                flips if lead else (),
+            )
             if s > 0:
-                parts[m] = lax.ppermute(parts[m], "section", [(2 * s + c, 2 * s - 2 + c) for c in range(2)])
+                pairs = [(2 * s + c, 2 * s - 2 + c) for c in range(2)]
+                parts[m] = lax.ppermute(parts[m], "section", pairs)
     store = jnp.stack(stores, axis=1)
 
     def narrowed(rows):

time: 140 us -> 145 us (1.036)
  waiting for transfers between devices: 28.1 us -> 30.8 us
  Pallas kernels: 25.4 us -> 27.2 us
    pallas_call x16, Pallas kernels: 9.13 us -> 12.4 us  [the longest x8 6.34 us: backward_stage(): pl.pallas_call(functools.partial(backward_body, image, first), in_specs=[...]
    ppermute x12, waiting for transfers between devices: 9.06 us -> 12 us  [on_device(): parts[m] = lax.ppermute(parts[m], 'section', pairs)]
  transfers between devices with their start and end apart: 19 -> 19, of which waited for: 6 -> 7; matrix products, arithmetic and copies ran while one was open for 2% -> 2% of each run, Pallas kernels for 9% -> 7%
where the time goes in v7:
time: 145 us; the launch traced here: 144 us
  starting transfers between devices  51.3 us (35%)
  waiting for transfers between devices  30.8 us (21%)
  Pallas kernels  27.2 us (19%)
  blocking collectives  26.7 us (18%)
  other arithmetic  3.61 us (2%)
  local copies, waits for them, and re-layouts  2.61 us (2%)
    all_to_all x1, blocking collectives, label_rows(): lax.all_to_all(rows.reshape(shards, micro, width), 'shard', 0, 0, tiled=T...  26.7 us
    all_to_all x1, waiting for transfers between devices, on_device(): lax.all_to_all(sums.reshape(shards, micro, -1), 'shard', 0, 0, tiled=True)  12.7 us
    ppermute x12, waiting for transfers between devices, on_device(): parts[m] = lax.ppermute(parts[m], 'section', pairs)  12 us
    ppermute x2, starting transfers between devices, on_device(): peer = tuple((lax.ppermute(w, 'section', swap) for w in own))  10.8 us
    ppermute x12, starting transfers between devices, on_device(): parts[m] = lax.ppermute(parts[m], 'section', pairs)  10.7 us
    ppermute x1, starting transfers between devices, on_device(): taken = lax.ppermute(given, 'section', swap)  9.67 us
    all_to_all x1, starting transfers between devices, on_device(): lax.all_to_all(sums.reshape(shards, micro, -1), 'shard', 0, 0, tiled=True)  9.35 us
    pallas_call x1, Pallas kernels, flip_all(): pl.pallas_call(flip_body, grid=(9,), in_specs=[pl.BlockSpec((C, C), lambd...  8.51 us
  transfers between devices with their start and end apart: 19, of which 7 were waited for; matrix products, arithmetic and copies ran while one was open for 2% of the time, Pallas kernels for 7%

profile of v7, /device:TPU:1, one launch (start us, length us, event | category | flops | bytes accessed | tf_op | source)
XLA Modules:
  0.0 144.1 jit_solution(8901803145588509155)
XLA Ops:
  0.0 8.9 %collective-permute-start = (bf16[2304,256]{1,0:T(8,128)(2,1)}, bf16[2304,256]{1,0:T(8,128)(2,1)S(1)}, u32[]{:S(2)}, u32[]{:S(2)}) collective-permute-start(bf16[2304,256]{1,0:T(8,128)(2,1)} %bitcast.41), channel_id=1, source_target_pairs={{0,64},{64,0},{128,192},{192,128},{256,320},{320,256},{384,448},{4... | collective-permute-start | bytes 3538952 | tf_op jit(solution)/shard_map/ppermute | solution.py:436
  8.9 1.9 %collective-permute-start.1 = (bf16[2304,256]{1,0:T(8,128)(2,1)}, bf16[2304,256]{1,0:T(8,128)(2,1)S(1)}, u32[]{:S(2)}, u32[]{:S(2)}) collective-permute-start(bf16[2304,256]{1,0:T(8,128)(2,1)} %bitcast.45), channel_id=1, source_target_pairs={{0,64},{64,0},{128,192},{192,128},{256,320},{320,256},{384,448},{4... | collective-permute-start | bytes 3538952 | tf_op jit(solution)/shard_map/ppermute | solution.py:436
  10.8 0.7 pad_maximum_fusion.own_vec
  11.5 2.4 %collective-permute-start.2 = (f32[3,256]{1,0:T(4,128)S(1)}, f32[3,256]{1,0:T(4,128)S(1)}, u32[]{:S(2)}, u32[]{:S(2)}) collective-permute-start(f32[3,256]{1,0:T(4,128)S(1)} %pad_maximum_fusion.own_vec), channel_id=1, source_target_pairs={{0,64},{64,0},{128,192},{192,128},{256,320},{320,256},{384,448},{4... | collective-permute-start | bytes 9224 | tf_op jit(solution)/shard_map/ppermute | solution.py:439
  14.6 0.2 constant_dynamic-slice_fusion
  14.9 0.5 pad_slice_fusion
  15.3 0.1 pad_add_fusion.1
  15.5 1.8 %load_weights.1 = (bf16[2,2,2304,256]{3,2,1,0:T(8,128)(2,1)S(1)}, f32[2,3,256]{2,1,0:T(4,128)S(1)}, bf16[196,256]{1,0:T(8,128)(2,1)S(1)}, bf16[256,512]{1,0:T(8,128)(2,1)S(1)}) custom-call(s32[1]{0:T(128)} %bitcast.5.flag, bf16[2304,256]{1,0:T(8,128)(2,1)} %bitcast.42, bf16[2304,256]{1,0:T(8,128)(2,1)} %bitcast.46, ...), custom_call_target="tpu_custom_call" | custom-call | flops 300000000 | bytes 9000000 | tf_op jit(solution)/shard_map/load_weights/pallas_call | solution.py:323
  17.4 3.5 %forward_stage.8 = (bf16[2,2,2304,256]{3,2,1,0:T(8,128)(2,1)S(1)}, bf16[1,224,256]{2,1,0:T(8,128)(2,1)S(1)}, bf16[2,224,256]{2,1,0:T(8,128)(2,1)}) custom-call(s32[2]{0:T(128)S(1)} %get-tuple-element.134.rest_7_.flag, bf16[1,224,256]{2,1,0:T(8,128)(2,1)S(1)} %bitcast.38, ...), custom_call_target="tpu_custom_call", output_to_operand_aliasing={{0}: (2, {})} | custom-call | flops 1056964608 | bytes 6000000 | tf_op jit(solution)/shard_map/forward_stage/pallas_call | solution.py:342
  20.9 2.4 %forward_stage.9 = (bf16[1,224,256]{2,1,0:T(8,128)(2,1)S(1)}, bf16[2,224,256]{2,1,0:T(8,128)(2,1)}) custom-call(s32[1]{0:T(128)} %bitcast.1.rest_3_.flag, bf16[1,224,256]{2,1,0:T(8,128)(2,1)S(1)} %bitcast.40, bf16[2,2,2304,256]{3,2,1,0:T(8,128)(2,1)S(1)} %get-tuple-element.70.held_in, f32[2,3,256]{2,1,0:T(4,128)S(1)} %get-tuple-element.69.vec_ref), custom_call_target="tpu_custom_call" | custom-call | flops 1056964608 | bytes 6000000 | tf_op jit(solution)/shard_map/forward_stage/pallas_call | solution.py:342
  23.3 1.3 collective-permute-start.3
  24.6 1.3 collective-permute-start.6
  25.9 0.7 collective-permute-done.3.x_ref
  26.6 0.7 collective-permute-start.4
  27.3 1.8 %collective-permute-done.6.x_ref = bf16[1,224,256]{2,1,0:T(8,128)(2,1)S(1)} collective-permute-done((bf16[1,224,256]{2,1,0:T(8,128)(2,1)S(1)}, bf16[1,224,256]{2,1,0:T(8,128)(2,1)S(1)}, u32[]{:S(2)}, u32[]{:S(2)}) %collective-permute-start.6) | collective-permute-done | bytes 114720 | tf_op jit(solution)/shard_map/ppermute | solution.py:467
  29.1 0.7 collective-permute-start.7
  29.8 0.0 copy-start.4
  29.8 0.8 collective-permute-start.5
  30.6 0.7 collective-permute-start.8
  31.3 0.4 multiply_reduce_fusion
  31.8 0.0 copy-start.6
  31.8 1.0 pool_and_embed.1
  32.9 28.3 %conditional.1 = (bf16[2,512]{1,0:T(2,128)(2,1)S(1)}) conditional(s32[]{:T(128)} %convert_element_type.41, () %tuple.13, (s32[]{:T(128)}, s32[4,64]{1,0:T(4,128)S(1)}, s32[1664]{0:T(1024)S(1)}, bf16[1664,512]{1,0:T(8,128)(2,1)S(1)}) %tuple.25), branch_computations={%region_2.3_spmd, %region_3.6_spmd} | conditional | flops 223561984 | bytes 4234300 | solution.py:488
  32.9 0.4 fusion
  33.3 0.1 copy.33
  33.4 0.1 dynamic-slice_bitcast_fusion
  33.4 0.1 eq.6
  33.6 0.6 fusion.5
  34.2 0.1 reshape.94
  34.3 26.7 %all_to_all.14 = bf16[64,2,512]{2,1,0:T(2,128)(2,1)S(1)} all-to-all(bf16[64,2,512]{2,1,0:T(2,128)(2,1)S(1)} %reshape.94), channel_id=1, replica_groups=mesh['section'=8,'shard'=64] {'shard'}, dimensions={0} | all-to-all | bytes 262144 | tf_op jit(solution)/shard_map/cond/branch_1_fun/all_to_all | solution.py:485
  61.0 0.1 reduce_sum.36
  61.1 7.1 %all-to-all-start.1 = ((bf16[64,2,512]{2,1,0:T(2,128)(2,1)}), bf16[64,2,512]{2,1,0:T(2,128)(2,1)S(1)}, u32[]{:S(2)}, u32[]{:S(2)}) async-start(bf16[64,2,512]{2,1,0:T(2,128)(2,1)} %get-tuple-element.81), calls=%async_computation.1 | async-start | bytes 262144 | tf_op jit(solution)/shard_map/all_to_all | solution.py:490
  68.3 8.5 %flip_all.1 = (bf16[2304,256]{1,0:T(8,128)(2,1)}, bf16[2304,256]{1,0:T(8,128)(2,1)}, bf16[2304,256]{1,0:T(8,128)(2,1)}, bf16[2304,256]{1,0:T(8,128)(2,1)}) custom-call(bf16[2304,256]{1,0:T(8,128)(2,1)} %bitcast.44, bf16[2304,256]{1,0:T(8,128)(2,1)} %bitcast.48, bf16[2304,256]{1,0:T(8,128)(2,1)} %copy-done.1, bf16[2304,256]{1,0:T(8,128)(2,1)} %copy-done.2), custom_call_target="tpu_custom_call" | custom-call | flops 1207959552 | bytes 9000000 | tf_op jit(solution)/shard_map/flip_all/pallas_call | solution.py:396
  76.8 0.1 copy.31
  76.9 0.1 reshape.138.labels_ref
  77.0 5.2 %all-to-all-done.1 = bf16[64,2,512]{2,1,0:T(2,128)(2,1)S(1)} async-done(((bf16[64,2,512]{2,1,0:T(2,128)(2,1)}), bf16[64,2,512]{2,1,0:T(2,128)(2,1)S(1)}, u32[]{:S(2)}, u32[]{:S(2)}) %all-to-all-start.1) | async-done | bytes 131104 | tf_op jit(solution)/shard_map/all_to_all | solution.py:490
  82.2 0.1 reshape.123.unit_ref
  82.3 0.0 copy-start.5
  82.3 1.0 class_sums.1
  83.2 0.7 reshape.125
  84.0 9.4 %all-to-all-start.2 = ((bf16[64,2,640]{2,1,0:T(2,128)(2,1)}), bf16[64,2,640]{2,1,0:T(2,128)(2,1)S(1)}, u32[]{:S(2)}, u32[]{:S(2)}) async-start(bf16[64,2,640]{2,1,0:T(2,128)(2,1)} %reshape.125), calls=%async_computation.2 | async-start | bytes 327680 | tf_op jit(solution)/shard_map/all_to_all | solution.py:493
  93.3 0.1 pad_add_fusion.flag
  93.4 1.3 collective-permute-start.9
  94.8 12.7 %all-to-all-done.2 = bf16[64,2,640]{2,1,0:T(2,128)(2,1)S(1)} async-done(((bf16[64,2,640]{2,1,0:T(2,128)(2,1)}), bf16[64,2,640]{2,1,0:T(2,128)(2,1)S(1)}, u32[]{:S(2)}, u32[]{:S(2)}) %all-to-all-start.2) | async-done | bytes 163872 | tf_op jit(solution)/shard_map/all_to_all | solution.py:493
  107.5 0.2 convert_reduce_fusion.sums_ref
  107.7 2.5 %tail.1 = (bf16[1,224,256]{2,1,0:T(8,128)(2,1)S(1)}, bf16[1,224,256]{2,1,0:T(8,128)(2,1)S(1)}, bf16[2,2,2304,256]{3,2,1,0:T(8,128)(2,1)S(1)}, bf16[2,2,224,256]{3,2,1,0:T(8,128)(2,1)S(1)}) custom-call(s32[2]{0:T(128)S(1)} %pad_add_fusion.flag, f32[2,640]{1,0:T(2,128)S(1)} %convert_reduce_fusion.sums_ref, ...), custom_call_target="tpu_custom_call" | custom-call | flops 300000000 | bytes 9000000 | tf_op jit(solution)/shard_map/tail/pallas_call | solution.py:291
  110.2 2.2 %backward_stage.8 = (bf16[2,2,2304,256]{3,2,1,0:T(8,128)(2,1)S(1)}, bf16[1,224,256]{2,1,0:T(8,128)(2,1)S(1)}, bf16[2,224,256]{2,1,0:T(8,128)(2,1)S(1)}) custom-call(s32[2]{0:T(128)S(1)} %get-tuple-element.135.rest_8_.flag, bf16[1,224,256]{2,1,0:T(8,128)(2,1)S(1)} %get-tuple-element.100.g_ref, ...), custom_call_target="tpu_custom_call", output_to_operand_aliasing={{2}: (5, {}), {0}: (2, {})} | custom-call | flops 1056964608 | bytes 6000000 | tf_op jit(solution)/shard_map/backward_stage/pallas_call | solution.py:368
  112.5 0.7 collective-permute-start.10
  113.1 0.7 collective-permute-start.13
  113.9 0.7 collective-permute-start.11
  114.6 0.7 collective-permute-start.14
  115.3 1.3 collective-permute-start.12
  116.6 1.3 collective-permute-start.15
  117.9 8.2 %collective-permute-done.12.g_ref = bf16[1,224,256]{2,1,0:T(8,128)(2,1)S(1)} collective-permute-done((bf16[1,224,256]{2,1,0:T(8,128)(2,1)S(1)}, bf16[1,224,256]{2,1,0:T(8,128)(2,1)S(1)}, u32[]{:S(2)}, u32[]{:S(2)}) %collective-permute-start.12) | collective-permute-done | bytes 114720 | tf_op jit(solution)/shard_map/ppermute | solution.py:509
  126.1 2.0 %backward_stage.12 = bf16[2,224,256]{2,1,0:T(8,128)(2,1)S(1)} custom-call(s32[1]{0:T(128)} %bitcast.1.rest_3_.flag, bf16[1,224,256]{2,1,0:T(8,128)(2,1)S(1)} %collective-permute-done.12.g_ref, bf16[2,2,2304,256]{3,2,1,0:T(8,128)(2,1)S(1)} %get-tuple-element.103.held_in, f32[2,3,256]{2,1,0:T(4,128)S(1)} %get-tuple-element.69.vec_ref, ...), custom_call_target="tpu_custom_call", output_to_operand_aliasing={{}: (5, {})} | custom-call | flops 1056964608 | bytes 6000000 | tf_op jit(solution)/shard_map/backward_stage/pallas_call | solution.py:368
  128.2 1.3 collective-permute-done.15.g_ref
  129.5 2.0 %backward_stage.15 = bf16[2,224,256]{2,1,0:T(8,128)(2,1)S(1)} custom-call(s32[1]{0:T(128)} %bitcast.1.rest_3_.flag, bf16[1,224,256]{2,1,0:T(8,128)(2,1)S(1)} %collective-permute-done.15.g_ref, bf16[2,2,2304,256]{3,2,1,0:T(8,128)(2,1)S(1)} %get-tuple-element.103.held_in, f32[2,3,256]{2,1,0:T(4,128)S(1)} %get-tuple-element.69.vec_ref, ...), custom_call_target="tpu_custom_call", output_to_operand_aliasing={{}: (5, {})} | custom-call | flops 1056964608 | bytes 6000000 | tf_op jit(solution)/shard_map/backward_stage/pallas_call | solution.py:368
  131.5 0.1 fusion.12
  131.6 0.2 copy.35
  131.8 9.7 %collective-permute-start.16 = (bf16[2,196,256]{2,0,1:T(2,128)(2,1)S(1)}, bf16[2,196,256]{2,0,1:T(2,128)(2,1)S(1)}, u32[]{:S(2)}, u32[]{:S(2)}) collective-permute-start(bf16[2,196,256]{2,0,1:T(2,128)(2,1)S(1)} %bitcast.52), channel_id=1, source_target_pairs={{0,64},{64,0},{128,192},{192,128},{256,320},{320,256},{384,448},{4... | collective-permute-start | bytes 602120 | tf_op jit(solution)/shard_map/ppermute | solution.py:517
  141.5 0.2 copy.34
  141.7 0.8 collective-permute-done.16
  142.6 0.3 broadcast_select_fusion.1
  142.9 1.2 maximum_bitcast_fusion
  (47 shorter events, 0.4 us)
Async XLA Ops:
  0.0 14.6 %copy-start = (bf16[4,1,196,256]{3,0,2,1:T(4,128)(2,1)S(1)}, bf16[4,1,196,256]{3,0,2,1:T(4,128)(2,1)}, u32[]{:S(2)}) copy-start(bf16[4,1,196,256]{3,0,2,1:T(4,128)(2,1)} %param.13) | copy-start | bytes 1204228
  0.0 15.5 %collective-permute-start = (bf16[2304,256]{1,0:T(8,128)(2,1)}, bf16[2304,256]{1,0:T(8,128)(2,1)S(1)}, u32[]{:S(2)}, u32[]{:S(2)}) collective-permute-start(bf16[2304,256]{1,0:T(8,128)(2,1)} %bitcast.41), channel_id=1, source_target_pairs={{0,64},{64,0},{128,192},{192,128},{256,320},{320,256},{384,448},{4... | collective-permute-start | bytes 3538952 | tf_op jit(solution)/shard_map/ppermute | solution.py:436
  8.9 6.6 %collective-permute-start.1 = (bf16[2304,256]{1,0:T(8,128)(2,1)}, bf16[2304,256]{1,0:T(8,128)(2,1)S(1)}, u32[]{:S(2)}, u32[]{:S(2)}) collective-permute-start(bf16[2304,256]{1,0:T(8,128)(2,1)} %bitcast.45), channel_id=1, source_target_pairs={{0,64},{64,0},{128,192},{192,128},{256,320},{320,256},{384,448},{4... | collective-permute-start | bytes 3538952 | tf_op jit(solution)/shard_map/ppermute | solution.py:436
  11.5 3.9 %collective-permute-start.2 = (f32[3,256]{1,0:T(4,128)S(1)}, f32[3,256]{1,0:T(4,128)S(1)}, u32[]{:S(2)}, u32[]{:S(2)}) collective-permute-start(f32[3,256]{1,0:T(4,128)S(1)} %pad_maximum_fusion.own_vec), channel_id=1, source_target_pairs={{0,64},{64,0},{128,192},{192,128},{256,320},{320,256},{384,448},{4... | collective-permute-start | bytes 9224 | tf_op jit(solution)/shard_map/ppermute | solution.py:439
  15.5 1.9 %copy-start.1 = (bf16[2304,256]{1,0:T(8,128)(2,1)}, bf16[2304,256]{1,0:T(8,128)(2,1)S(1)}, u32[]{:S(2)}) copy-start(bf16[2304,256]{1,0:T(8,128)(2,1)S(1)} %collective-permute-done.peer1.rest_2_.refs_2_) | copy-start | bytes 3538948
  15.5 1.9 %copy-start.2 = (bf16[2304,256]{1,0:T(8,128)(2,1)}, bf16[2304,256]{1,0:T(8,128)(2,1)S(1)}, u32[]{:S(2)}) copy-start(bf16[2304,256]{1,0:T(8,128)(2,1)S(1)} %collective-permute-done.1.peer2.rest_3_.refs_3_) | copy-start | bytes 3538948
  23.3 3.3 %collective-permute-start.3 = (bf16[1,224,256]{2,1,0:T(8,128)(2,1)S(1)}, bf16[1,224,256]{2,1,0:T(8,128)(2,1)S(1)}, u32[]{:S(2)}, u32[]{:S(2)}) collective-permute-start(bf16[1,224,256]{2,1,0:T(8,128)(2,1)S(1)} %get-tuple-element.71), channel_id=1, source_target_pairs={{0,128},{64,192},{1,129},{65,193},{2,130},{66,194},{3,131},{67,195... | collective-permute-start | bytes 344072 | tf_op jit(solution)/shard_map/ppermute | solution.py:467
  24.6 4.5 %collective-permute-start.6 = (bf16[1,224,256]{2,1,0:T(8,128)(2,1)S(1)}, bf16[1,224,256]{2,1,0:T(8,128)(2,1)S(1)}, u32[]{:S(2)}, u32[]{:S(2)}) collective-permute-start(bf16[1,224,256]{2,1,0:T(8,128)(2,1)S(1)} %get-tuple-element.75), channel_id=1, source_target_pairs={{0,128},{64,192},{1,129},{65,193},{2,130},{66,194},{3,131},{67,195... | collective-permute-start | bytes 344072 | tf_op jit(solution)/shard_map/ppermute | solution.py:467
  26.6 3.1 %collective-permute-start.4 = (bf16[1,224,256]{2,1,0:T(8,128)(2,1)S(1)}, bf16[1,224,256]{2,1,0:T(8,128)(2,1)S(1)}, u32[]{:S(2)}, u32[]{:S(2)}) collective-permute-start(bf16[1,224,256]{2,1,0:T(8,128)(2,1)S(1)} %get-tuple-element.72), channel_id=1, source_target_pairs={{128,256},{192,320},{129,257},{193,321},{130,258},{194,322},{131,2... | collective-permute-start | bytes 344072 | tf_op jit(solution)/shard_map/ppermute | solution.py:467
  29.1 1.5 %collective-permute-start.7 = (bf16[1,224,256]{2,1,0:T(8,128)(2,1)S(1)}, bf16[1,224,256]{2,1,0:T(8,128)(2,1)S(1)}, u32[]{:S(2)}, u32[]{:S(2)}) collective-permute-start(bf16[1,224,256]{2,1,0:T(8,128)(2,1)S(1)} %get-tuple-element.76), channel_id=1, source_target_pairs={{128,256},{192,320},{129,257},{193,321},{130,258},{194,322},{131,2... | collective-permute-start | bytes 344072 | tf_op jit(solution)/shard_map/ppermute | solution.py:467
  29.8 1.5 %copy-start.4 = (bf16[1664,512]{1,0:T(8,128)(2,1)S(1)}, bf16[1664,512]{1,0:T(8,128)(2,1)}, u32[]{:S(2)}) copy-start(bf16[1664,512]{1,0:T(8,128)(2,1)} %centres_ref.1) | copy-start | bytes 5111812
  29.8 2.0 %collective-permute-start.5 = (bf16[1,224,256]{2,1,0:T(8,128)(2,1)S(1)}, bf16[1,224,256]{2,1,0:T(8,128)(2,1)S(1)}, u32[]{:S(2)}, u32[]{:S(2)}) collective-permute-start(bf16[1,224,256]{2,1,0:T(8,128)(2,1)S(1)} %get-tuple-element.73), channel_id=1, source_target_pairs={{256,384},{320,448},{257,385},{321,449},{258,386},{322,450},{259,3... | collective-permute-start | bytes 344072 | tf_op jit(solution)/shard_map/ppermute | solution.py:467
  30.6 1.2 collective-permute-start.8
  31.8 1.1 copy-start.6
  61.1 21.1 %all-to-all-start.1 = ((bf16[64,2,512]{2,1,0:T(2,128)(2,1)}), bf16[64,2,512]{2,1,0:T(2,128)(2,1)S(1)}, u32[]{:S(2)}, u32[]{:S(2)}) async-start(bf16[64,2,512]{2,1,0:T(2,128)(2,1)} %get-tuple-element.81), calls=%async_computation.1 | async-start | bytes 262144 | tf_op jit(solution)/shard_map/all_to_all | solution.py:490
  82.3 12.5 %copy-start.5 = (bf16[196,256]{1,0:T(8,128)(2,1)S(1)}, bf16[196,256]{1,0:T(8,128)(2,1)}, u32[]{:S(2)}) copy-start(bf16[196,256]{1,0:T(8,128)(2,1)} %pool.1) | copy-start | bytes 301060
  83.2 24.5 %copy-start.3 = (bf16[256,512]{1,0:T(8,128)(2,1)S(1)}, bf16[256,512]{1,0:T(8,128)(2,1)}, u32[]{:S(2)}) copy-start(bf16[256,512]{1,0:T(8,128)(2,1)} %embed_ref) | copy-start | bytes 786436
  84.0 23.5 %all-to-all-start.2 = ((bf16[64,2,640]{2,1,0:T(2,128)(2,1)}), bf16[64,2,640]{2,1,0:T(2,128)(2,1)S(1)}, u32[]{:S(2)}, u32[]{:S(2)}) async-start(bf16[64,2,640]{2,1,0:T(2,128)(2,1)} %reshape.125), calls=%async_computation.2 | async-start | bytes 327680 | tf_op jit(solution)/shard_map/all_to_all | solution.py:493
  93.4 14.3 %collective-permute-start.9 = (bf16[2,512]{1,0:T(2,128)(2,1)S(1)}, bf16[2,512]{1,0:T(2,128)(2,1)S(1)}, u32[]{:S(2)}, u32[]{:S(2)}) collective-permute-start(bf16[2,512]{1,0:T(2,128)(2,1)S(1)} %get-tuple-element.136), channel_id=1, source_target_pairs={{0,384},{64,448},{1,385},{65,449},{2,386},{66,450},{3,387},{67,451... | collective-permute-start | bytes 6152 | tf_op jit(solution)/shard_map/ppermute | solution.py:489
  112.5 1.4 collective-permute-start.10
  113.1 1.4 collective-permute-start.13
  113.9 1.4 collective-permute-start.11
  114.6 2.0 %collective-permute-start.14 = (bf16[1,224,256]{2,1,0:T(8,128)(2,1)S(1)}, bf16[1,224,256]{2,1,0:T(8,128)(2,1)S(1)}, u32[]{:S(2)}, u32[]{:S(2)}) collective-permute-start(bf16[1,224,256]{2,1,0:T(8,128)(2,1)S(1)} %get-tuple-element.112), channel_id=1, source_target_pairs={{256,128},{320,192},{257,129},{321,193},{258,130},{322,194},{259,1... | collective-permute-start | bytes 344072 | tf_op jit(solution)/shard_map/ppermute | solution.py:509
  115.3 10.8 %collective-permute-start.12 = (bf16[1,224,256]{2,1,0:T(8,128)(2,1)S(1)}, bf16[1,224,256]{2,1,0:T(8,128)(2,1)S(1)}, u32[]{:S(2)}, u32[]{:S(2)}) collective-permute-start(bf16[1,224,256]{2,1,0:T(8,128)(2,1)S(1)} %get-tuple-element.108), channel_id=1, source_target_pairs={{128,0},{192,64},{129,1},{193,65},{130,2},{194,66},{131,3},{195,67... | collective-permute-start | bytes 344072 | tf_op jit(solution)/shard_map/ppermute | solution.py:509
  116.6 12.9 %collective-permute-start.15 = (bf16[1,224,256]{2,1,0:T(8,128)(2,1)S(1)}, bf16[1,224,256]{2,1,0:T(8,128)(2,1)S(1)}, u32[]{:S(2)}, u32[]{:S(2)}) collective-permute-start(bf16[1,224,256]{2,1,0:T(8,128)(2,1)S(1)} %get-tuple-element.114), channel_id=1, source_target_pairs={{128,0},{192,64},{129,1},{193,65},{130,2},{194,66},{131,3},{195,67... | collective-permute-start | bytes 344072 | tf_op jit(solution)/shard_map/ppermute | solution.py:509
  131.8 10.7 %collective-permute-start.16 = (bf16[2,196,256]{2,0,1:T(2,128)(2,1)S(1)}, bf16[2,196,256]{2,0,1:T(2,128)(2,1)S(1)}, u32[]{:S(2)}, u32[]{:S(2)}) collective-permute-start(bf16[2,196,256]{2,0,1:T(2,128)(2,1)S(1)} %bitcast.52), channel_id=1, source_target_pairs={{0,64},{64,0},{128,192},{192,128},{256,320},{320,256},{384,448},{4... | collective-permute-start | bytes 602120 | tf_op jit(solution)/shard_map/ppermute | solution.py:517
